TPU v7x, 256 devices: a whole 4x4x8 slice. The times are simulated.
256 devices in a mesh: tm: 8 (over y, core), space: 32 (over z, x).
Axes of the slice: x: 4, y: 4, z: 8, core: 2. Of those that a mesh axis runs over, the one named last changes fastest.
Arguments:
- state: bfloat16 [8, 16384, 137], P('tm', 'space'), may hold values from -6 to 6
- obs_start: int32 [131072], P(('tm', 'space')), may hold values from 0 to 16383, as said below
- foot_weight: bfloat16 [131072, 8], P(('tm', 'space')), may hold values from 0.019897461 to 0.29882812
- obs_slot: int32 [131072], P(('tm', 'space')), may hold values from 0 to 6
- obs_frac: float32 [131072], P(('tm', 'space')), may hold values from 0 to 1
- live_count: int32 [8, 32], P('tm', 'space'), may hold values from 64 to 512
- obs_values: float32 [131072, 128], P(('tm', 'space')), may hold values from -6 to 6
- jacobian: bfloat16 [137, 128], replicated, may hold values from -0.5 to 0.5
- inv_var: float32 [128], replicated, may hold values from 0.25 to 4
Outputs:
- departures: float32 [131072, 128], P(('tm', 'space'))
- adjoint: float32 [8, 16384, 137], P('tm', 'space')
Inputs may be any that keep to these rules, and one draw needn't show every extreme that they name: `obs_start`: on the devices of space index s, every observation's footprint columns lie within 256 columns of tile s, that is within s * 512 - 256 .. (s + 1) * 512 + 255 taken modulo 16384. `live_count`: rows at or beyond a device's count are padding.
All inputs are finite; a program needn't handle non-finite values.
Results may differ from a plain program's by a relative error of at most 0.008.
Values may be sent and summed in bfloat16 or wider, within the bound.
No kernel may reach another device: no remote copies, remote signals or barrier semaphores. Data moves between devices by JAX's collectives and lax.ppermute only.
A program may use at most 64 MiB of HBM per device.

v0:
```python
import functools

import jax
import jax.numpy as jnp
from jax import lax
from jax.experimental import pallas as pl
from jax.experimental.pallas import tpu as pltpu
from jax.sharding import PartitionSpec as P


F32 = jnp.float32
BF16 = jnp.bfloat16
GROUP = 16


VMEM = pl.BlockSpec(memory_space=pltpu.VMEM)
SMEM = pl.BlockSpec(memory_space=pltpu.SMEM)
HBM = pl.BlockSpec(memory_space=pltpu.HBM)


def held_slots():
    turn = lax.axis_index("tm")
    return turn.astype(F32), (turn ^ 1).astype(F32)


def project_kernel(state, jac, full, head, tail, field, levels, sems):
    half = full.shape[1] // 2
    copies = [
        pltpu.make_async_copy(state, field, sems.at[0]),
        pltpu.make_async_copy(jac, levels, sems.at[1]),
    ]
    for copy in copies:
        copy.start()
    for copy in copies:
        copy.wait()
    out = lax.dot_general(
        levels[...], field[...], (((0,), (0,)), ((), ())), preferred_element_type=F32
    ).astype(BF16)
    full[...] = out
    head[...] = out[:, :half]
    tail[...] = out[:, half:]


def info_kernel(cols, tiles, start, weight, slot, frac, info):
    base = lax.axis_index("space") * cols - cols // 2
    total = cols * tiles
    local = start[...] - base
    local = jnp.where(local < 0, local + total, local)
    local = jnp.where(local >= total, local - total, local)
    rows = lax.broadcasted_iota(jnp.int32, (8, local.shape[1]), 0)
    extra = jnp.where(rows == 0, local.astype(F32), 0.0)
    extra = jnp.where(rows == 1, slot[...].astype(F32), extra)
    extra = jnp.where(rows == 2, frac[...], extra)
    info[0:8, :] = weight[...].astype(F32)
    info[8:16, :] = extra


def widen_kernel(full, left, right, wide):
    cols = full.shape[1]
    half = cols // 2
    wide[:, :half] = left[...]
    wide[:, half : half + cols] = full[...]
    wide[:, half + cols :] = right[...]


def matrix_kernel(n, *refs):
    for info, mat in zip(refs[:n], refs[n:]):
        footprint(info, mat)


def footprint(info, mat):
    width, obs = mat.shape
    local = info[8:9, :].astype(jnp.int32)
    low = local & (GROUP - 1)
    high = lax.shift_right_logical(local, 4)
    rows = lax.broadcasted_iota(jnp.int32, (GROUP, obs), 0)
    offset = (rows - low) & (GROUP - 1)
    piece = jnp.zeros((GROUP, obs), F32)
    for k in range(8):
        piece = piece + jnp.where(offset == k, info[k : k + 1, :], 0.0)
    piece = piece.astype(BF16)
    group = (high + jnp.where(rows < low, 1, 0)).astype(F32).astype(BF16)
    zero = jnp.zeros((GROUP, obs), BF16)
    for g in range(width // GROUP):
        mat[g * GROUP : (g + 1) * GROUP, :] = jnp.where(
            group == jnp.full((GROUP, obs), g, BF16), piece, zero
        )


def slot_weight(info, held):
    slot = info[9:10, :]
    frac = info[10:11, :]
    return jnp.where(slot == held, 1.0 - frac, 0.0) + jnp.where(slot + 1.0 == held, frac, 0.0)


def gather_kernel(n, mine, other, *refs):
    infos, mats, outs = refs[:n], refs[n : 2 * n], refs[2 * n :]
    chan = mine.shape[0]
    field = jnp.concatenate([mine[...], other[...]], axis=0)
    own_slot, other_slot = held_slots()
    for info, mat, out in zip(infos, mats, outs):
        both = jnp.dot(field, mat[...], preferred_element_type=F32)
        first = slot_weight(info, own_slot)
        second = slot_weight(info, other_slot)
        out[...] = (first * both[:chan] + second * both[chan:]).astype(BF16)


def turn_kernel(source, out):
    out[...] = jnp.transpose(source[...])


def values_kernel(source, inv_var, values, scale, held, sem):
    copy = pltpu.make_async_copy(source, held, sem)
    copy.start()
    scale[...] = jnp.transpose(jnp.broadcast_to(inv_var[...], scale.shape))
    copy.wait()
    values[...] = jnp.transpose(held[...])


def depart_kernel(n, count, *refs):
    parts = refs[:n]
    values, scale, gaps, scaled = refs[n:]
    chan, obs = values.shape
    total = parts[0][...].astype(F32)
    for part in parts[1:]:
        total = total + part[...].astype(F32)
    live = lax.broadcasted_iota(jnp.int32, (chan, obs), 1) < count[0, 0]
    gap = jnp.where(live, values[...] - total, 0.0)
    gaps[...] = gap
    scaled[...] = (gap * scale[:, 0:1]).astype(BF16)


def spread_part(infos, scaled, mats):
    own_slot, other_slot = held_slots()
    total = None
    for info, source, mat in zip(infos, scaled, mats):
        rows = source[...].astype(F32)
        mine = (slot_weight(info, own_slot) * rows).astype(BF16)
        other = (slot_weight(info, other_slot) * rows).astype(BF16)
        part = lax.dot_general(
            jnp.concatenate([mine, other], axis=0),
            mat[...],
            (((1,), (1,)), ((), ())),
            preferred_element_type=F32,
        )
        total = part if total is None else total + part
    return total


def spread_own_kernel(info, scaled, mat, acc):
    acc[...] = spread_part([info], [scaled], [mat])


def spread_rest_kernel(n, acc, *refs):
    infos, scaled, mats = refs[:n], refs[n : 2 * n], refs[2 * n : 3 * n]
    own, give = refs[3 * n :]
    chan = own.shape[0]
    total = acc[...] + spread_part(infos, scaled, mats)
    own[...] = total[:chan]
    give[...] = total[chan:].astype(BF16)


def join_kernel(own, got, mid, left, right):
    cols = mid.shape[1]
    half = cols // 2
    mid[...] = own[:, half : half + cols] + got[:, half : half + cols].astype(F32)
    left[...] = (own[:, :half] + got[:, :half].astype(F32)).astype(BF16)
    right[...] = (own[:, half + cols :] + got[:, half + cols :].astype(F32)).astype(BF16)


def finish_kernel(mid, head, tail, jac, out):
    half = head.shape[1]
    first = mid[:, :half] + head[...].astype(F32)
    last = mid[:, half:] + tail[...].astype(F32)
    total = jnp.concatenate([first, last], axis=1).astype(BF16)
    out[:, 0, :] = jnp.dot(jac[...], total, preferred_element_type=F32)


def call(kernel, outs, *args, specs=None, scratch=(), flops=1 << 20):
    return pl.pallas_call(
        kernel,
        out_shape=[jax.ShapeDtypeStruct(shape, dtype) for shape, dtype in outs],
        in_specs=specs or [VMEM] * len(args),
        out_specs=[VMEM] * len(outs),
        scratch_shapes=scratch,
        compiler_params=pltpu.CompilerParams(vmem_limit_bytes=8 << 20),
        cost_estimate=pl.CostEstimate(flops=flops, bytes_accessed=1 << 20, transcendentals=0),
    )(*args)


def make_body(n_tm, n_space):
    lanes = n_tm // 2

    def move(block, turn, swap, shift):
        route = []
        for t in range(n_tm):
            for s in range(n_space):
                y, core = t // 2, t % 2
                t_from = ((y + turn) % lanes) * 2 + (core ^ swap)
                s_from = (s + shift) % n_space
                route.append((t_from * n_space + s_from, t * n_space + s))
        return lax.ppermute(block, ("tm", "space"), route)

    def steps(
        state, obs_start, foot_weight, obs_slot, obs_frac, live_count, obs_values, jacobian, inv_var
    ):
        own = state[0]
        cols, levels = own.shape
        half = cols // 2
        width = 2 * cols
        chan = jacobian.shape[1]
        obs = obs_start.shape[0]

        def flat(vector):
            return vector.reshape(1, -1)

        full, head, tail = call(
            project_kernel,
            [((chan, cols), BF16), ((chan, half), BF16), ((chan, half), BF16)],
            own.T,
            jacobian,
            specs=[HBM, HBM],
            scratch=[
                pltpu.VMEM((levels, cols), BF16),
                pltpu.VMEM((levels, chan), BF16),
                pltpu.SemaphoreType.DMA((2,)),
            ],
        )
        (info,) = call(
            functools.partial(info_kernel, cols, n_space),
            [((16, obs), F32)],
            flat(obs_start),
            foot_weight.T,
            flat(obs_slot),
            flat(obs_frac),
        )
        left, right = move(tail, 0, 0, -1), move(head, 0, 0, 1)
        infos = [info] + [move(info, j, 0, 0) for j in range(1, lanes)]
        (wide,) = call(widen_kernel, [((chan, width), BF16)], full, left, right)
        other = move(wide, 0, 1, 0)
        mats = call(functools.partial(matrix_kernel, lanes), [((width, obs), BF16)] * lanes, *infos)

        def gather(which):
            return call(
                functools.partial(gather_kernel, len(which)),
                [((chan, obs), BF16)] * len(which),
                wide,
                other,
                *[infos[j] for j in which],
                *[mats[j] for j in which],
            )

        (far,) = gather([2])
        far = move(far, -2, 0, 0)
        after, before = gather([1, 3])
        after, before = move(after, -1, 0, 0), move(before, 1, 0, 0)
        (kept,) = gather([0])
        values, scale = call(
            values_kernel,
            [((chan, obs), F32), ((chan, chan), F32)],
            obs_values,
            flat(inv_var),
            specs=[HBM, VMEM],
            scratch=[pltpu.VMEM((obs, chan), F32), pltpu.SemaphoreType.DMA],
        )
        gaps, scaled = call(
            functools.partial(depart_kernel, lanes),
            [((chan, obs), F32), ((chan, obs), BF16)],
            live_count,
            kept,
            far,
            after,
            before,
            values,
            scale,
            specs=[SMEM] + [VMEM] * (lanes + 2),
        )
        all_scaled = [scaled] + [move(scaled, j, 0, 0) for j in range(1, lanes)]
        (acc,) = call(spread_own_kernel, [((2 * chan, width), F32)], info, scaled, mats[0])
        (departures,) = call(turn_kernel, [((obs, chan), F32)], gaps)
        mine, give = call(
            functools.partial(spread_rest_kernel, lanes - 1),
            [((chan, width), F32), ((chan, width), BF16)],
            acc,
            *infos[1:],
            *all_scaled[1:],
            *mats[1:],
        )
        mid, to_left, to_right = call(
            join_kernel,
            [((chan, cols), F32)] + [((chan, half), BF16)] * 2,
            mine,
            move(give, 0, 1, 0),
        )
        (adjoint,) = call(
            finish_kernel,
            [((levels, 1, cols), F32)],
            mid,
            move(to_right, 0, 0, -1),
            move(to_left, 0, 0, 1),
            jacobian,
        )
        return (departures, jnp.transpose(adjoint, (1, 2, 0)))

    return steps


def solution(mesh):
    return jax.shard_map(
        make_body(mesh.shape["tm"], mesh.shape["space"]),
        mesh=mesh,
        in_specs=(
            P("tm", "space", None),
            P(("tm", "space")),
            P(("tm", "space"), None),
            P(("tm", "space")),
            P(("tm", "space")),
            P("tm", "space"),
            P(("tm", "space"), None),
            P(),
            P(),
        ),
        out_specs=(P(("tm", "space"), None), P("tm", "space", None)),
        check_vma=False,
    )
```

profile of v0, /device:TPU:1, one launch (start us, length us, event | category | flops | bytes accessed | tf_op | source)
XLA Modules:
  0.0 55.7 jit_solution(1327375084215197576)
XLA Ops:
  0.6 0.0 copy-start.1
  0.6 0.8 %copy-done.1 = bf16[137,128]{1,0:T(8,128)(2,1)S(1)} copy-done((bf16[137,128]{1,0:T(8,128)(2,1)S(1)}, bf16[137,128]{1,0:T(8,128)(2,1)}, u32[]{:S(2)}) %copy-start.1) | copy-done | bytes 35096
  1.4 0.0 copy-start.3
  1.4 0.9 %copy-done.3 = bf16[1,512,137]{1,2,0:T(8,128)(2,1)S(1)} copy-done((bf16[1,512,137]{1,2,0:T(8,128)(2,1)S(1)}, bf16[1,512,137]{1,2,0:T(8,128)(2,1)}, u32[]{:S(2)}) %copy-start.3) | copy-done | bytes 140312
  2.3 0.4 shard_map.104
  2.8 2.1 %collective-permute-start = (bf16[128,256]{1,0:T(8,128)(2,1)S(1)}, bf16[128,256]{1,0:T(8,128)(2,1)S(1)}, u32[]{:S(2)}, u32[]{:S(2)}) collective-permute-start(bf16[128,256]{1,0:T(8,128)(2,1)S(1)} %get-tuple-element.21), channel_id=1, source_target_pairs={{31,0},{0,1},{1,2},{2,3},{3,4},{4,5},{5,6},{6,7},{7,8},{8,9},{9,10... | collective-permute-start | bytes 196616 | tf_op jit(solution)/shard_map/ppermute | solution.py:202
  4.9 6.6 %collective-permute-start.1 = (bf16[128,256]{1,0:T(8,128)(2,1)S(1)}, bf16[128,256]{1,0:T(8,128)(2,1)S(1)}, u32[]{:S(2)}, u32[]{:S(2)}) collective-permute-start(bf16[128,256]{1,0:T(8,128)(2,1)S(1)} %get-tuple-element.22), channel_id=1, source_target_pairs={{1,0},{2,1},{3,2},{4,3},{5,4},{6,5},{7,6},{8,7},{9,8},{10,9},{11,1... | collective-permute-start | bytes 196616 | tf_op jit(solution)/shard_map/ppermute | solution.py:202
  11.5 1.6 %collective-permute-done.left = bf16[128,256]{1,0:T(8,128)(2,1)S(1)} collective-permute-done((bf16[128,256]{1,0:T(8,128)(2,1)S(1)}, bf16[128,256]{1,0:T(8,128)(2,1)S(1)}, u32[]{:S(2)}, u32[]{:S(2)}) %collective-permute-start) | collective-permute-done | bytes 65568 | tf_op jit(solution)/shard_map/ppermute | solution.py:202
  13.1 0.0 collective-permute-done.1.right
  13.1 0.0 copy-start.4
  13.1 0.0 copy-start.7
  13.1 1.6 %collective-permute-start.2 = (bf16[128,1024]{1,0:T(8,128)(2,1)S(1)}, bf16[128,1024]{1,0:T(8,128)(2,1)S(1)}, u32[]{:S(2)}, u32[]{:S(2)}) collective-permute-start(bf16[128,1024]{1,0:T(8,128)(2,1)S(1)} %shard_map.105.mine), channel_id=1, source_target_pairs={{32,0},{33,1},{34,2},{35,3},{36,4},{37,5},{38,6},{39,7},{40,8},{41... | collective-permute-start | bytes 786440 | tf_op jit(solution)/shard_map/ppermute | solution.py:202
  14.8 0.0 copy-start.6
  14.8 0.0 copy-start.5
  14.8 0.0 copy-done.4
  14.8 0.0 copy-done.7
  14.8 0.7 %copy-done.6 = s32[512]{0:T(512)S(1)} copy-done((s32[512]{0:T(512)S(1)}, s32[512]{0:T(512)}, u32[]{:S(2)}) %copy-start.6) | copy-done | bytes 2072
  15.4 0.0 copy-done.5
  15.5 2.8 %collective-permute-start.3 = (f32[16,512]{1,0:T(8,128)S(1)}, f32[16,512]{1,0:T(8,128)S(1)}, u32[]{:S(2)}, u32[]{:S(2)}) collective-permute-start(f32[16,512]{1,0:T(8,128)S(1)} %shard_map.106.refs_0_.info), channel_id=1, source_target_pairs={{64,0},{65,1},{66,2},{67,3},{68,4},{69,5},{70,6},{71,7},{72,8},{73... | collective-permute-start | bytes 98312 | tf_op jit(solution)/shard_map/ppermute | solution.py:202
  18.3 0.4 collective-permute-start.4
  18.6 0.7 %collective-permute-start.5 = (f32[16,512]{1,0:T(8,128)S(1)}, f32[16,512]{1,0:T(8,128)S(1)}, u32[]{:S(2)}, u32[]{:S(2)}) collective-permute-start(f32[16,512]{1,0:T(8,128)S(1)} %shard_map.106.refs_0_.info), channel_id=1, source_target_pairs={{192,0},{193,1},{194,2},{195,3},{196,4},{197,5},{198,6},{199,7},{2... | collective-permute-start | bytes 98312 | tf_op jit(solution)/shard_map/ppermute | solution.py:202
  19.3 0.0 collective-permute-done.3.refs_1_.refs_0_
  19.3 3.3 %collective-permute-done.4.refs_2_.refs_0_.refs_1_ = f32[16,512]{1,0:T(8,128)S(1)} collective-permute-done((f32[16,512]{1,0:T(8,128)S(1)}, f32[16,512]{1,0:T(8,128)S(1)}, u32[]{:S(2)}, u32[]{:S(2)}) %collective-permute-start.4) | collective-permute-done | bytes 32800 | tf_op jit(solution)/shard_map/ppermute | solution.py:202
  22.6 0.6 %collective-permute-done.5.refs_3_.refs_1_.refs_2_ = f32[16,512]{1,0:T(8,128)S(1)} collective-permute-done((f32[16,512]{1,0:T(8,128)S(1)}, f32[16,512]{1,0:T(8,128)S(1)}, u32[]{:S(2)}, u32[]{:S(2)}) %collective-permute-start.5) | collective-permute-done | bytes 32800 | tf_op jit(solution)/shard_map/ppermute | solution.py:202
  23.2 0.6 %shard_map.107 = (bf16[1024,512]{1,0:T(8,128)(2,1)S(1)}, bf16[1024,512]{1,0:T(8,128)(2,1)S(1)}, bf16[1024,512]{1,0:T(8,128)(2,1)S(1)}, bf16[1024,512]{1,0:T(8,128)(2,1)S(1)}) custom-call(f32[16,512]{1,0:T(8,128)S(1)} %shard_map.106.refs_0_.info, f32[16,512]{1,0:T(8,128)S(1)} %collective-permute-done.3.refs_1_.refs_0_, ...), custom_call_target="tpu_custom_call" | custom-call | flops 1048576 | bytes 1048576 | tf_op jit(solution)/shard_map/pallas_call | solution.py:180
  23.8 0.0 collective-permute-done.2.other
  23.8 0.4 shard_map.109
  24.2 1.1 %collective-permute-start.6 = (bf16[128,512]{1,0:T(8,128)(2,1)S(1)}, bf16[128,512]{1,0:T(8,128)(2,1)S(1)}, u32[]{:S(2)}, u32[]{:S(2)}) collective-permute-start(bf16[128,512]{1,0:T(8,128)(2,1)S(1)} %shard_map.109), channel_id=1, source_target_pairs={{128,0},{129,1},{130,2},{131,3},{132,4},{133,5},{134,6},{135,7},{1... | collective-permute-start | bytes 393224 | tf_op jit(solution)/shard_map/ppermute | solution.py:202
  25.4 0.0 copy-start
  25.4 0.7 %shard_map.110 = (bf16[128,512]{1,0:T(8,128)(2,1)S(1)}, bf16[128,512]{1,0:T(8,128)(2,1)S(1)}) custom-call(bf16[128,1024]{1,0:T(8,128)(2,1)S(1)} %shard_map.105.mine, bf16[128,1024]{1,0:T(8,128)(2,1)S(1)} %collective-permute-done.2.other, f32[16,512]{1,0:T(8,128)S(1)} %collective-permute-done.3.refs_1_.refs_0_, ...), custom_call_target="tpu_custom_call" | custom-call | flops 1048576 | bytes 1048576 | tf_op jit(solution)/shard_map/pallas_call | solution.py:180
  26.1 0.1 collective-permute-start.7
  26.2 2.7 %collective-permute-start.8 = (bf16[128,512]{1,0:T(8,128)(2,1)S(1)}, bf16[128,512]{1,0:T(8,128)(2,1)S(1)}, u32[]{:S(2)}, u32[]{:S(2)}) collective-permute-start(bf16[128,512]{1,0:T(8,128)(2,1)S(1)} %get-tuple-element.28), channel_id=1, source_target_pairs={{64,0},{65,1},{66,2},{67,3},{68,4},{69,5},{70,6},{71,7},{72,8},{73... | collective-permute-start | bytes 393224 | tf_op jit(solution)/shard_map/ppermute | solution.py:202
  29.5 0.0 copy-start.8
  29.5 0.0 copy-done
  29.5 0.6 %copy-done.8 = f32[128]{0:T(128)S(1)} copy-done((f32[128]{0:T(128)S(1)}, f32[128]{0:T(128)}, u32[]{:S(2)}) %copy-start.8) | copy-done | bytes 536
  30.2 0.3 shard_map.111
  30.4 0.4 shard_map.108.refs_0_
  30.9 0.0 collective-permute-done.6.refs_1_
  30.9 2.3 %collective-permute-done.7.refs_2_ = bf16[128,512]{1,0:T(8,128)(2,1)S(1)} collective-permute-done((bf16[128,512]{1,0:T(8,128)(2,1)S(1)}, bf16[128,512]{1,0:T(8,128)(2,1)S(1)}, u32[]{:S(2)}, u32[]{:S(2)}) %collective-permute-start.7) | collective-permute-done | bytes 131104 | tf_op jit(solution)/shard_map/ppermute | solution.py:202
  33.1 0.0 collective-permute-done.8.refs_3_
  33.1 0.1 shard_map.112
  33.2 0.8 %collective-permute-start.9 = (bf16[128,512]{1,0:T(8,128)(2,1)S(1)}, bf16[128,512]{1,0:T(8,128)(2,1)S(1)}, u32[]{:S(2)}, u32[]{:S(2)}) collective-permute-start(bf16[128,512]{1,0:T(8,128)(2,1)S(1)} %get-tuple-element.32.scaled), channel_id=1, source_target_pairs={{64,0},{65,1},{66,2},{67,3},{68,4},{69,5},{70,6},{71,7},{72,8},{73... | collective-permute-start | bytes 393224 | tf_op jit(solution)/shard_map/ppermute | solution.py:202
  34.1 0.3 collective-permute-start.10
  34.4 0.7 %collective-permute-start.11 = (bf16[128,512]{1,0:T(8,128)(2,1)S(1)}, bf16[128,512]{1,0:T(8,128)(2,1)S(1)}, u32[]{:S(2)}, u32[]{:S(2)}) collective-permute-start(bf16[128,512]{1,0:T(8,128)(2,1)S(1)} %get-tuple-element.32.scaled), channel_id=1, source_target_pairs={{192,0},{193,1},{194,2},{195,3},{196,4},{197,5},{198,6},{199,7},{2... | collective-permute-start | bytes 393224 | tf_op jit(solution)/shard_map/ppermute | solution.py:202
  35.1 0.5 shard_map.114.acc
  35.6 1.6 %collective-permute-done.9.refs_3_ = bf16[128,512]{1,0:T(8,128)(2,1)S(1)} collective-permute-done((bf16[128,512]{1,0:T(8,128)(2,1)S(1)}, bf16[128,512]{1,0:T(8,128)(2,1)S(1)}, u32[]{:S(2)}, u32[]{:S(2)}) %collective-permute-start.9) | collective-permute-done | bytes 131104 | tf_op jit(solution)/shard_map/ppermute | solution.py:202
  37.1 2.3 %collective-permute-done.10.refs_4_ = bf16[128,512]{1,0:T(8,128)(2,1)S(1)} collective-permute-done((bf16[128,512]{1,0:T(8,128)(2,1)S(1)}, bf16[128,512]{1,0:T(8,128)(2,1)S(1)}, u32[]{:S(2)}, u32[]{:S(2)}) %collective-permute-start.10) | collective-permute-done | bytes 131104 | tf_op jit(solution)/shard_map/ppermute | solution.py:202
  39.5 1.3 %collective-permute-done.11.refs_5_ = bf16[128,512]{1,0:T(8,128)(2,1)S(1)} collective-permute-done((bf16[128,512]{1,0:T(8,128)(2,1)S(1)}, bf16[128,512]{1,0:T(8,128)(2,1)S(1)}, u32[]{:S(2)}, u32[]{:S(2)}) %collective-permute-start.11) | collective-permute-done | bytes 131104 | tf_op jit(solution)/shard_map/ppermute | solution.py:202
  40.8 1.0 %shard_map.115 = (f32[128,1024]{1,0:T(8,128)S(1)}, bf16[128,1024]{1,0:T(8,128)(2,1)S(1)}) custom-call(f32[256,1024]{1,0:T(8,128)S(1)} %shard_map.114.acc, f32[16,512]{1,0:T(8,128)S(1)} %collective-permute-done.3.refs_1_.refs_0_, f32[16,512]{1,0:T(8,128)S(1)} %collective-permute-done.4.refs_2_.refs_0_.refs_1_, ...), custom_call_target="tpu_custom_call" | custom-call | flops 1048576 | bytes 1048576 | tf_op jit(solution)/shard_map/pallas_call | solution.py:180
  41.8 4.4 %collective-permute-start.12 = (bf16[128,1024]{1,0:T(8,128)(2,1)S(1)}, bf16[128,1024]{1,0:T(8,128)(2,1)S(1)}, u32[]{:S(2)}, u32[]{:S(2)}) collective-permute-start(bf16[128,1024]{1,0:T(8,128)(2,1)S(1)} %get-tuple-element.34), channel_id=1, source_target_pairs={{32,0},{33,1},{34,2},{35,3},{36,4},{37,5},{38,6},{39,7},{40,8},{41... | collective-permute-start | bytes 786440 | tf_op jit(solution)/shard_map/ppermute | solution.py:202
  46.2 1.2 %collective-permute-done.12.got = bf16[128,1024]{1,0:T(8,128)(2,1)S(1)} collective-permute-done((bf16[128,1024]{1,0:T(8,128)(2,1)S(1)}, bf16[128,1024]{1,0:T(8,128)(2,1)S(1)}, u32[]{:S(2)}, u32[]{:S(2)}) %collective-permute-start.12) | collective-permute-done | bytes 262176 | tf_op jit(solution)/shard_map/ppermute | solution.py:202
  47.4 0.1 shard_map.116
  47.5 0.1 collective-permute-start.13
  47.6 5.2 %collective-permute-start.14 = (bf16[128,256]{1,0:T(8,128)(2,1)S(1)}, bf16[128,256]{1,0:T(8,128)(2,1)S(1)}, u32[]{:S(2)}, u32[]{:S(2)}) collective-permute-start(bf16[128,256]{1,0:T(8,128)(2,1)S(1)} %get-tuple-element.37), channel_id=1, source_target_pairs={{1,0},{2,1},{3,2},{4,3},{5,4},{6,5},{7,6},{8,7},{9,8},{10,9},{11,1... | collective-permute-start | bytes 196616 | tf_op jit(solution)/shard_map/ppermute | solution.py:202
  52.8 0.0 copy-start.2
  52.8 0.8 %shard_map.113 = f32[512,128]{1,0:T(8,128)} custom-call(f32[128,512]{1,0:T(8,128)S(1)} %get-tuple-element.31.source), custom_call_target="tpu_custom_call" | custom-call | flops 1048576 | bytes 1048576 | tf_op jit(solution)/shard_map/pallas_call | solution.py:180
  53.6 1.2 %collective-permute-done.13.head = bf16[128,256]{1,0:T(8,128)(2,1)S(1)} collective-permute-done((bf16[128,256]{1,0:T(8,128)(2,1)S(1)}, bf16[128,256]{1,0:T(8,128)(2,1)S(1)}, u32[]{:S(2)}, u32[]{:S(2)}) %collective-permute-start.13) | collective-permute-done | bytes 65568 | tf_op jit(solution)/shard_map/ppermute | solution.py:202
  54.8 0.0 collective-permute-done.14.tail
  54.8 0.0 copy-done.2
  54.8 0.9 %shard_map.117 = f32[137,1,512]{2,1,0:T(1,128)} custom-call(f32[128,512]{1,0:T(8,128)S(1)} %get-tuple-element.35.mid, bf16[128,256]{1,0:T(8,128)(2,1)S(1)} %collective-permute-done.13.head, bf16[128,256]{1,0:T(8,128)(2,1)S(1)} %collective-permute-done.14.tail, bf16[137,128]{1,0:T(8,128)(2,1)S(1)} %copy-done.2), custom_call_target="tpu_custom_call" | custom-call | flops 1048576 | bytes 1048576 | tf_op jit(solution)/shard_map/pallas_call | solution.py:180
  (2 shorter events, 0.0 us)
Async XLA Ops:
  0.6 0.8 %copy-start.1 = (bf16[137,128]{1,0:T(8,128)(2,1)S(1)}, bf16[137,128]{1,0:T(8,128)(2,1)}, u32[]{:S(2)}) copy-start(bf16[137,128]{1,0:T(8,128)(2,1)} %jac.3) | copy-start | bytes 105220
  1.4 0.9 %copy-start.3 = (bf16[1,512,137]{1,2,0:T(8,128)(2,1)S(1)}, bf16[1,512,137]{1,2,0:T(8,128)(2,1)}, u32[]{:S(2)}) copy-start(bf16[1,512,137]{1,2,0:T(8,128)(2,1)} %param.9) | copy-start | bytes 420868
  2.8 10.3 %collective-permute-start = (bf16[128,256]{1,0:T(8,128)(2,1)S(1)}, bf16[128,256]{1,0:T(8,128)(2,1)S(1)}, u32[]{:S(2)}, u32[]{:S(2)}) collective-permute-start(bf16[128,256]{1,0:T(8,128)(2,1)S(1)} %get-tuple-element.21), channel_id=1, source_target_pairs={{31,0},{0,1},{1,2},{2,3},{3,4},{4,5},{5,6},{6,7},{7,8},{8,9},{9,10... | collective-permute-start | bytes 196616 | tf_op jit(solution)/shard_map/ppermute | solution.py:202
  4.9 8.2 %collective-permute-start.1 = (bf16[128,256]{1,0:T(8,128)(2,1)S(1)}, bf16[128,256]{1,0:T(8,128)(2,1)S(1)}, u32[]{:S(2)}, u32[]{:S(2)}) collective-permute-start(bf16[128,256]{1,0:T(8,128)(2,1)S(1)} %get-tuple-element.22), channel_id=1, source_target_pairs={{1,0},{2,1},{3,2},{4,3},{5,4},{6,5},{7,6},{8,7},{9,8},{10,9},{11,1... | collective-permute-start | bytes 196616 | tf_op jit(solution)/shard_map/ppermute | solution.py:202
  13.1 1.7 %copy-start.4 = (bf16[512,8]{0,1:T(8,128)(2,1)S(1)}, bf16[512,8]{0,1:T(8,128)(2,1)}, u32[]{:S(2)}) copy-start(bf16[512,8]{0,1:T(8,128)(2,1)} %param.11) | copy-start | bytes 24580
  13.1 1.7 %copy-start.7 = (f32[512]{0:T(512)S(1)}, f32[512]{0:T(512)}, u32[]{:S(2)}) copy-start(f32[512]{0:T(512)} %param.13) | copy-start | bytes 6148
  13.1 10.7 %collective-permute-start.2 = (bf16[128,1024]{1,0:T(8,128)(2,1)S(1)}, bf16[128,1024]{1,0:T(8,128)(2,1)S(1)}, u32[]{:S(2)}, u32[]{:S(2)}) collective-permute-start(bf16[128,1024]{1,0:T(8,128)(2,1)S(1)} %shard_map.105.mine), channel_id=1, source_target_pairs={{32,0},{33,1},{34,2},{35,3},{36,4},{37,5},{38,6},{39,7},{40,8},{41... | collective-permute-start | bytes 786440 | tf_op jit(solution)/shard_map/ppermute | solution.py:202
  14.8 0.7 %copy-start.6 = (s32[512]{0:T(512)S(1)}, s32[512]{0:T(512)}, u32[]{:S(2)}) copy-start(s32[512]{0:T(512)} %param.12) | copy-start | bytes 6148
  14.8 0.7 %copy-start.5 = (s32[512]{0:T(512)S(1)}, s32[512]{0:T(512)}, u32[]{:S(2)}) copy-start(s32[512]{0:T(512)} %param.10) | copy-start | bytes 6148
  15.5 3.9 %collective-permute-start.3 = (f32[16,512]{1,0:T(8,128)S(1)}, f32[16,512]{1,0:T(8,128)S(1)}, u32[]{:S(2)}, u32[]{:S(2)}) collective-permute-start(f32[16,512]{1,0:T(8,128)S(1)} %shard_map.106.refs_0_.info), channel_id=1, source_target_pairs={{64,0},{65,1},{66,2},{67,3},{68,4},{69,5},{70,6},{71,7},{72,8},{73... | collective-permute-start | bytes 98312 | tf_op jit(solution)/shard_map/ppermute | solution.py:202
  18.3 4.3 %collective-permute-start.4 = (f32[16,512]{1,0:T(8,128)S(1)}, f32[16,512]{1,0:T(8,128)S(1)}, u32[]{:S(2)}, u32[]{:S(2)}) collective-permute-start(f32[16,512]{1,0:T(8,128)S(1)} %shard_map.106.refs_0_.info), channel_id=1, source_target_pairs={{128,0},{129,1},{130,2},{131,3},{132,4},{133,5},{134,6},{135,7},{1... | collective-permute-start | bytes 98312 | tf_op jit(solution)/shard_map/ppermute | solution.py:202
  18.6 4.6 %collective-permute-start.5 = (f32[16,512]{1,0:T(8,128)S(1)}, f32[16,512]{1,0:T(8,128)S(1)}, u32[]{:S(2)}, u32[]{:S(2)}) collective-permute-start(f32[16,512]{1,0:T(8,128)S(1)} %shard_map.106.refs_0_.info), channel_id=1, source_target_pairs={{192,0},{193,1},{194,2},{195,3},{196,4},{197,5},{198,6},{199,7},{2... | collective-permute-start | bytes 98312 | tf_op jit(solution)/shard_map/ppermute | solution.py:202
  24.2 6.6 %collective-permute-start.6 = (bf16[128,512]{1,0:T(8,128)(2,1)S(1)}, bf16[128,512]{1,0:T(8,128)(2,1)S(1)}, u32[]{:S(2)}, u32[]{:S(2)}) collective-permute-start(bf16[128,512]{1,0:T(8,128)(2,1)S(1)} %shard_map.109), channel_id=1, source_target_pairs={{128,0},{129,1},{130,2},{131,3},{132,4},{133,5},{134,6},{135,7},{1... | collective-permute-start | bytes 393224 | tf_op jit(solution)/shard_map/ppermute | solution.py:202
  25.4 4.1 %copy-start = (f32[512,128]{1,0:T(8,128)S(1)}, f32[512,128]{1,0:T(8,128)}, u32[]{:S(2)}) copy-start(f32[512,128]{1,0:T(8,128)} %source.1) | copy-start | bytes 786436
  26.1 7.0 %collective-permute-start.7 = (bf16[128,512]{1,0:T(8,128)(2,1)S(1)}, bf16[128,512]{1,0:T(8,128)(2,1)S(1)}, u32[]{:S(2)}, u32[]{:S(2)}) collective-permute-start(bf16[128,512]{1,0:T(8,128)(2,1)S(1)} %get-tuple-element.27), channel_id=1, source_target_pairs={{192,0},{193,1},{194,2},{195,3},{196,4},{197,5},{198,6},{199,7},{2... | collective-permute-start | bytes 393224 | tf_op jit(solution)/shard_map/ppermute | solution.py:202
  26.2 7.0 %collective-permute-start.8 = (bf16[128,512]{1,0:T(8,128)(2,1)S(1)}, bf16[128,512]{1,0:T(8,128)(2,1)S(1)}, u32[]{:S(2)}, u32[]{:S(2)}) collective-permute-start(bf16[128,512]{1,0:T(8,128)(2,1)S(1)} %get-tuple-element.28), channel_id=1, source_target_pairs={{64,0},{65,1},{66,2},{67,3},{68,4},{69,5},{70,6},{71,7},{72,8},{73... | collective-permute-start | bytes 393224 | tf_op jit(solution)/shard_map/ppermute | solution.py:202
  29.5 0.7 %copy-start.8 = (f32[128]{0:T(128)S(1)}, f32[128]{0:T(128)}, u32[]{:S(2)}) copy-start(f32[128]{0:T(128)} %param.17) | copy-start | bytes 1540
  33.2 3.9 %collective-permute-start.9 = (bf16[128,512]{1,0:T(8,128)(2,1)S(1)}, bf16[128,512]{1,0:T(8,128)(2,1)S(1)}, u32[]{:S(2)}, u32[]{:S(2)}) collective-permute-start(bf16[128,512]{1,0:T(8,128)(2,1)S(1)} %get-tuple-element.32.scaled), channel_id=1, source_target_pairs={{64,0},{65,1},{66,2},{67,3},{68,4},{69,5},{70,6},{71,7},{72,8},{73... | collective-permute-start | bytes 393224 | tf_op jit(solution)/shard_map/ppermute | solution.py:202
  34.1 5.4 %collective-permute-start.10 = (bf16[128,512]{1,0:T(8,128)(2,1)S(1)}, bf16[128,512]{1,0:T(8,128)(2,1)S(1)}, u32[]{:S(2)}, u32[]{:S(2)}) collective-permute-start(bf16[128,512]{1,0:T(8,128)(2,1)S(1)} %get-tuple-element.32.scaled), channel_id=1, source_target_pairs={{128,0},{129,1},{130,2},{131,3},{132,4},{133,5},{134,6},{135,7},{1... | collective-permute-start | bytes 393224 | tf_op jit(solution)/shard_map/ppermute | solution.py:202
  34.4 6.4 %collective-permute-start.11 = (bf16[128,512]{1,0:T(8,128)(2,1)S(1)}, bf16[128,512]{1,0:T(8,128)(2,1)S(1)}, u32[]{:S(2)}, u32[]{:S(2)}) collective-permute-start(bf16[128,512]{1,0:T(8,128)(2,1)S(1)} %get-tuple-element.32.scaled), channel_id=1, source_target_pairs={{192,0},{193,1},{194,2},{195,3},{196,4},{197,5},{198,6},{199,7},{2... | collective-permute-start | bytes 393224 | tf_op jit(solution)/shard_map/ppermute | solution.py:202
  41.8 5.6 %collective-permute-start.12 = (bf16[128,1024]{1,0:T(8,128)(2,1)S(1)}, bf16[128,1024]{1,0:T(8,128)(2,1)S(1)}, u32[]{:S(2)}, u32[]{:S(2)}) collective-permute-start(bf16[128,1024]{1,0:T(8,128)(2,1)S(1)} %get-tuple-element.34), channel_id=1, source_target_pairs={{32,0},{33,1},{34,2},{35,3},{36,4},{37,5},{38,6},{39,7},{40,8},{41... | collective-permute-start | bytes 786440 | tf_op jit(solution)/shard_map/ppermute | solution.py:202
  47.5 7.3 %collective-permute-start.13 = (bf16[128,256]{1,0:T(8,128)(2,1)S(1)}, bf16[128,256]{1,0:T(8,128)(2,1)S(1)}, u32[]{:S(2)}, u32[]{:S(2)}) collective-permute-start(bf16[128,256]{1,0:T(8,128)(2,1)S(1)} %get-tuple-element.36), channel_id=1, source_target_pairs={{31,0},{0,1},{1,2},{2,3},{3,4},{4,5},{5,6},{6,7},{7,8},{8,9},{9,10... | collective-permute-start | bytes 196616 | tf_op jit(solution)/shard_map/ppermute | solution.py:202
  47.6 7.2 %collective-permute-start.14 = (bf16[128,256]{1,0:T(8,128)(2,1)S(1)}, bf16[128,256]{1,0:T(8,128)(2,1)S(1)}, u32[]{:S(2)}, u32[]{:S(2)}) collective-permute-start(bf16[128,256]{1,0:T(8,128)(2,1)S(1)} %get-tuple-element.37), channel_id=1, source_target_pairs={{1,0},{2,1},{3,2},{4,3},{5,4},{6,5},{7,6},{8,7},{9,8},{10,9},{11,1... | collective-permute-start | bytes 196616 | tf_op jit(solution)/shard_map/ppermute | solution.py:202
  52.8 2.0 %copy-start.2 = (bf16[137,128]{1,0:T(8,128)(2,1)S(1)}, bf16[137,128]{1,0:T(8,128)(2,1)}, u32[]{:S(2)}) copy-start(bf16[137,128]{1,0:T(8,128)(2,1)} %jac.3) | copy-start | bytes 105220
where the time goes:
time: 55.9 us; the launch traced here: 55.7 us
  starting transfers between devices  29.7 us (53%)
  waiting for transfers between devices  15.2 us (27%)
  Pallas kernels  6.31 us (11%)
  local copies, waits for them, and re-layouts  3.02 us (5%)
  between operations  1.43 us (3%)
    ppermute x15, starting transfers between devices, move(): return lax.ppermute(block, ('tm', 'space'), route)  29.7 us
    ppermute x15, waiting for transfers between devices, move(): return lax.ppermute(block, ('tm', 'space'), route)  15.2 us
    pallas_call x14, Pallas kernels, call(): pl.pallas_call(kernel, out_shape=[jax.ShapeDtypeStruct(shape, dtype) for...  6.31 us
    unnamed x18, local copies, waits for them, and re-layouts  3.02 us
  transfers between devices with their start and end apart: 15, of which 9 were waited for; matrix products, arithmetic and copies ran while one was open for 0% of the time, Pallas kernels for 6%

commit v1 on v0

--- a/solution.py
+++ b/solution.py
@@ -63,11 +63,6 @@
     wide[:, half + cols :] = right[...]
 
 
-def matrix_kernel(n, *refs):
-    for info, mat in zip(refs[:n], refs[n:]):
-        footprint(info, mat)
-
-
 def footprint(info, mat):
     width, obs = mat.shape
     local = info[8:9, :].astype(jnp.int32)
@@ -93,16 +88,25 @@
     return jnp.where(slot == held, 1.0 - frac, 0.0) + jnp.where(slot + 1.0 == held, frac, 0.0)
 
 
-def gather_kernel(n, mine, other, *refs):
+def gather_one(field, info, mat, out):
+    chan = out.shape[0]
+    own_slot, other_slot = held_slots()
+    both = jnp.dot(field, mat[...], preferred_element_type=F32)
+    first = slot_weight(info, own_slot)
+    second = slot_weight(info, other_slot)
+    out[...] = (first * both[:chan] + second * both[chan:]).astype(BF16)
+
+
+def gather_kernel(mine, other, info, mat, out):
+    gather_one(jnp.concatenate([mine[...], other[...]], axis=0), info, mat, out)
+
+
+def build_gather_kernel(n, mine, other, *refs):
     infos, mats, outs = refs[:n], refs[n : 2 * n], refs[2 * n :]
-    chan = mine.shape[0]
     field = jnp.concatenate([mine[...], other[...]], axis=0)
-    own_slot, other_slot = held_slots()
     for info, mat, out in zip(infos, mats, outs):
-        both = jnp.dot(field, mat[...], preferred_element_type=F32)
-        first = slot_weight(info, own_slot)
-        second = slot_weight(info, other_slot)
-        out[...] = (first * both[:chan] + second * both[chan:]).astype(BF16)
+        footprint(info, mat)
+        gather_one(field, info, mat, out)
 
 
 def turn_kernel(source, out):
@@ -130,32 +134,30 @@
     scaled[...] = (gap * scale[:, 0:1]).astype(BF16)
 
 
-def spread_part(infos, scaled, mats):
+def spread_one(info, source, mat):
     own_slot, other_slot = held_slots()
-    total = None
-    for info, source, mat in zip(infos, scaled, mats):
-        rows = source[...].astype(F32)
-        mine = (slot_weight(info, own_slot) * rows).astype(BF16)
-        other = (slot_weight(info, other_slot) * rows).astype(BF16)
-        part = lax.dot_general(
-            jnp.concatenate([mine, other], axis=0),
-            mat[...],
-            (((1,), (1,)), ((), ())),
-            preferred_element_type=F32,
-        )
-        total = part if total is None else total + part
-    return total
-
-
-def spread_own_kernel(info, scaled, mat, acc):
-    acc[...] = spread_part([info], [scaled], [mat])
-
-
-def spread_rest_kernel(n, acc, *refs):
-    infos, scaled, mats = refs[:n], refs[n : 2 * n], refs[2 * n : 3 * n]
-    own, give = refs[3 * n :]
+    rows = source[...].astype(F32)
+    mine = (slot_weight(info, own_slot) * rows).astype(BF16)
+    other = (slot_weight(info, other_slot) * rows).astype(BF16)
+    return lax.dot_general(
+        jnp.concatenate([mine, other], axis=0),
+        mat[...],
+        (((1,), (1,)), ((), ())),
+        preferred_element_type=F32,
+    )
+
+
+def spread_first_kernel(info, scaled, mat, acc):
+    acc[...] = spread_one(info, scaled, mat)
+
+
+def spread_next_kernel(before, info, scaled, mat, acc):
+    acc[...] = before[...] + spread_one(info, scaled, mat)
+
+
+def spread_last_kernel(before, info, scaled, mat, own, give):
     chan = own.shape[0]
-    total = acc[...] + spread_part(infos, scaled, mats)
+    total = before[...] + spread_one(info, scaled, mat)
     own[...] = total[:chan]
     give[...] = total[chan:].astype(BF16)
 
@@ -168,22 +170,31 @@
     right[...] = (own[:, half + cols :] + got[:, half + cols :].astype(F32)).astype(BF16)
 
 
-def finish_kernel(mid, head, tail, jac, out):
+def finish_kernel(mid, head, tail, jac, out, rows, sems):
     half = head.shape[1]
+    levels = jac.shape[0]
+    cut = (levels // 2 + 15) // 16 * 16
     first = mid[:, :half] + head[...].astype(F32)
     last = mid[:, half:] + tail[...].astype(F32)
     total = jnp.concatenate([first, last], axis=1).astype(BF16)
-    out[:, 0, :] = jnp.dot(jac[...], total, preferred_element_type=F32)
-
-
-def call(kernel, outs, *args, specs=None, scratch=(), flops=1 << 20):
+    copies = []
+    for index, part in enumerate((slice(0, cut), slice(cut, levels))):
+        rows[part, 0, :] = jnp.dot(jac[part, :], total, preferred_element_type=F32)
+        copy = pltpu.make_async_copy(rows.at[part], out.at[part], sems.at[index])
+        copy.start()
+        copies.append(copy)
+    for copy in copies:
+        copy.wait()
+
+
+def call(kernel, outs, *args, specs=None, out_specs=None, scratch=(), limit=8 << 20, flops=1 << 20):
     return pl.pallas_call(
         kernel,
         out_shape=[jax.ShapeDtypeStruct(shape, dtype) for shape, dtype in outs],
         in_specs=specs or [VMEM] * len(args),
-        out_specs=[VMEM] * len(outs),
+        out_specs=out_specs or [VMEM] * len(outs),
         scratch_shapes=scratch,
-        compiler_params=pltpu.CompilerParams(vmem_limit_bytes=8 << 20),
+        compiler_params=pltpu.CompilerParams(vmem_limit_bytes=limit),
         cost_estimate=pl.CostEstimate(flops=flops, bytes_accessed=1 << 20, transcendentals=0),
     )(*args)
 
@@ -220,6 +231,7 @@
             own.T,
             jacobian,
             specs=[HBM, HBM],
+            flops=1 << 20,
             scratch=[
                 pltpu.VMEM((levels, cols), BF16),
                 pltpu.VMEM((levels, chan), BF16),
@@ -238,19 +250,22 @@
         infos = [info] + [move(info, j, 0, 0) for j in range(1, lanes)]
         (wide,) = call(widen_kernel, [((chan, width), BF16)], full, left, right)
         other = move(wide, 0, 1, 0)
-        mats = call(functools.partial(matrix_kernel, lanes), [((width, obs), BF16)] * lanes, *infos)
+        mats = [None] * lanes
+        (mats[2],) = call(footprint, [((width, obs), BF16)], infos[2])
 
         def gather(which):
-            return call(
-                functools.partial(gather_kernel, len(which)),
-                [((chan, obs), BF16)] * len(which),
+            outs = call(
+                functools.partial(build_gather_kernel, len(which)),
+                [((width, obs), BF16)] * len(which) + [((chan, obs), BF16)] * len(which),
                 wide,
                 other,
                 *[infos[j] for j in which],
-                *[mats[j] for j in which],
             )
-
-        (far,) = gather([2])
+            for index, j in enumerate(which):
+                mats[j] = outs[index]
+            return outs[len(which) :]
+
+        (far,) = call(gather_kernel, [((chan, obs), BF16)], wide, other, infos[2], mats[2])
         far = move(far, -2, 0, 0)
         after, before = gather([1, 3])
         after, before = move(after, -1, 0, 0), move(before, 1, 0, 0)
@@ -276,15 +291,24 @@
             specs=[SMEM] + [VMEM] * (lanes + 2),
         )
         all_scaled = [scaled] + [move(scaled, j, 0, 0) for j in range(1, lanes)]
-        (acc,) = call(spread_own_kernel, [((2 * chan, width), F32)], info, scaled, mats[0])
+        (acc,) = call(spread_first_kernel, [((2 * chan, width), F32)], info, scaled, mats[0])
         (departures,) = call(turn_kernel, [((obs, chan), F32)], gaps)
+        for j in range(1, lanes - 1):
+            (acc,) = call(
+                spread_next_kernel,
+                [((2 * chan, width), F32)],
+                acc,
+                infos[j],
+                all_scaled[j],
+                mats[j],
+            )
         mine, give = call(
-            functools.partial(spread_rest_kernel, lanes - 1),
+            spread_last_kernel,
             [((chan, width), F32), ((chan, width), BF16)],
             acc,
-            *infos[1:],
-            *all_scaled[1:],
-            *mats[1:],
+            infos[lanes - 1],
+            all_scaled[lanes - 1],
+            mats[lanes - 1],
         )
         mid, to_left, to_right = call(
             join_kernel,
@@ -299,6 +323,8 @@
             move(to_right, 0, 0, -1),
             move(to_left, 0, 0, 1),
             jacobian,
+            out_specs=[HBM],
+            scratch=[pltpu.VMEM((levels, 1, cols), F32), pltpu.SemaphoreType.DMA((2,))],
         )
         return (departures, jnp.transpose(adjoint, (1, 2, 0)))
 

time: 55.9 us -> 53.2 us (0.952)
  waiting for transfers between devices: 15.2 us -> 7.78 us
  starting transfers between devices: 29.7 us -> 34.4 us
    ppermute x15, waiting for transfers between devices: 15.2 us -> 7.78 us  [move(): return lax.ppermute(block, ('tm', 'space'), route)]
    ppermute x15, starting transfers between devices: 29.7 us -> 34.4 us  [move(): return lax.ppermute(block, ('tm', 'space'), route)]
    pallas_call x14 -> x16, Pallas kernels: 6.31 us -> 6.36 us  [call(): pl.pallas_call(kernel, out_shape=[jax.ShapeDtypeStruct(shape, dtype) for...]
  transfers between devices with their start and end apart: 15 -> 15, of which waited for: 9 -> 6; matrix products, arithmetic and copies ran while one was open for 0% -> 0% of each run, Pallas kernels for 6% -> 8%
where the time goes in v1:
time: 53.2 us; the launch traced here: 53 us
  starting transfers between devices  34.4 us (65%)
  waiting for transfers between devices  7.78 us (15%)
  Pallas kernels  6.36 us (12%)
  local copies, waits for them, and re-layouts  3.02 us (6%)
  between operations  1.46 us (3%)
    ppermute x15, starting transfers between devices, move(): return lax.ppermute(block, ('tm', 'space'), route)  34.4 us
    ppermute x15, waiting for transfers between devices, move(): return lax.ppermute(block, ('tm', 'space'), route)  7.78 us
    pallas_call x16, Pallas kernels, call(): pl.pallas_call(kernel, out_shape=[jax.ShapeDtypeStruct(shape, dtype) for...  6.36 us
    unnamed x18, local copies, waits for them, and re-layouts  3.02 us
  transfers between devices with their start and end apart: 15, of which 6 were waited for; matrix products, arithmetic and copies ran while one was open for 0% of the time, Pallas kernels for 8%

profile of v1, /device:TPU:1, one launch (start us, length us, event | category | flops | bytes accessed | tf_op | source)
XLA Modules:
  0.0 53.0 jit_solution(8848874653886915171)
XLA Ops:
  0.6 0.0 copy-start.1
  0.6 0.8 %copy-done.1 = bf16[137,128]{1,0:T(8,128)(2,1)S(1)} copy-done((bf16[137,128]{1,0:T(8,128)(2,1)S(1)}, bf16[137,128]{1,0:T(8,128)(2,1)}, u32[]{:S(2)}) %copy-start.1) | copy-done | bytes 35096
  1.4 0.0 copy-start.3
  1.4 0.9 %copy-done.3 = bf16[1,512,137]{1,2,0:T(8,128)(2,1)S(1)} copy-done((bf16[1,512,137]{1,2,0:T(8,128)(2,1)S(1)}, bf16[1,512,137]{1,2,0:T(8,128)(2,1)}, u32[]{:S(2)}) %copy-start.3) | copy-done | bytes 140312
  2.3 0.4 shard_map.104
  2.8 2.1 %collective-permute-start = (bf16[128,256]{1,0:T(8,128)(2,1)S(1)}, bf16[128,256]{1,0:T(8,128)(2,1)S(1)}, u32[]{:S(2)}, u32[]{:S(2)}) collective-permute-start(bf16[128,256]{1,0:T(8,128)(2,1)S(1)} %get-tuple-element.21), channel_id=1, source_target_pairs={{31,0},{0,1},{1,2},{2,3},{3,4},{4,5},{5,6},{6,7},{7,8},{8,9},{9,10... | collective-permute-start | bytes 196616 | tf_op jit(solution)/shard_map/ppermute | solution.py:213
  4.9 6.6 %collective-permute-start.1 = (bf16[128,256]{1,0:T(8,128)(2,1)S(1)}, bf16[128,256]{1,0:T(8,128)(2,1)S(1)}, u32[]{:S(2)}, u32[]{:S(2)}) collective-permute-start(bf16[128,256]{1,0:T(8,128)(2,1)S(1)} %get-tuple-element.22), channel_id=1, source_target_pairs={{1,0},{2,1},{3,2},{4,3},{5,4},{6,5},{7,6},{8,7},{9,8},{10,9},{11,1... | collective-permute-start | bytes 196616 | tf_op jit(solution)/shard_map/ppermute | solution.py:213
  11.5 1.6 %collective-permute-done.left = bf16[128,256]{1,0:T(8,128)(2,1)S(1)} collective-permute-done((bf16[128,256]{1,0:T(8,128)(2,1)S(1)}, bf16[128,256]{1,0:T(8,128)(2,1)S(1)}, u32[]{:S(2)}, u32[]{:S(2)}) %collective-permute-start) | collective-permute-done | bytes 65568 | tf_op jit(solution)/shard_map/ppermute | solution.py:213
  13.1 0.0 collective-permute-done.1.right
  13.1 0.0 copy-start.4
  13.1 0.0 copy-start.7
  13.1 1.6 %collective-permute-start.2 = (bf16[128,1024]{1,0:T(8,128)(2,1)S(1)}, bf16[128,1024]{1,0:T(8,128)(2,1)S(1)}, u32[]{:S(2)}, u32[]{:S(2)}) collective-permute-start(bf16[128,1024]{1,0:T(8,128)(2,1)S(1)} %shard_map.105.mine), channel_id=1, source_target_pairs={{32,0},{33,1},{34,2},{35,3},{36,4},{37,5},{38,6},{39,7},{40,8},{41... | collective-permute-start | bytes 786440 | tf_op jit(solution)/shard_map/ppermute | solution.py:213
  14.8 0.0 copy-start.6
  14.8 0.0 copy-start.5
  14.8 0.0 copy-done.4
  14.8 0.0 copy-done.7
  14.8 0.7 %copy-done.6 = s32[512]{0:T(512)S(1)} copy-done((s32[512]{0:T(512)S(1)}, s32[512]{0:T(512)}, u32[]{:S(2)}) %copy-start.6) | copy-done | bytes 2072
  15.4 0.0 copy-done.5
  15.5 3.0 %collective-permute-start.3 = (f32[16,512]{1,0:T(8,128)S(1)}, f32[16,512]{1,0:T(8,128)S(1)}, u32[]{:S(2)}, u32[]{:S(2)}) collective-permute-start(f32[16,512]{1,0:T(8,128)S(1)} %shard_map.106.refs_0_.info), channel_id=1, source_target_pairs={{128,0},{129,1},{130,2},{131,3},{132,4},{133,5},{134,6},{135,7},{1... | collective-permute-start | bytes 98312 | tf_op jit(solution)/shard_map/ppermute | solution.py:213
  18.5 0.8 %collective-permute-start.5 = (f32[16,512]{1,0:T(8,128)S(1)}, f32[16,512]{1,0:T(8,128)S(1)}, u32[]{:S(2)}, u32[]{:S(2)}) collective-permute-start(f32[16,512]{1,0:T(8,128)S(1)} %shard_map.106.refs_0_.info), channel_id=1, source_target_pairs={{64,0},{65,1},{66,2},{67,3},{68,4},{69,5},{70,6},{71,7},{72,8},{73... | collective-permute-start | bytes 98312 | tf_op jit(solution)/shard_map/ppermute | solution.py:213
  19.2 0.7 %collective-permute-start.6 = (f32[16,512]{1,0:T(8,128)S(1)}, f32[16,512]{1,0:T(8,128)S(1)}, u32[]{:S(2)}, u32[]{:S(2)}) collective-permute-start(f32[16,512]{1,0:T(8,128)S(1)} %shard_map.106.refs_0_.info), channel_id=1, source_target_pairs={{192,0},{193,1},{194,2},{195,3},{196,4},{197,5},{198,6},{199,7},{2... | collective-permute-start | bytes 98312 | tf_op jit(solution)/shard_map/ppermute | solution.py:213
  19.9 0.0 collective-permute-done.3.info
  19.9 0.2 shard_map.108.mat
  20.1 0.0 collective-permute-done.2.other
  20.1 0.4 shard_map.109
  20.5 0.0 copy-start
  20.6 2.9 %collective-permute-start.4 = (bf16[128,512]{1,0:T(8,128)(2,1)S(1)}, bf16[128,512]{1,0:T(8,128)(2,1)S(1)}, u32[]{:S(2)}, u32[]{:S(2)}) collective-permute-start(bf16[128,512]{1,0:T(8,128)(2,1)S(1)} %shard_map.109), channel_id=1, source_target_pairs={{128,0},{129,1},{130,2},{131,3},{132,4},{133,5},{134,6},{135,7},{1... | collective-permute-start | bytes 393224 | tf_op jit(solution)/shard_map/ppermute | solution.py:213
  23.4 0.0 collective-permute-done.5.refs_0_.info
  23.5 0.0 collective-permute-done.6.refs_1_.info
  23.5 0.8 %shard_map.110 = (bf16[1024,512]{1,0:T(8,128)(2,1)S(1)}, bf16[1024,512]{1,0:T(8,128)(2,1)S(1)}, bf16[128,512]{1,0:T(8,128)(2,1)S(1)}, bf16[128,512]{1,0:T(8,128)(2,1)S(1)}) custom-call(bf16[128,1024]{1,0:T(8,128)(2,1)S(1)} %shard_map.105.mine, bf16[128,1024]{1,0:T(8,128)(2,1)S(1)} %collective-permute-done.2.other, ...), custom_call_target="tpu_custom_call" | custom-call | flops 1048576 | bytes 1048576 | tf_op jit(solution)/shard_map/pallas_call | solution.py:191
  24.2 0.5 collective-permute-start.7
  24.7 2.3 %collective-permute-start.8 = (bf16[128,512]{1,0:T(8,128)(2,1)S(1)}, bf16[128,512]{1,0:T(8,128)(2,1)S(1)}, u32[]{:S(2)}, u32[]{:S(2)}) collective-permute-start(bf16[128,512]{1,0:T(8,128)(2,1)S(1)} %get-tuple-element.25), channel_id=1, source_target_pairs={{64,0},{65,1},{66,2},{67,3},{68,4},{69,5},{70,6},{71,7},{72,8},{73... | collective-permute-start | bytes 393224 | tf_op jit(solution)/shard_map/ppermute | solution.py:213
  27.6 0.0 copy-start.8
  27.6 0.0 copy-done
  27.6 0.6 %copy-done.8 = f32[128]{0:T(128)S(1)} copy-done((f32[128]{0:T(128)S(1)}, f32[128]{0:T(128)}, u32[]{:S(2)}) %copy-start.8) | copy-done | bytes 536
  28.3 0.3 shard_map.111
  28.6 0.5 shard_map.107
  29.0 0.0 collective-permute-done.4.refs_1_
  29.1 0.3 collective-permute-done.7.refs_2_
  29.3 0.0 collective-permute-done.8.refs_3_
  29.3 0.1 shard_map.112
  29.4 2.9 %collective-permute-start.9 = (bf16[128,512]{1,0:T(8,128)(2,1)S(1)}, bf16[128,512]{1,0:T(8,128)(2,1)S(1)}, u32[]{:S(2)}, u32[]{:S(2)}) collective-permute-start(bf16[128,512]{1,0:T(8,128)(2,1)S(1)} %get-tuple-element.29.scaled), channel_id=1, source_target_pairs={{64,0},{65,1},{66,2},{67,3},{68,4},{69,5},{70,6},{71,7},{72,8},{73... | collective-permute-start | bytes 393224 | tf_op jit(solution)/shard_map/ppermute | solution.py:213
  32.4 0.9 %collective-permute-start.10 = (bf16[128,512]{1,0:T(8,128)(2,1)S(1)}, bf16[128,512]{1,0:T(8,128)(2,1)S(1)}, u32[]{:S(2)}, u32[]{:S(2)}) collective-permute-start(bf16[128,512]{1,0:T(8,128)(2,1)S(1)} %get-tuple-element.29.scaled), channel_id=1, source_target_pairs={{128,0},{129,1},{130,2},{131,3},{132,4},{133,5},{134,6},{135,7},{1... | collective-permute-start | bytes 393224 | tf_op jit(solution)/shard_map/ppermute | solution.py:213
  33.3 0.8 %collective-permute-start.11 = (bf16[128,512]{1,0:T(8,128)(2,1)S(1)}, bf16[128,512]{1,0:T(8,128)(2,1)S(1)}, u32[]{:S(2)}, u32[]{:S(2)}) collective-permute-start(bf16[128,512]{1,0:T(8,128)(2,1)S(1)} %get-tuple-element.29.scaled), channel_id=1, source_target_pairs={{192,0},{193,1},{194,2},{195,3},{196,4},{197,5},{198,6},{199,7},{2... | collective-permute-start | bytes 393224 | tf_op jit(solution)/shard_map/ppermute | solution.py:213
  34.1 0.5 shard_map.114.before
  34.5 0.0 collective-permute-done.9.scaled
  34.5 0.5 shard_map.115.before
  35.0 2.7 %collective-permute-done.10.scaled = bf16[128,512]{1,0:T(8,128)(2,1)S(1)} collective-permute-done((bf16[128,512]{1,0:T(8,128)(2,1)S(1)}, bf16[128,512]{1,0:T(8,128)(2,1)S(1)}, u32[]{:S(2)}, u32[]{:S(2)}) %collective-permute-start.10) | collective-permute-done | bytes 131104 | tf_op jit(solution)/shard_map/ppermute | solution.py:213
  37.8 0.5 shard_map.116.before
  38.2 0.8 %collective-permute-done.11.scaled = bf16[128,512]{1,0:T(8,128)(2,1)S(1)} collective-permute-done((bf16[128,512]{1,0:T(8,128)(2,1)S(1)}, bf16[128,512]{1,0:T(8,128)(2,1)S(1)}, u32[]{:S(2)}, u32[]{:S(2)}) %collective-permute-start.11) | collective-permute-done | bytes 131104 | tf_op jit(solution)/shard_map/ppermute | solution.py:213
  39.1 0.5 shard_map.117
  39.6 4.0 %collective-permute-start.12 = (bf16[128,1024]{1,0:T(8,128)(2,1)S(1)}, bf16[128,1024]{1,0:T(8,128)(2,1)S(1)}, u32[]{:S(2)}, u32[]{:S(2)}) collective-permute-start(bf16[128,1024]{1,0:T(8,128)(2,1)S(1)} %get-tuple-element.34), channel_id=1, source_target_pairs={{32,0},{33,1},{34,2},{35,3},{36,4},{37,5},{38,6},{39,7},{40,8},{41... | collective-permute-start | bytes 786440 | tf_op jit(solution)/shard_map/ppermute | solution.py:213
  43.5 1.2 %collective-permute-done.12.got = bf16[128,1024]{1,0:T(8,128)(2,1)S(1)} collective-permute-done((bf16[128,1024]{1,0:T(8,128)(2,1)S(1)}, bf16[128,1024]{1,0:T(8,128)(2,1)S(1)}, u32[]{:S(2)}, u32[]{:S(2)}) %collective-permute-start.12) | collective-permute-done | bytes 262176 | tf_op jit(solution)/shard_map/ppermute | solution.py:213
  44.7 0.1 shard_map.118
  44.8 0.1 collective-permute-start.13
  44.8 5.2 %collective-permute-start.14 = (bf16[128,256]{1,0:T(8,128)(2,1)S(1)}, bf16[128,256]{1,0:T(8,128)(2,1)S(1)}, u32[]{:S(2)}, u32[]{:S(2)}) collective-permute-start(bf16[128,256]{1,0:T(8,128)(2,1)S(1)} %get-tuple-element.37), channel_id=1, source_target_pairs={{1,0},{2,1},{3,2},{4,3},{5,4},{6,5},{7,6},{8,7},{9,8},{10,9},{11,1... | collective-permute-start | bytes 196616 | tf_op jit(solution)/shard_map/ppermute | solution.py:213
  50.1 0.0 copy-start.2
  50.1 0.8 %shard_map.113 = f32[512,128]{1,0:T(8,128)} custom-call(f32[128,512]{1,0:T(8,128)S(1)} %get-tuple-element.28.source), custom_call_target="tpu_custom_call" | custom-call | flops 1048576 | bytes 1048576 | tf_op jit(solution)/shard_map/pallas_call | solution.py:191
  50.9 1.2 %collective-permute-done.13.head = bf16[128,256]{1,0:T(8,128)(2,1)S(1)} collective-permute-done((bf16[128,256]{1,0:T(8,128)(2,1)S(1)}, bf16[128,256]{1,0:T(8,128)(2,1)S(1)}, u32[]{:S(2)}, u32[]{:S(2)}) %collective-permute-start.13) | collective-permute-done | bytes 65568 | tf_op jit(solution)/shard_map/ppermute | solution.py:213
  52.1 0.0 collective-permute-done.14.tail
  52.1 0.0 copy-done.2
  52.1 0.9 %shard_map.119 = f32[137,1,512]{2,1,0:T(1,128)} custom-call(f32[128,512]{1,0:T(8,128)S(1)} %get-tuple-element.35.mid, bf16[128,256]{1,0:T(8,128)(2,1)S(1)} %collective-permute-done.13.head, bf16[128,256]{1,0:T(8,128)(2,1)S(1)} %collective-permute-done.14.tail, bf16[137,128]{1,0:T(8,128)(2,1)S(1)} %copy-done.2), custom_call_target="tpu_custom_call" | custom-call | flops 1048576 | bytes 1048576 | tf_op jit(solution)/shard_map/pallas_call | solution.py:191
  (2 shorter events, 0.0 us)
Async XLA Ops:
  0.6 0.8 %copy-start.1 = (bf16[137,128]{1,0:T(8,128)(2,1)S(1)}, bf16[137,128]{1,0:T(8,128)(2,1)}, u32[]{:S(2)}) copy-start(bf16[137,128]{1,0:T(8,128)(2,1)} %jac.3) | copy-start | bytes 105220
  1.4 0.9 %copy-start.3 = (bf16[1,512,137]{1,2,0:T(8,128)(2,1)S(1)}, bf16[1,512,137]{1,2,0:T(8,128)(2,1)}, u32[]{:S(2)}) copy-start(bf16[1,512,137]{1,2,0:T(8,128)(2,1)} %param.9) | copy-start | bytes 420868
  2.8 10.3 %collective-permute-start = (bf16[128,256]{1,0:T(8,128)(2,1)S(1)}, bf16[128,256]{1,0:T(8,128)(2,1)S(1)}, u32[]{:S(2)}, u32[]{:S(2)}) collective-permute-start(bf16[128,256]{1,0:T(8,128)(2,1)S(1)} %get-tuple-element.21), channel_id=1, source_target_pairs={{31,0},{0,1},{1,2},{2,3},{3,4},{4,5},{5,6},{6,7},{7,8},{8,9},{9,10... | collective-permute-start | bytes 196616 | tf_op jit(solution)/shard_map/ppermute | solution.py:213
  4.9 8.2 %collective-permute-start.1 = (bf16[128,256]{1,0:T(8,128)(2,1)S(1)}, bf16[128,256]{1,0:T(8,128)(2,1)S(1)}, u32[]{:S(2)}, u32[]{:S(2)}) collective-permute-start(bf16[128,256]{1,0:T(8,128)(2,1)S(1)} %get-tuple-element.22), channel_id=1, source_target_pairs={{1,0},{2,1},{3,2},{4,3},{5,4},{6,5},{7,6},{8,7},{9,8},{10,9},{11,1... | collective-permute-start | bytes 196616 | tf_op jit(solution)/shard_map/ppermute | solution.py:213
  13.1 1.7 %copy-start.4 = (bf16[512,8]{0,1:T(8,128)(2,1)S(1)}, bf16[512,8]{0,1:T(8,128)(2,1)}, u32[]{:S(2)}) copy-start(bf16[512,8]{0,1:T(8,128)(2,1)} %param.11) | copy-start | bytes 24580
  13.1 1.7 %copy-start.7 = (f32[512]{0:T(512)S(1)}, f32[512]{0:T(512)}, u32[]{:S(2)}) copy-start(f32[512]{0:T(512)} %param.13) | copy-start | bytes 6148
  13.1 7.0 %collective-permute-start.2 = (bf16[128,1024]{1,0:T(8,128)(2,1)S(1)}, bf16[128,1024]{1,0:T(8,128)(2,1)S(1)}, u32[]{:S(2)}, u32[]{:S(2)}) collective-permute-start(bf16[128,1024]{1,0:T(8,128)(2,1)S(1)} %shard_map.105.mine), channel_id=1, source_target_pairs={{32,0},{33,1},{34,2},{35,3},{36,4},{37,5},{38,6},{39,7},{40,8},{41... | collective-permute-start | bytes 786440 | tf_op jit(solution)/shard_map/ppermute | solution.py:213
  14.8 0.7 %copy-start.6 = (s32[512]{0:T(512)S(1)}, s32[512]{0:T(512)}, u32[]{:S(2)}) copy-start(s32[512]{0:T(512)} %param.12) | copy-start | bytes 6148
  14.8 0.7 %copy-start.5 = (s32[512]{0:T(512)S(1)}, s32[512]{0:T(512)}, u32[]{:S(2)}) copy-start(s32[512]{0:T(512)} %param.10) | copy-start | bytes 6148
  15.5 4.5 %collective-permute-start.3 = (f32[16,512]{1,0:T(8,128)S(1)}, f32[16,512]{1,0:T(8,128)S(1)}, u32[]{:S(2)}, u32[]{:S(2)}) collective-permute-start(f32[16,512]{1,0:T(8,128)S(1)} %shard_map.106.refs_0_.info), channel_id=1, source_target_pairs={{128,0},{129,1},{130,2},{131,3},{132,4},{133,5},{134,6},{135,7},{1... | collective-permute-start | bytes 98312 | tf_op jit(solution)/shard_map/ppermute | solution.py:213
  18.5 5.0 %collective-permute-start.5 = (f32[16,512]{1,0:T(8,128)S(1)}, f32[16,512]{1,0:T(8,128)S(1)}, u32[]{:S(2)}, u32[]{:S(2)}) collective-permute-start(f32[16,512]{1,0:T(8,128)S(1)} %shard_map.106.refs_0_.info), channel_id=1, source_target_pairs={{64,0},{65,1},{66,2},{67,3},{68,4},{69,5},{70,6},{71,7},{72,8},{73... | collective-permute-start | bytes 98312 | tf_op jit(solution)/shard_map/ppermute | solution.py:213
  19.2 4.2 %collective-permute-start.6 = (f32[16,512]{1,0:T(8,128)S(1)}, f32[16,512]{1,0:T(8,128)S(1)}, u32[]{:S(2)}, u32[]{:S(2)}) collective-permute-start(f32[16,512]{1,0:T(8,128)S(1)} %shard_map.106.refs_0_.info), channel_id=1, source_target_pairs={{192,0},{193,1},{194,2},{195,3},{196,4},{197,5},{198,6},{199,7},{2... | collective-permute-start | bytes 98312 | tf_op jit(solution)/shard_map/ppermute | solution.py:213
  20.5 7.1 %copy-start = (f32[512,128]{1,0:T(8,128)S(1)}, f32[512,128]{1,0:T(8,128)}, u32[]{:S(2)}) copy-start(f32[512,128]{1,0:T(8,128)} %source.1) | copy-start | bytes 786436
  20.6 8.5 %collective-permute-start.4 = (bf16[128,512]{1,0:T(8,128)(2,1)S(1)}, bf16[128,512]{1,0:T(8,128)(2,1)S(1)}, u32[]{:S(2)}, u32[]{:S(2)}) collective-permute-start(bf16[128,512]{1,0:T(8,128)(2,1)S(1)} %shard_map.109), channel_id=1, source_target_pairs={{128,0},{129,1},{130,2},{131,3},{132,4},{133,5},{134,6},{135,7},{1... | collective-permute-start | bytes 393224 | tf_op jit(solution)/shard_map/ppermute | solution.py:213
  24.2 5.1 %collective-permute-start.7 = (bf16[128,512]{1,0:T(8,128)(2,1)S(1)}, bf16[128,512]{1,0:T(8,128)(2,1)S(1)}, u32[]{:S(2)}, u32[]{:S(2)}) collective-permute-start(bf16[128,512]{1,0:T(8,128)(2,1)S(1)} %get-tuple-element.24), channel_id=1, source_target_pairs={{192,0},{193,1},{194,2},{195,3},{196,4},{197,5},{198,6},{199,7},{2... | collective-permute-start | bytes 393224 | tf_op jit(solution)/shard_map/ppermute | solution.py:213
  24.7 4.6 %collective-permute-start.8 = (bf16[128,512]{1,0:T(8,128)(2,1)S(1)}, bf16[128,512]{1,0:T(8,128)(2,1)S(1)}, u32[]{:S(2)}, u32[]{:S(2)}) collective-permute-start(bf16[128,512]{1,0:T(8,128)(2,1)S(1)} %get-tuple-element.25), channel_id=1, source_target_pairs={{64,0},{65,1},{66,2},{67,3},{68,4},{69,5},{70,6},{71,7},{72,8},{73... | collective-permute-start | bytes 393224 | tf_op jit(solution)/shard_map/ppermute | solution.py:213
  27.6 0.7 %copy-start.8 = (f32[128]{0:T(128)S(1)}, f32[128]{0:T(128)}, u32[]{:S(2)}) copy-start(f32[128]{0:T(128)} %param.17) | copy-start | bytes 1540
  29.4 5.1 %collective-permute-start.9 = (bf16[128,512]{1,0:T(8,128)(2,1)S(1)}, bf16[128,512]{1,0:T(8,128)(2,1)S(1)}, u32[]{:S(2)}, u32[]{:S(2)}) collective-permute-start(bf16[128,512]{1,0:T(8,128)(2,1)S(1)} %get-tuple-element.29.scaled), channel_id=1, source_target_pairs={{64,0},{65,1},{66,2},{67,3},{68,4},{69,5},{70,6},{71,7},{72,8},{73... | collective-permute-start | bytes 393224 | tf_op jit(solution)/shard_map/ppermute | solution.py:213
  32.4 5.4 %collective-permute-start.10 = (bf16[128,512]{1,0:T(8,128)(2,1)S(1)}, bf16[128,512]{1,0:T(8,128)(2,1)S(1)}, u32[]{:S(2)}, u32[]{:S(2)}) collective-permute-start(bf16[128,512]{1,0:T(8,128)(2,1)S(1)} %get-tuple-element.29.scaled), channel_id=1, source_target_pairs={{128,0},{129,1},{130,2},{131,3},{132,4},{133,5},{134,6},{135,7},{1... | collective-permute-start | bytes 393224 | tf_op jit(solution)/shard_map/ppermute | solution.py:213
  33.3 5.8 %collective-permute-start.11 = (bf16[128,512]{1,0:T(8,128)(2,1)S(1)}, bf16[128,512]{1,0:T(8,128)(2,1)S(1)}, u32[]{:S(2)}, u32[]{:S(2)}) collective-permute-start(bf16[128,512]{1,0:T(8,128)(2,1)S(1)} %get-tuple-element.29.scaled), channel_id=1, source_target_pairs={{192,0},{193,1},{194,2},{195,3},{196,4},{197,5},{198,6},{199,7},{2... | collective-permute-start | bytes 393224 | tf_op jit(solution)/shard_map/ppermute | solution.py:213
  39.6 5.1 %collective-permute-start.12 = (bf16[128,1024]{1,0:T(8,128)(2,1)S(1)}, bf16[128,1024]{1,0:T(8,128)(2,1)S(1)}, u32[]{:S(2)}, u32[]{:S(2)}) collective-permute-start(bf16[128,1024]{1,0:T(8,128)(2,1)S(1)} %get-tuple-element.34), channel_id=1, source_target_pairs={{32,0},{33,1},{34,2},{35,3},{36,4},{37,5},{38,6},{39,7},{40,8},{41... | collective-permute-start | bytes 786440 | tf_op jit(solution)/shard_map/ppermute | solution.py:213
  44.8 7.3 %collective-permute-start.13 = (bf16[128,256]{1,0:T(8,128)(2,1)S(1)}, bf16[128,256]{1,0:T(8,128)(2,1)S(1)}, u32[]{:S(2)}, u32[]{:S(2)}) collective-permute-start(bf16[128,256]{1,0:T(8,128)(2,1)S(1)} %get-tuple-element.36), channel_id=1, source_target_pairs={{31,0},{0,1},{1,2},{2,3},{3,4},{4,5},{5,6},{6,7},{7,8},{8,9},{9,10... | collective-permute-start | bytes 196616 | tf_op jit(solution)/shard_map/ppermute | solution.py:213
  44.8 7.2 %collective-permute-start.14 = (bf16[128,256]{1,0:T(8,128)(2,1)S(1)}, bf16[128,256]{1,0:T(8,128)(2,1)S(1)}, u32[]{:S(2)}, u32[]{:S(2)}) collective-permute-start(bf16[128,256]{1,0:T(8,128)(2,1)S(1)} %get-tuple-element.37), channel_id=1, source_target_pairs={{1,0},{2,1},{3,2},{4,3},{5,4},{6,5},{7,6},{8,7},{9,8},{10,9},{11,1... | collective-permute-start | bytes 196616 | tf_op jit(solution)/shard_map/ppermute | solution.py:213
  50.1 2.0 %copy-start.2 = (bf16[137,128]{1,0:T(8,128)(2,1)S(1)}, bf16[137,128]{1,0:T(8,128)(2,1)}, u32[]{:S(2)}) copy-start(bf16[137,128]{1,0:T(8,128)(2,1)} %jac.3) | copy-start | bytes 105220

commit v2 on v1

--- a/solution.py
+++ b/solution.py
@@ -23,7 +23,23 @@
     return turn.astype(F32), (turn ^ 1).astype(F32)
 
 
-def project_kernel(state, jac, full, head, tail, field, levels, sems):
+def even_tile():
+    return lax.axis_index("space") % 2 == 0
+
+
+def put_rims(near, far, left, right):
+    @pl.when(even_tile())
+    def _():
+        near[...] = right
+        far[...] = left
+
+    @pl.when(jnp.logical_not(even_tile()))
+    def _():
+        near[...] = left
+        far[...] = right
+
+
+def project_kernel(state, jac, full, near, far, field, levels, sems):
     half = full.shape[1] // 2
     copies = [
         pltpu.make_async_copy(state, field, sems.at[0]),
@@ -37,8 +53,7 @@
         levels[...], field[...], (((0,), (0,)), ((), ())), preferred_element_type=F32
     ).astype(BF16)
     full[...] = out
-    head[...] = out[:, :half]
-    tail[...] = out[:, half:]
+    put_rims(near, far, out[:, :half], out[:, half:])
 
 
 def info_kernel(cols, tiles, start, weight, slot, frac, info):
@@ -55,12 +70,20 @@
     info[8:16, :] = extra
 
 
-def widen_kernel(full, left, right, wide):
+def widen_kernel(full, near, far, wide):
     cols = full.shape[1]
     half = cols // 2
-    wide[:, :half] = left[...]
     wide[:, half : half + cols] = full[...]
-    wide[:, half + cols :] = right[...]
+
+    @pl.when(even_tile())
+    def _():
+        wide[:, :half] = far[...]
+        wide[:, half + cols :] = near[...]
+
+    @pl.when(jnp.logical_not(even_tile()))
+    def _():
+        wide[:, :half] = near[...]
+        wide[:, half + cols :] = far[...]
 
 
 def footprint(info, mat):
@@ -162,20 +185,22 @@
     give[...] = total[chan:].astype(BF16)
 
 
-def join_kernel(own, got, mid, left, right):
+def join_kernel(own, got, mid, near, far):
     cols = mid.shape[1]
     half = cols // 2
     mid[...] = own[:, half : half + cols] + got[:, half : half + cols].astype(F32)
-    left[...] = (own[:, :half] + got[:, :half].astype(F32)).astype(BF16)
-    right[...] = (own[:, half + cols :] + got[:, half + cols :].astype(F32)).astype(BF16)
-
-
-def finish_kernel(mid, head, tail, jac, out, rows, sems):
-    half = head.shape[1]
+    left = (own[:, :half] + got[:, :half].astype(F32)).astype(BF16)
+    right = (own[:, half + cols :] + got[:, half + cols :].astype(F32)).astype(BF16)
+    put_rims(near, far, left, right)
+
+
+def finish_kernel(mid, near, far, jac, out, rows, sems):
+    half = near.shape[1]
     levels = jac.shape[0]
     cut = (levels // 2 + 15) // 16 * 16
-    first = mid[:, :half] + head[...].astype(F32)
-    last = mid[:, half:] + tail[...].astype(F32)
+    even = even_tile()
+    first = mid[:, :half] + jnp.where(even, far[...], near[...]).astype(F32)
+    last = mid[:, half:] + jnp.where(even, near[...], far[...]).astype(F32)
     total = jnp.concatenate([first, last], axis=1).astype(BF16)
     copies = []
     for index, part in enumerate((slice(0, cut), slice(cut, levels))):
@@ -202,14 +227,17 @@
 def make_body(n_tm, n_space):
     lanes = n_tm // 2
 
-    def move(block, turn, swap, shift):
+    def swap(block, y=0, core=0, tile=None):
+        partner = {
+            None: lambda s: s,
+            "near": lambda s: s ^ 1,
+            "far": lambda s: (s + 1 if s % 2 else s - 1) % n_space,
+        }[tile]
         route = []
         for t in range(n_tm):
             for s in range(n_space):
-                y, core = t // 2, t % 2
-                t_from = ((y + turn) % lanes) * 2 + (core ^ swap)
-                s_from = (s + shift) % n_space
-                route.append((t_from * n_space + s_from, t * n_space + s))
+                other = (t // 2 ^ y) * 2 + (t % 2 ^ core)
+                route.append((other * n_space + partner(s), t * n_space + s))
         return lax.ppermute(block, ("tm", "space"), route)
 
     def steps(
@@ -225,7 +253,7 @@
         def flat(vector):
             return vector.reshape(1, -1)
 
-        full, head, tail = call(
+        full, near, far = call(
             project_kernel,
             [((chan, cols), BF16), ((chan, half), BF16), ((chan, half), BF16)],
             own.T,
@@ -246,10 +274,10 @@
             flat(obs_slot),
             flat(obs_frac),
         )
-        left, right = move(tail, 0, 0, -1), move(head, 0, 0, 1)
-        infos = [info] + [move(info, j, 0, 0) for j in range(1, lanes)]
-        (wide,) = call(widen_kernel, [((chan, width), BF16)], full, left, right)
-        other = move(wide, 0, 1, 0)
+        near, far = swap(near, tile="near"), swap(far, tile="far")
+        infos = [info] + [swap(info, y=j) for j in range(1, lanes)]
+        (wide,) = call(widen_kernel, [((chan, width), BF16)], full, near, far)
+        other = swap(wide, core=1)
         mats = [None] * lanes
         (mats[2],) = call(footprint, [((width, obs), BF16)], infos[2])
 
@@ -266,10 +294,11 @@
             return outs[len(which) :]
 
         (far,) = call(gather_kernel, [((chan, obs), BF16)], wide, other, infos[2], mats[2])
-        far = move(far, -2, 0, 0)
-        after, before = gather([1, 3])
-        after, before = move(after, -1, 0, 0), move(before, 1, 0, 0)
-        (kept,) = gather([0])
+        parts = [None] * lanes
+        parts[2] = swap(far, y=2)
+        for j, part in zip((1, 3), gather([1, 3])):
+            parts[j] = swap(part, y=j)
+        (parts[0],) = gather([0])
         values, scale = call(
             values_kernel,
             [((chan, obs), F32), ((chan, chan), F32)],
@@ -282,15 +311,12 @@
             functools.partial(depart_kernel, lanes),
             [((chan, obs), F32), ((chan, obs), BF16)],
             live_count,
-            kept,
-            far,
-            after,
-            before,
+            *parts,
             values,
             scale,
             specs=[SMEM] + [VMEM] * (lanes + 2),
         )
-        all_scaled = [scaled] + [move(scaled, j, 0, 0) for j in range(1, lanes)]
+        all_scaled = [scaled] + [swap(scaled, y=j) for j in range(1, lanes)]
         (acc,) = call(spread_first_kernel, [((2 * chan, width), F32)], info, scaled, mats[0])
         (departures,) = call(turn_kernel, [((obs, chan), F32)], gaps)
         for j in range(1, lanes - 1):
@@ -310,18 +336,18 @@
             all_scaled[lanes - 1],
             mats[lanes - 1],
         )
-        mid, to_left, to_right = call(
+        mid, near, far = call(
             join_kernel,
             [((chan, cols), F32)] + [((chan, half), BF16)] * 2,
             mine,
-            move(give, 0, 1, 0),
+            swap(give, core=1),
         )
         (adjoint,) = call(
             finish_kernel,
             [((levels, 1, cols), F32)],
             mid,
-            move(to_right, 0, 0, -1),
-            move(to_left, 0, 0, 1),
+            swap(near, tile="near"),
+            swap(far, tile="far"),
             jacobian,
             out_specs=[HBM],
             scratch=[pltpu.VMEM((levels, 1, cols), F32), pltpu.SemaphoreType.DMA((2,))],

time: 53.2 us -> 56.6 us (1.064)
  waiting for transfers between devices: 7.78 us -> 15.7 us
  starting transfers between devices: 34.4 us -> 29.8 us
    ppermute x15, waiting for transfers between devices: 7.78 us -> 15.7 us  [swap(): return lax.ppermute(block, ('tm', 'space'), route)]
    ppermute x15, starting transfers between devices: 34.4 us -> 29.8 us  [swap(): return lax.ppermute(block, ('tm', 'space'), route)]
  transfers between devices with their start and end apart: 15 -> 15, of which waited for: 6 -> 10; matrix products, arithmetic and copies ran while one was open for 0% -> 0% of each run, Pallas kernels for 8% -> 6%
where the time goes in v2:
time: 56.6 us; the launch traced here: 56.4 us
  starting transfers between devices  29.8 us (53%)
  waiting for transfers between devices  15.7 us (28%)
  Pallas kernels  6.38 us (11%)
  local copies, waits for them, and re-layouts  3.02 us (5%)
  between operations  1.47 us (3%)
    ppermute x15, starting transfers between devices, swap(): return lax.ppermute(block, ('tm', 'space'), route)  29.8 us
    ppermute x15, waiting for transfers between devices, swap(): return lax.ppermute(block, ('tm', 'space'), route)  15.7 us
    pallas_call x16, Pallas kernels, call(): pl.pallas_call(kernel, out_shape=[jax.ShapeDtypeStruct(shape, dtype) for...  6.38 us
    unnamed x18, local copies, waits for them, and re-layouts  3.02 us
  transfers between devices with their start and end apart: 15, of which 10 were waited for; matrix products, arithmetic and copies ran while one was open for 0% of the time, Pallas kernels for 6%

profile of v2, /device:TPU:1, one launch (start us, length us, event | category | flops | bytes accessed | tf_op | source)
XLA Modules:
  0.0 56.4 jit_solution(2735774340023787466)
XLA Ops:
  0.6 0.0 copy-start.1
  0.6 0.8 %copy-done.1 = bf16[137,128]{1,0:T(8,128)(2,1)S(1)} copy-done((bf16[137,128]{1,0:T(8,128)(2,1)S(1)}, bf16[137,128]{1,0:T(8,128)(2,1)}, u32[]{:S(2)}) %copy-start.1) | copy-done | bytes 35096
  1.4 0.0 copy-start.3
  1.4 0.9 %copy-done.3 = bf16[1,512,137]{1,2,0:T(8,128)(2,1)S(1)} copy-done((bf16[1,512,137]{1,2,0:T(8,128)(2,1)S(1)}, bf16[1,512,137]{1,2,0:T(8,128)(2,1)}, u32[]{:S(2)}) %copy-start.3) | copy-done | bytes 140312
  2.3 0.5 shard_map.104
  2.8 2.1 %collective-permute-start = (bf16[128,256]{1,0:T(8,128)(2,1)S(1)}, bf16[128,256]{1,0:T(8,128)(2,1)S(1)}, u32[]{:S(2)}, u32[]{:S(2)}) collective-permute-start(bf16[128,256]{1,0:T(8,128)(2,1)S(1)} %get-tuple-element.21), channel_id=1, source_target_pairs={{1,0},{0,1},{3,2},{2,3},{5,4},{4,5},{7,6},{6,7},{9,8},{8,9},{11,10... | collective-permute-start | bytes 196616 | tf_op jit(solution)/shard_map/ppermute | solution.py:241
  4.9 7.1 %collective-permute-start.1 = (bf16[128,256]{1,0:T(8,128)(2,1)S(1)}, bf16[128,256]{1,0:T(8,128)(2,1)S(1)}, u32[]{:S(2)}, u32[]{:S(2)}) collective-permute-start(bf16[128,256]{1,0:T(8,128)(2,1)S(1)} %get-tuple-element.22), channel_id=1, source_target_pairs={{31,0},{2,1},{1,2},{4,3},{3,4},{6,5},{5,6},{8,7},{7,8},{10,9},{9,1... | collective-permute-start | bytes 196616 | tf_op jit(solution)/shard_map/ppermute | solution.py:241
  12.0 0.0 collective-permute-done.near
  12.0 1.6 %collective-permute-done.1.far = bf16[128,256]{1,0:T(8,128)(2,1)S(1)} collective-permute-done((bf16[128,256]{1,0:T(8,128)(2,1)S(1)}, bf16[128,256]{1,0:T(8,128)(2,1)S(1)}, u32[]{:S(2)}, u32[]{:S(2)}) %collective-permute-start.1) | collective-permute-done | bytes 65568 | tf_op jit(solution)/shard_map/ppermute | solution.py:241
  13.6 0.0 copy-start.4
  13.6 0.0 copy-start.7
  13.7 1.9 %collective-permute-start.2 = (bf16[128,1024]{1,0:T(8,128)(2,1)S(1)}, bf16[128,1024]{1,0:T(8,128)(2,1)S(1)}, u32[]{:S(2)}, u32[]{:S(2)}) collective-permute-start(bf16[128,1024]{1,0:T(8,128)(2,1)S(1)} %shard_map.105.mine), channel_id=1, source_target_pairs={{32,0},{33,1},{34,2},{35,3},{36,4},{37,5},{38,6},{39,7},{40,8},{41... | collective-permute-start | bytes 786440 | tf_op jit(solution)/shard_map/ppermute | solution.py:241
  15.6 0.0 copy-start.6
  15.6 0.0 copy-start.5
  15.6 0.0 copy-done.4
  15.6 0.0 copy-done.7
  15.6 0.7 %copy-done.6 = s32[512]{0:T(512)S(1)} copy-done((s32[512]{0:T(512)S(1)}, s32[512]{0:T(512)}, u32[]{:S(2)}) %copy-start.6) | copy-done | bytes 2072
  16.3 0.0 copy-done.5
  16.3 3.0 %collective-permute-start.6 = (f32[16,512]{1,0:T(8,128)S(1)}, f32[16,512]{1,0:T(8,128)S(1)}, u32[]{:S(2)}, u32[]{:S(2)}) collective-permute-start(f32[16,512]{1,0:T(8,128)S(1)} %shard_map.106.refs_0_.info), channel_id=1, source_target_pairs={{128,0},{129,1},{130,2},{131,3},{132,4},{133,5},{134,6},{135,7},{1... | collective-permute-start | bytes 98312 | tf_op jit(solution)/shard_map/ppermute | solution.py:241
  19.3 0.4 collective-permute-start.3
  19.7 0.4 collective-permute-start.4
  20.1 0.6 %collective-permute-done.6.info = f32[16,512]{1,0:T(8,128)S(1)} collective-permute-done((f32[16,512]{1,0:T(8,128)S(1)}, f32[16,512]{1,0:T(8,128)S(1)}, u32[]{:S(2)}, u32[]{:S(2)}) %collective-permute-start.6) | collective-permute-done | bytes 32800 | tf_op jit(solution)/shard_map/ppermute | solution.py:241
  20.7 0.2 shard_map.109.mat
  20.8 1.3 %collective-permute-done.3.refs_0_.info = f32[16,512]{1,0:T(8,128)S(1)} collective-permute-done((f32[16,512]{1,0:T(8,128)S(1)}, f32[16,512]{1,0:T(8,128)S(1)}, u32[]{:S(2)}, u32[]{:S(2)}) %collective-permute-start.3) | collective-permute-done | bytes 32800 | tf_op jit(solution)/shard_map/ppermute | solution.py:241
  22.1 1.6 %collective-permute-done.4.refs_1_.info = f32[16,512]{1,0:T(8,128)S(1)} collective-permute-done((f32[16,512]{1,0:T(8,128)S(1)}, f32[16,512]{1,0:T(8,128)S(1)}, u32[]{:S(2)}, u32[]{:S(2)}) %collective-permute-start.4) | collective-permute-done | bytes 32800 | tf_op jit(solution)/shard_map/ppermute | solution.py:241
  23.7 0.0 collective-permute-done.2.other
  23.7 0.8 %shard_map.108 = (bf16[1024,512]{1,0:T(8,128)(2,1)S(1)}, bf16[1024,512]{1,0:T(8,128)(2,1)S(1)}, bf16[128,512]{1,0:T(8,128)(2,1)S(1)}, bf16[128,512]{1,0:T(8,128)(2,1)S(1)}) custom-call(bf16[128,1024]{1,0:T(8,128)(2,1)S(1)} %shard_map.105.mine, bf16[128,1024]{1,0:T(8,128)(2,1)S(1)} %collective-permute-done.2.other, ...), custom_call_target="tpu_custom_call" | custom-call | flops 1048576 | bytes 1048576 | tf_op jit(solution)/shard_map/pallas_call | solution.py:216
  24.5 0.0 copy-start
  24.5 0.1 collective-permute-start.5
  24.6 0.4 shard_map.110
  25.0 1.8 %collective-permute-start.7 = (bf16[128,512]{1,0:T(8,128)(2,1)S(1)}, bf16[128,512]{1,0:T(8,128)(2,1)S(1)}, u32[]{:S(2)}, u32[]{:S(2)}) collective-permute-start(bf16[128,512]{1,0:T(8,128)(2,1)S(1)} %shard_map.110), channel_id=1, source_target_pairs={{128,0},{129,1},{130,2},{131,3},{132,4},{133,5},{134,6},{135,7},{1... | collective-permute-start | bytes 393224 | tf_op jit(solution)/shard_map/ppermute | solution.py:241
  26.8 2.1 %collective-permute-start.8 = (bf16[128,512]{1,0:T(8,128)(2,1)S(1)}, bf16[128,512]{1,0:T(8,128)(2,1)S(1)}, u32[]{:S(2)}, u32[]{:S(2)}) collective-permute-start(bf16[128,512]{1,0:T(8,128)(2,1)S(1)} %get-tuple-element.25), channel_id=1, source_target_pairs={{192,0},{193,1},{194,2},{195,3},{196,4},{197,5},{198,6},{199,7},{2... | collective-permute-start | bytes 393224 | tf_op jit(solution)/shard_map/ppermute | solution.py:241
  29.6 0.0 copy-start.8
  29.6 0.0 copy-done
  29.6 0.6 %copy-done.8 = f32[128]{0:T(128)S(1)} copy-done((f32[128]{0:T(128)S(1)}, f32[128]{0:T(128)}, u32[]{:S(2)}) %copy-start.8) | copy-done | bytes 536
  30.3 0.3 shard_map.111
  30.5 0.5 shard_map.107
  31.0 0.0 collective-permute-done.5.refs_1_
  31.0 1.1 %collective-permute-done.7.refs_2_ = bf16[128,512]{1,0:T(8,128)(2,1)S(1)} collective-permute-done((bf16[128,512]{1,0:T(8,128)(2,1)S(1)}, bf16[128,512]{1,0:T(8,128)(2,1)S(1)}, u32[]{:S(2)}, u32[]{:S(2)}) %collective-permute-start.7) | collective-permute-done | bytes 131104 | tf_op jit(solution)/shard_map/ppermute | solution.py:241
  32.1 2.8 %collective-permute-done.8.refs_3_ = bf16[128,512]{1,0:T(8,128)(2,1)S(1)} collective-permute-done((bf16[128,512]{1,0:T(8,128)(2,1)S(1)}, bf16[128,512]{1,0:T(8,128)(2,1)S(1)}, u32[]{:S(2)}, u32[]{:S(2)}) %collective-permute-start.8) | collective-permute-done | bytes 131104 | tf_op jit(solution)/shard_map/ppermute | solution.py:241
  34.9 0.1 shard_map.112
  35.0 0.1 collective-permute-start.9
  35.1 2.2 %collective-permute-start.10 = (bf16[128,512]{1,0:T(8,128)(2,1)S(1)}, bf16[128,512]{1,0:T(8,128)(2,1)S(1)}, u32[]{:S(2)}, u32[]{:S(2)}) collective-permute-start(bf16[128,512]{1,0:T(8,128)(2,1)S(1)} %get-tuple-element.29.scaled), channel_id=1, source_target_pairs={{128,0},{129,1},{130,2},{131,3},{132,4},{133,5},{134,6},{135,7},{1... | collective-permute-start | bytes 393224 | tf_op jit(solution)/shard_map/ppermute | solution.py:241
  37.3 1.6 %collective-permute-start.11 = (bf16[128,512]{1,0:T(8,128)(2,1)S(1)}, bf16[128,512]{1,0:T(8,128)(2,1)S(1)}, u32[]{:S(2)}, u32[]{:S(2)}) collective-permute-start(bf16[128,512]{1,0:T(8,128)(2,1)S(1)} %get-tuple-element.29.scaled), channel_id=1, source_target_pairs={{192,0},{193,1},{194,2},{195,3},{196,4},{197,5},{198,6},{199,7},{2... | collective-permute-start | bytes 393224 | tf_op jit(solution)/shard_map/ppermute | solution.py:241
  38.9 0.5 shard_map.114.before
  39.4 0.0 collective-permute-done.9.scaled
  39.4 0.5 shard_map.115.before
  39.9 1.9 %collective-permute-done.10.scaled = bf16[128,512]{1,0:T(8,128)(2,1)S(1)} collective-permute-done((bf16[128,512]{1,0:T(8,128)(2,1)S(1)}, bf16[128,512]{1,0:T(8,128)(2,1)S(1)}, u32[]{:S(2)}, u32[]{:S(2)}) %collective-permute-start.10) | collective-permute-done | bytes 131104 | tf_op jit(solution)/shard_map/ppermute | solution.py:241
  41.8 0.5 shard_map.116.before
  42.3 2.4 %collective-permute-done.11.scaled = bf16[128,512]{1,0:T(8,128)(2,1)S(1)} collective-permute-done((bf16[128,512]{1,0:T(8,128)(2,1)S(1)}, bf16[128,512]{1,0:T(8,128)(2,1)S(1)}, u32[]{:S(2)}, u32[]{:S(2)}) %collective-permute-start.11) | collective-permute-done | bytes 131104 | tf_op jit(solution)/shard_map/ppermute | solution.py:241
  44.7 0.5 shard_map.117
  45.2 1.7 %collective-permute-start.12 = (bf16[128,1024]{1,0:T(8,128)(2,1)S(1)}, bf16[128,1024]{1,0:T(8,128)(2,1)S(1)}, u32[]{:S(2)}, u32[]{:S(2)}) collective-permute-start(bf16[128,1024]{1,0:T(8,128)(2,1)S(1)} %get-tuple-element.34), channel_id=1, source_target_pairs={{32,0},{33,1},{34,2},{35,3},{36,4},{37,5},{38,6},{39,7},{40,8},{41... | collective-permute-start | bytes 786440 | tf_op jit(solution)/shard_map/ppermute | solution.py:241
  46.9 1.2 %collective-permute-done.12.got = bf16[128,1024]{1,0:T(8,128)(2,1)S(1)} collective-permute-done((bf16[128,1024]{1,0:T(8,128)(2,1)S(1)}, bf16[128,1024]{1,0:T(8,128)(2,1)S(1)}, u32[]{:S(2)}, u32[]{:S(2)}) %collective-permute-start.12) | collective-permute-done | bytes 262176 | tf_op jit(solution)/shard_map/ppermute | solution.py:241
  48.0 0.1 shard_map.118
  48.1 0.1 collective-permute-start.13
  48.2 5.1 %collective-permute-start.14 = (bf16[128,256]{1,0:T(8,128)(2,1)S(1)}, bf16[128,256]{1,0:T(8,128)(2,1)S(1)}, u32[]{:S(2)}, u32[]{:S(2)}) collective-permute-start(bf16[128,256]{1,0:T(8,128)(2,1)S(1)} %get-tuple-element.37), channel_id=1, source_target_pairs={{31,0},{2,1},{1,2},{4,3},{3,4},{6,5},{5,6},{8,7},{7,8},{10,9},{9,1... | collective-permute-start | bytes 196616 | tf_op jit(solution)/shard_map/ppermute | solution.py:241
  53.3 0.0 copy-start.2
  53.3 0.8 %shard_map.113 = f32[512,128]{1,0:T(8,128)} custom-call(f32[128,512]{1,0:T(8,128)S(1)} %get-tuple-element.28.source), custom_call_target="tpu_custom_call" | custom-call | flops 1048576 | bytes 1048576 | tf_op jit(solution)/shard_map/pallas_call | solution.py:216
  54.2 0.0 collective-permute-done.13.near
  54.2 1.3 %collective-permute-done.14.far = bf16[128,256]{1,0:T(8,128)(2,1)S(1)} collective-permute-done((bf16[128,256]{1,0:T(8,128)(2,1)S(1)}, bf16[128,256]{1,0:T(8,128)(2,1)S(1)}, u32[]{:S(2)}, u32[]{:S(2)}) %collective-permute-start.14) | collective-permute-done | bytes 65568 | tf_op jit(solution)/shard_map/ppermute | solution.py:241
  55.4 0.0 copy-done.2
  55.4 0.9 %shard_map.119 = f32[137,1,512]{2,1,0:T(1,128)} custom-call(f32[128,512]{1,0:T(8,128)S(1)} %get-tuple-element.35.mid, bf16[128,256]{1,0:T(8,128)(2,1)S(1)} %collective-permute-done.13.near, bf16[128,256]{1,0:T(8,128)(2,1)S(1)} %collective-permute-done.14.far, bf16[137,128]{1,0:T(8,128)(2,1)S(1)} %copy-done.2), custom_call_target="tpu_custom_call" | custom-call | flops 1048576 | bytes 1048576 | tf_op jit(solution)/shard_map/pallas_call | solution.py:216
  (2 shorter events, 0.0 us)
Async XLA Ops:
  0.6 0.8 %copy-start.1 = (bf16[137,128]{1,0:T(8,128)(2,1)S(1)}, bf16[137,128]{1,0:T(8,128)(2,1)}, u32[]{:S(2)}) copy-start(bf16[137,128]{1,0:T(8,128)(2,1)} %jac.3) | copy-start | bytes 105220
  1.4 0.9 %copy-start.3 = (bf16[1,512,137]{1,2,0:T(8,128)(2,1)S(1)}, bf16[1,512,137]{1,2,0:T(8,128)(2,1)}, u32[]{:S(2)}) copy-start(bf16[1,512,137]{1,2,0:T(8,128)(2,1)} %param.9) | copy-start | bytes 420868
  2.8 9.2 %collective-permute-start = (bf16[128,256]{1,0:T(8,128)(2,1)S(1)}, bf16[128,256]{1,0:T(8,128)(2,1)S(1)}, u32[]{:S(2)}, u32[]{:S(2)}) collective-permute-start(bf16[128,256]{1,0:T(8,128)(2,1)S(1)} %get-tuple-element.21), channel_id=1, source_target_pairs={{1,0},{0,1},{3,2},{2,3},{5,4},{4,5},{7,6},{6,7},{9,8},{8,9},{11,10... | collective-permute-start | bytes 196616 | tf_op jit(solution)/shard_map/ppermute | solution.py:241
  4.9 8.8 %collective-permute-start.1 = (bf16[128,256]{1,0:T(8,128)(2,1)S(1)}, bf16[128,256]{1,0:T(8,128)(2,1)S(1)}, u32[]{:S(2)}, u32[]{:S(2)}) collective-permute-start(bf16[128,256]{1,0:T(8,128)(2,1)S(1)} %get-tuple-element.22), channel_id=1, source_target_pairs={{31,0},{2,1},{1,2},{4,3},{3,4},{6,5},{5,6},{8,7},{7,8},{10,9},{9,1... | collective-permute-start | bytes 196616 | tf_op jit(solution)/shard_map/ppermute | solution.py:241
  13.6 2.0 %copy-start.4 = (bf16[512,8]{0,1:T(8,128)(2,1)S(1)}, bf16[512,8]{0,1:T(8,128)(2,1)}, u32[]{:S(2)}) copy-start(bf16[512,8]{0,1:T(8,128)(2,1)} %param.11) | copy-start | bytes 24580
  13.6 2.0 %copy-start.7 = (f32[512]{0:T(512)S(1)}, f32[512]{0:T(512)}, u32[]{:S(2)}) copy-start(f32[512]{0:T(512)} %param.13) | copy-start | bytes 6148
  13.7 10.0 %collective-permute-start.2 = (bf16[128,1024]{1,0:T(8,128)(2,1)S(1)}, bf16[128,1024]{1,0:T(8,128)(2,1)S(1)}, u32[]{:S(2)}, u32[]{:S(2)}) collective-permute-start(bf16[128,1024]{1,0:T(8,128)(2,1)S(1)} %shard_map.105.mine), channel_id=1, source_target_pairs={{32,0},{33,1},{34,2},{35,3},{36,4},{37,5},{38,6},{39,7},{40,8},{41... | collective-permute-start | bytes 786440 | tf_op jit(solution)/shard_map/ppermute | solution.py:241
  15.6 0.7 %copy-start.6 = (s32[512]{0:T(512)S(1)}, s32[512]{0:T(512)}, u32[]{:S(2)}) copy-start(s32[512]{0:T(512)} %param.12) | copy-start | bytes 6148
  15.6 0.7 %copy-start.5 = (s32[512]{0:T(512)S(1)}, s32[512]{0:T(512)}, u32[]{:S(2)}) copy-start(s32[512]{0:T(512)} %param.10) | copy-start | bytes 6148
  16.3 4.4 %collective-permute-start.6 = (f32[16,512]{1,0:T(8,128)S(1)}, f32[16,512]{1,0:T(8,128)S(1)}, u32[]{:S(2)}, u32[]{:S(2)}) collective-permute-start(f32[16,512]{1,0:T(8,128)S(1)} %shard_map.106.refs_0_.info), channel_id=1, source_target_pairs={{128,0},{129,1},{130,2},{131,3},{132,4},{133,5},{134,6},{135,7},{1... | collective-permute-start | bytes 98312 | tf_op jit(solution)/shard_map/ppermute | solution.py:241
  19.3 2.8 %collective-permute-start.3 = (f32[16,512]{1,0:T(8,128)S(1)}, f32[16,512]{1,0:T(8,128)S(1)}, u32[]{:S(2)}, u32[]{:S(2)}) collective-permute-start(f32[16,512]{1,0:T(8,128)S(1)} %shard_map.106.refs_0_.info), channel_id=1, source_target_pairs={{64,0},{65,1},{66,2},{67,3},{68,4},{69,5},{70,6},{71,7},{72,8},{73... | collective-permute-start | bytes 98312 | tf_op jit(solution)/shard_map/ppermute | solution.py:241
  19.7 4.0 %collective-permute-start.4 = (f32[16,512]{1,0:T(8,128)S(1)}, f32[16,512]{1,0:T(8,128)S(1)}, u32[]{:S(2)}, u32[]{:S(2)}) collective-permute-start(f32[16,512]{1,0:T(8,128)S(1)} %shard_map.106.refs_0_.info), channel_id=1, source_target_pairs={{192,0},{193,1},{194,2},{195,3},{196,4},{197,5},{198,6},{199,7},{2... | collective-permute-start | bytes 98312 | tf_op jit(solution)/shard_map/ppermute | solution.py:241
  24.5 5.2 %copy-start = (f32[512,128]{1,0:T(8,128)S(1)}, f32[512,128]{1,0:T(8,128)}, u32[]{:S(2)}) copy-start(f32[512,128]{1,0:T(8,128)} %source.1) | copy-start | bytes 786436
  24.5 6.6 %collective-permute-start.5 = (bf16[128,512]{1,0:T(8,128)(2,1)S(1)}, bf16[128,512]{1,0:T(8,128)(2,1)S(1)}, u32[]{:S(2)}, u32[]{:S(2)}) collective-permute-start(bf16[128,512]{1,0:T(8,128)(2,1)S(1)} %get-tuple-element.24), channel_id=1, source_target_pairs={{64,0},{65,1},{66,2},{67,3},{68,4},{69,5},{70,6},{71,7},{72,8},{73... | collective-permute-start | bytes 393224 | tf_op jit(solution)/shard_map/ppermute | solution.py:241
  25.0 7.1 %collective-permute-start.7 = (bf16[128,512]{1,0:T(8,128)(2,1)S(1)}, bf16[128,512]{1,0:T(8,128)(2,1)S(1)}, u32[]{:S(2)}, u32[]{:S(2)}) collective-permute-start(bf16[128,512]{1,0:T(8,128)(2,1)S(1)} %shard_map.110), channel_id=1, source_target_pairs={{128,0},{129,1},{130,2},{131,3},{132,4},{133,5},{134,6},{135,7},{1... | collective-permute-start | bytes 393224 | tf_op jit(solution)/shard_map/ppermute | solution.py:241
  26.8 8.1 %collective-permute-start.8 = (bf16[128,512]{1,0:T(8,128)(2,1)S(1)}, bf16[128,512]{1,0:T(8,128)(2,1)S(1)}, u32[]{:S(2)}, u32[]{:S(2)}) collective-permute-start(bf16[128,512]{1,0:T(8,128)(2,1)S(1)} %get-tuple-element.25), channel_id=1, source_target_pairs={{192,0},{193,1},{194,2},{195,3},{196,4},{197,5},{198,6},{199,7},{2... | collective-permute-start | bytes 393224 | tf_op jit(solution)/shard_map/ppermute | solution.py:241
  29.6 0.7 %copy-start.8 = (f32[128]{0:T(128)S(1)}, f32[128]{0:T(128)}, u32[]{:S(2)}) copy-start(f32[128]{0:T(128)} %param.17) | copy-start | bytes 1540
  35.0 4.4 %collective-permute-start.9 = (bf16[128,512]{1,0:T(8,128)(2,1)S(1)}, bf16[128,512]{1,0:T(8,128)(2,1)S(1)}, u32[]{:S(2)}, u32[]{:S(2)}) collective-permute-start(bf16[128,512]{1,0:T(8,128)(2,1)S(1)} %get-tuple-element.29.scaled), channel_id=1, source_target_pairs={{64,0},{65,1},{66,2},{67,3},{68,4},{69,5},{70,6},{71,7},{72,8},{73... | collective-permute-start | bytes 393224 | tf_op jit(solution)/shard_map/ppermute | solution.py:241
  35.1 6.7 %collective-permute-start.10 = (bf16[128,512]{1,0:T(8,128)(2,1)S(1)}, bf16[128,512]{1,0:T(8,128)(2,1)S(1)}, u32[]{:S(2)}, u32[]{:S(2)}) collective-permute-start(bf16[128,512]{1,0:T(8,128)(2,1)S(1)} %get-tuple-element.29.scaled), channel_id=1, source_target_pairs={{128,0},{129,1},{130,2},{131,3},{132,4},{133,5},{134,6},{135,7},{1... | collective-permute-start | bytes 393224 | tf_op jit(solution)/shard_map/ppermute | solution.py:241
  37.3 7.4 %collective-permute-start.11 = (bf16[128,512]{1,0:T(8,128)(2,1)S(1)}, bf16[128,512]{1,0:T(8,128)(2,1)S(1)}, u32[]{:S(2)}, u32[]{:S(2)}) collective-permute-start(bf16[128,512]{1,0:T(8,128)(2,1)S(1)} %get-tuple-element.29.scaled), channel_id=1, source_target_pairs={{192,0},{193,1},{194,2},{195,3},{196,4},{197,5},{198,6},{199,7},{2... | collective-permute-start | bytes 393224 | tf_op jit(solution)/shard_map/ppermute | solution.py:241
  45.2 2.9 %collective-permute-start.12 = (bf16[128,1024]{1,0:T(8,128)(2,1)S(1)}, bf16[128,1024]{1,0:T(8,128)(2,1)S(1)}, u32[]{:S(2)}, u32[]{:S(2)}) collective-permute-start(bf16[128,1024]{1,0:T(8,128)(2,1)S(1)} %get-tuple-element.34), channel_id=1, source_target_pairs={{32,0},{33,1},{34,2},{35,3},{36,4},{37,5},{38,6},{39,7},{40,8},{41... | collective-permute-start | bytes 786440 | tf_op jit(solution)/shard_map/ppermute | solution.py:241
  48.1 6.1 %collective-permute-start.13 = (bf16[128,256]{1,0:T(8,128)(2,1)S(1)}, bf16[128,256]{1,0:T(8,128)(2,1)S(1)}, u32[]{:S(2)}, u32[]{:S(2)}) collective-permute-start(bf16[128,256]{1,0:T(8,128)(2,1)S(1)} %get-tuple-element.36), channel_id=1, source_target_pairs={{1,0},{0,1},{3,2},{2,3},{5,4},{4,5},{7,6},{6,7},{9,8},{8,9},{11,10... | collective-permute-start | bytes 196616 | tf_op jit(solution)/shard_map/ppermute | solution.py:241
  48.2 7.2 %collective-permute-start.14 = (bf16[128,256]{1,0:T(8,128)(2,1)S(1)}, bf16[128,256]{1,0:T(8,128)(2,1)S(1)}, u32[]{:S(2)}, u32[]{:S(2)}) collective-permute-start(bf16[128,256]{1,0:T(8,128)(2,1)S(1)} %get-tuple-element.37), channel_id=1, source_target_pairs={{31,0},{2,1},{1,2},{4,3},{3,4},{6,5},{5,6},{8,7},{7,8},{10,9},{9,1... | collective-permute-start | bytes 196616 | tf_op jit(solution)/shard_map/ppermute | solution.py:241
  53.3 2.1 %copy-start.2 = (bf16[137,128]{1,0:T(8,128)(2,1)S(1)}, bf16[137,128]{1,0:T(8,128)(2,1)}, u32[]{:S(2)}) copy-start(bf16[137,128]{1,0:T(8,128)(2,1)} %jac.3) | copy-start | bytes 105220

commit v3 on v2

--- a/solution.py
+++ b/solution.py
@@ -11,6 +11,7 @@
 F32 = jnp.float32
 BF16 = jnp.bfloat16
 GROUP = 16
+FIRST_FLOPS = 1 << 34
 
 
 VMEM = pl.BlockSpec(memory_space=pltpu.VMEM)
@@ -39,24 +40,20 @@
         far[...] = right
 
 
-def project_kernel(state, jac, full, near, far, field, levels, sems):
+def first_kernel(out):
+    out[...] = jnp.zeros_like(out)
+
+
+def project_kernel(first, state, jac, full, near, far):
     half = full.shape[1] // 2
-    copies = [
-        pltpu.make_async_copy(state, field, sems.at[0]),
-        pltpu.make_async_copy(jac, levels, sems.at[1]),
-    ]
-    for copy in copies:
-        copy.start()
-    for copy in copies:
-        copy.wait()
     out = lax.dot_general(
-        levels[...], field[...], (((0,), (0,)), ((), ())), preferred_element_type=F32
+        jac[...], state[...], (((0,), (0,)), ((), ())), preferred_element_type=F32
     ).astype(BF16)
     full[...] = out
     put_rims(near, far, out[:, :half], out[:, half:])
 
 
-def info_kernel(cols, tiles, start, weight, slot, frac, info):
+def info_kernel(cols, tiles, first, start, weight, slot, frac, info):
     base = lax.axis_index("space") * cols - cols // 2
     total = cols * tiles
     local = start[...] - base
@@ -253,26 +250,23 @@
         def flat(vector):
             return vector.reshape(1, -1)
 
-        full, near, far = call(
-            project_kernel,
-            [((chan, cols), BF16), ((chan, half), BF16), ((chan, half), BF16)],
-            own.T,
-            jacobian,
-            specs=[HBM, HBM],
-            flops=1 << 20,
-            scratch=[
-                pltpu.VMEM((levels, cols), BF16),
-                pltpu.VMEM((levels, chan), BF16),
-                pltpu.SemaphoreType.DMA((2,)),
-            ],
-        )
+        (first,) = call(first_kernel, [((8, 128), F32)], flops=FIRST_FLOPS)
         (info,) = call(
             functools.partial(info_kernel, cols, n_space),
             [((16, obs), F32)],
+            first,
             flat(obs_start),
             foot_weight.T,
             flat(obs_slot),
             flat(obs_frac),
+            flops=FIRST_FLOPS,
+        )
+        full, near, far = call(
+            project_kernel,
+            [((chan, cols), BF16), ((chan, half), BF16), ((chan, half), BF16)],
+            info,
+            own.T,
+            jacobian,
         )
         near, far = swap(near, tile="near"), swap(far, tile="far")
         infos = [info] + [swap(info, y=j) for j in range(1, lanes)]

time: 56.6 us -> 55.2 us (0.975)
  local copies, waits for them, and re-layouts: 3.02 us -> 2.25 us
    unnamed x18 -> x16, local copies, waits for them, and re-layouts: 3.02 us -> 2.25 us
    pallas_call x16 -> x17, Pallas kernels: 6.38 us -> 6.18 us  [call(): pl.pallas_call(kernel, out_shape=[jax.ShapeDtypeStruct(shape, dtype) for...]
  transfers between devices with their start and end apart: 15 -> 15, of which waited for: 10 -> 10; matrix products, arithmetic and copies ran while one was open for 0% -> 0% of each run, Pallas kernels for 6% -> 7%
where the time goes in v3:
time: 55.2 us; the launch traced here: 55.1 us
  starting transfers between devices  29.8 us (54%)
  waiting for transfers between devices  15.4 us (28%)
  Pallas kernels  6.18 us (11%)
  local copies, waits for them, and re-layouts  2.25 us (4%)
  between operations  1.5 us (3%)
    ppermute x15, starting transfers between devices, swap(): return lax.ppermute(block, ('tm', 'space'), route)  29.8 us
    ppermute x15, waiting for transfers between devices, swap(): return lax.ppermute(block, ('tm', 'space'), route)  15.4 us
    pallas_call x17, Pallas kernels, call(): pl.pallas_call(kernel, out_shape=[jax.ShapeDtypeStruct(shape, dtype) for...  6.18 us
    unnamed x16, local copies, waits for them, and re-layouts  2.25 us
  transfers between devices with their start and end apart: 15, of which 10 were waited for; matrix products, arithmetic and copies ran while one was open for 0% of the time, Pallas kernels for 7%

profile of v3, /device:TPU:1, one launch (start us, length us, event | category | flops | bytes accessed | tf_op | source)
XLA Modules:
  0.0 55.1 jit_solution(5734905760824628783)
XLA Ops:
  0.6 0.0 copy-start.4
  0.6 0.0 copy-start.6
  0.7 0.0 copy-start.7
  0.7 0.0 copy-start.5
  0.7 0.6 %copy-done.4 = bf16[512,8]{0,1:T(8,128)(2,1)S(1)} copy-done((bf16[512,8]{0,1:T(8,128)(2,1)S(1)}, bf16[512,8]{0,1:T(8,128)(2,1)}, u32[]{:S(2)}) %copy-start.4) | copy-done | bytes 8216
  1.3 0.0 copy-done.6
  1.3 0.0 copy-done.7
  1.3 0.0 copy-done.5
  1.4 0.0 copy-start.1
  1.4 0.0 copy-start.2
  1.4 0.7 %copy-done.1 = bf16[137,128]{1,0:T(8,128)(2,1)S(1)} copy-done((bf16[137,128]{1,0:T(8,128)(2,1)S(1)}, bf16[137,128]{1,0:T(8,128)(2,1)}, u32[]{:S(2)}) %copy-start.1) | copy-done | bytes 35096
  2.1 0.2 copy-done.2
  2.3 0.2 shard_map.106
  2.5 2.1 %collective-permute-start = (bf16[128,256]{1,0:T(8,128)(2,1)S(1)}, bf16[128,256]{1,0:T(8,128)(2,1)S(1)}, u32[]{:S(2)}, u32[]{:S(2)}) collective-permute-start(bf16[128,256]{1,0:T(8,128)(2,1)S(1)} %get-tuple-element.21), channel_id=1, source_target_pairs={{1,0},{0,1},{3,2},{2,3},{5,4},{4,5},{7,6},{6,7},{9,8},{8,9},{11,10... | collective-permute-start | bytes 196616 | tf_op jit(solution)/shard_map/ppermute | solution.py:238
  4.6 7.1 %collective-permute-start.1 = (bf16[128,256]{1,0:T(8,128)(2,1)S(1)}, bf16[128,256]{1,0:T(8,128)(2,1)S(1)}, u32[]{:S(2)}, u32[]{:S(2)}) collective-permute-start(bf16[128,256]{1,0:T(8,128)(2,1)S(1)} %get-tuple-element.22), channel_id=1, source_target_pairs={{31,0},{2,1},{1,2},{4,3},{3,4},{6,5},{5,6},{8,7},{7,8},{10,9},{9,1... | collective-permute-start | bytes 196616 | tf_op jit(solution)/shard_map/ppermute | solution.py:238
  11.8 0.0 collective-permute-done.near
  11.8 1.6 %collective-permute-done.1.far = bf16[128,256]{1,0:T(8,128)(2,1)S(1)} collective-permute-done((bf16[128,256]{1,0:T(8,128)(2,1)S(1)}, bf16[128,256]{1,0:T(8,128)(2,1)S(1)}, u32[]{:S(2)}, u32[]{:S(2)}) %collective-permute-start.1) | collective-permute-done | bytes 65568 | tf_op jit(solution)/shard_map/ppermute | solution.py:238
  13.4 1.9 %collective-permute-start.2 = (bf16[128,1024]{1,0:T(8,128)(2,1)S(1)}, bf16[128,1024]{1,0:T(8,128)(2,1)S(1)}, u32[]{:S(2)}, u32[]{:S(2)}) collective-permute-start(bf16[128,1024]{1,0:T(8,128)(2,1)S(1)} %shard_map.107.mine), channel_id=1, source_target_pairs={{32,0},{33,1},{34,2},{35,3},{36,4},{37,5},{38,6},{39,7},{40,8},{41... | collective-permute-start | bytes 786440 | tf_op jit(solution)/shard_map/ppermute | solution.py:238
  15.4 2.9 %collective-permute-start.6 = (f32[16,512]{1,0:T(8,128)S(1)}, f32[16,512]{1,0:T(8,128)S(1)}, u32[]{:S(2)}, u32[]{:S(2)}) collective-permute-start(f32[16,512]{1,0:T(8,128)S(1)} %shard_map.105.first.refs_0_.info), channel_id=1, source_target_pairs={{128,0},{129,1},{130,2},{131,3},{132,4},{133,5},{134,6},{135,7},{1... | collective-permute-start | bytes 98312 | tf_op jit(solution)/shard_map/ppermute | solution.py:238
  18.3 0.4 collective-permute-start.3
  18.7 0.4 collective-permute-start.4
  19.0 0.6 %collective-permute-done.6.info = f32[16,512]{1,0:T(8,128)S(1)} collective-permute-done((f32[16,512]{1,0:T(8,128)S(1)}, f32[16,512]{1,0:T(8,128)S(1)}, u32[]{:S(2)}, u32[]{:S(2)}) %collective-permute-start.6) | collective-permute-done | bytes 32800 | tf_op jit(solution)/shard_map/ppermute | solution.py:238
  19.6 0.2 shard_map.110.mat
  19.8 1.3 %collective-permute-done.3.refs_0_.info = f32[16,512]{1,0:T(8,128)S(1)} collective-permute-done((f32[16,512]{1,0:T(8,128)S(1)}, f32[16,512]{1,0:T(8,128)S(1)}, u32[]{:S(2)}, u32[]{:S(2)}) %collective-permute-start.3) | collective-permute-done | bytes 32800 | tf_op jit(solution)/shard_map/ppermute | solution.py:238
  21.0 1.6 %collective-permute-done.4.refs_1_.info = f32[16,512]{1,0:T(8,128)S(1)} collective-permute-done((f32[16,512]{1,0:T(8,128)S(1)}, f32[16,512]{1,0:T(8,128)S(1)}, u32[]{:S(2)}, u32[]{:S(2)}) %collective-permute-start.4) | collective-permute-done | bytes 32800 | tf_op jit(solution)/shard_map/ppermute | solution.py:238
  22.6 0.0 collective-permute-done.2.other
  22.6 0.8 %shard_map.109 = (bf16[1024,512]{1,0:T(8,128)(2,1)S(1)}, bf16[1024,512]{1,0:T(8,128)(2,1)S(1)}, bf16[128,512]{1,0:T(8,128)(2,1)S(1)}, bf16[128,512]{1,0:T(8,128)(2,1)S(1)}) custom-call(bf16[128,1024]{1,0:T(8,128)(2,1)S(1)} %shard_map.107.mine, bf16[128,1024]{1,0:T(8,128)(2,1)S(1)} %collective-permute-done.2.other, ...), custom_call_target="tpu_custom_call" | custom-call | flops 1048576 | bytes 1048576 | tf_op jit(solution)/shard_map/pallas_call | solution.py:213
  23.4 0.0 copy-start
  23.4 0.1 collective-permute-start.5
  23.5 0.4 shard_map.111
  24.0 1.9 %collective-permute-start.7 = (bf16[128,512]{1,0:T(8,128)(2,1)S(1)}, bf16[128,512]{1,0:T(8,128)(2,1)S(1)}, u32[]{:S(2)}, u32[]{:S(2)}) collective-permute-start(bf16[128,512]{1,0:T(8,128)(2,1)S(1)} %shard_map.111), channel_id=1, source_target_pairs={{128,0},{129,1},{130,2},{131,3},{132,4},{133,5},{134,6},{135,7},{1... | collective-permute-start | bytes 393224 | tf_op jit(solution)/shard_map/ppermute | solution.py:238
  25.8 2.0 %collective-permute-start.8 = (bf16[128,512]{1,0:T(8,128)(2,1)S(1)}, bf16[128,512]{1,0:T(8,128)(2,1)S(1)}, u32[]{:S(2)}, u32[]{:S(2)}) collective-permute-start(bf16[128,512]{1,0:T(8,128)(2,1)S(1)} %get-tuple-element.25), channel_id=1, source_target_pairs={{192,0},{193,1},{194,2},{195,3},{196,4},{197,5},{198,6},{199,7},{2... | collective-permute-start | bytes 393224 | tf_op jit(solution)/shard_map/ppermute | solution.py:238
  28.5 0.0 copy-start.3
  28.6 0.0 copy-done
  28.6 0.6 %copy-done.3 = f32[128]{0:T(128)S(1)} copy-done((f32[128]{0:T(128)S(1)}, f32[128]{0:T(128)}, u32[]{:S(2)}) %copy-start.3) | copy-done | bytes 536
  29.2 0.3 shard_map.112
  29.5 0.5 shard_map.108
  30.0 0.0 collective-permute-done.5.refs_1_
  30.0 0.8 %collective-permute-done.7.refs_2_ = bf16[128,512]{1,0:T(8,128)(2,1)S(1)} collective-permute-done((bf16[128,512]{1,0:T(8,128)(2,1)S(1)}, bf16[128,512]{1,0:T(8,128)(2,1)S(1)}, u32[]{:S(2)}, u32[]{:S(2)}) %collective-permute-start.7) | collective-permute-done | bytes 131104 | tf_op jit(solution)/shard_map/ppermute | solution.py:238
  30.7 3.1 %collective-permute-done.8.refs_3_ = bf16[128,512]{1,0:T(8,128)(2,1)S(1)} collective-permute-done((bf16[128,512]{1,0:T(8,128)(2,1)S(1)}, bf16[128,512]{1,0:T(8,128)(2,1)S(1)}, u32[]{:S(2)}, u32[]{:S(2)}) %collective-permute-start.8) | collective-permute-done | bytes 131104 | tf_op jit(solution)/shard_map/ppermute | solution.py:238
  33.8 0.1 shard_map.113
  33.9 0.1 collective-permute-start.9
  34.0 2.1 %collective-permute-start.10 = (bf16[128,512]{1,0:T(8,128)(2,1)S(1)}, bf16[128,512]{1,0:T(8,128)(2,1)S(1)}, u32[]{:S(2)}, u32[]{:S(2)}) collective-permute-start(bf16[128,512]{1,0:T(8,128)(2,1)S(1)} %get-tuple-element.29.scaled), channel_id=1, source_target_pairs={{128,0},{129,1},{130,2},{131,3},{132,4},{133,5},{134,6},{135,7},{1... | collective-permute-start | bytes 393224 | tf_op jit(solution)/shard_map/ppermute | solution.py:238
  36.1 1.8 %collective-permute-start.11 = (bf16[128,512]{1,0:T(8,128)(2,1)S(1)}, bf16[128,512]{1,0:T(8,128)(2,1)S(1)}, u32[]{:S(2)}, u32[]{:S(2)}) collective-permute-start(bf16[128,512]{1,0:T(8,128)(2,1)S(1)} %get-tuple-element.29.scaled), channel_id=1, source_target_pairs={{192,0},{193,1},{194,2},{195,3},{196,4},{197,5},{198,6},{199,7},{2... | collective-permute-start | bytes 393224 | tf_op jit(solution)/shard_map/ppermute | solution.py:238
  37.9 0.5 shard_map.115.before
  38.4 0.0 collective-permute-done.9.scaled
  38.4 0.5 shard_map.116.before
  38.9 1.6 %collective-permute-done.10.scaled = bf16[128,512]{1,0:T(8,128)(2,1)S(1)} collective-permute-done((bf16[128,512]{1,0:T(8,128)(2,1)S(1)}, bf16[128,512]{1,0:T(8,128)(2,1)S(1)}, u32[]{:S(2)}, u32[]{:S(2)}) %collective-permute-start.10) | collective-permute-done | bytes 131104 | tf_op jit(solution)/shard_map/ppermute | solution.py:238
  40.5 0.5 shard_map.117.before
  40.9 2.4 %collective-permute-done.11.scaled = bf16[128,512]{1,0:T(8,128)(2,1)S(1)} collective-permute-done((bf16[128,512]{1,0:T(8,128)(2,1)S(1)}, bf16[128,512]{1,0:T(8,128)(2,1)S(1)}, u32[]{:S(2)}, u32[]{:S(2)}) %collective-permute-start.11) | collective-permute-done | bytes 131104 | tf_op jit(solution)/shard_map/ppermute | solution.py:238
  43.3 0.5 shard_map.118
  43.8 1.7 %collective-permute-start.12 = (bf16[128,1024]{1,0:T(8,128)(2,1)S(1)}, bf16[128,1024]{1,0:T(8,128)(2,1)S(1)}, u32[]{:S(2)}, u32[]{:S(2)}) collective-permute-start(bf16[128,1024]{1,0:T(8,128)(2,1)S(1)} %get-tuple-element.34), channel_id=1, source_target_pairs={{32,0},{33,1},{34,2},{35,3},{36,4},{37,5},{38,6},{39,7},{40,8},{41... | collective-permute-start | bytes 786440 | tf_op jit(solution)/shard_map/ppermute | solution.py:238
  45.6 1.2 %collective-permute-done.12.got = bf16[128,1024]{1,0:T(8,128)(2,1)S(1)} collective-permute-done((bf16[128,1024]{1,0:T(8,128)(2,1)S(1)}, bf16[128,1024]{1,0:T(8,128)(2,1)S(1)}, u32[]{:S(2)}, u32[]{:S(2)}) %collective-permute-start.12) | collective-permute-done | bytes 262176 | tf_op jit(solution)/shard_map/ppermute | solution.py:238
  46.7 0.1 shard_map.119
  46.8 0.1 collective-permute-start.13
  46.9 5.2 %collective-permute-start.14 = (bf16[128,256]{1,0:T(8,128)(2,1)S(1)}, bf16[128,256]{1,0:T(8,128)(2,1)S(1)}, u32[]{:S(2)}, u32[]{:S(2)}) collective-permute-start(bf16[128,256]{1,0:T(8,128)(2,1)S(1)} %get-tuple-element.37), channel_id=1, source_target_pairs={{31,0},{2,1},{1,2},{4,3},{3,4},{6,5},{5,6},{8,7},{7,8},{10,9},{9,1... | collective-permute-start | bytes 196616 | tf_op jit(solution)/shard_map/ppermute | solution.py:238
  52.1 0.8 %shard_map.114 = f32[512,128]{1,0:T(8,128)} custom-call(f32[128,512]{1,0:T(8,128)S(1)} %get-tuple-element.28.source), custom_call_target="tpu_custom_call" | custom-call | flops 1048576 | bytes 1048576 | tf_op jit(solution)/shard_map/pallas_call | solution.py:213
  52.9 0.0 collective-permute-done.13.near
  52.9 1.3 %collective-permute-done.14.far = bf16[128,256]{1,0:T(8,128)(2,1)S(1)} collective-permute-done((bf16[128,256]{1,0:T(8,128)(2,1)S(1)}, bf16[128,256]{1,0:T(8,128)(2,1)S(1)}, u32[]{:S(2)}, u32[]{:S(2)}) %collective-permute-start.14) | collective-permute-done | bytes 65568 | tf_op jit(solution)/shard_map/ppermute | solution.py:238
  54.2 0.9 %shard_map.120 = f32[137,1,512]{2,1,0:T(1,128)} custom-call(f32[128,512]{1,0:T(8,128)S(1)} %get-tuple-element.35.mid, bf16[128,256]{1,0:T(8,128)(2,1)S(1)} %collective-permute-done.13.near, bf16[128,256]{1,0:T(8,128)(2,1)S(1)} %collective-permute-done.14.far, bf16[137,128]{1,0:T(8,128)(2,1)S(1)} %copy-done.1), custom_call_target="tpu_custom_call" | custom-call | flops 1048576 | bytes 1048576 | tf_op jit(solution)/shard_map/pallas_call | solution.py:213
  (3 shorter events, 0.0 us)
Async XLA Ops:
  0.6 0.7 %copy-start.4 = (bf16[512,8]{0,1:T(8,128)(2,1)S(1)}, bf16[512,8]{0,1:T(8,128)(2,1)}, u32[]{:S(2)}) copy-start(bf16[512,8]{0,1:T(8,128)(2,1)} %param.11) | copy-start | bytes 24580
  0.6 0.7 %copy-start.6 = (s32[512]{0:T(512)S(1)}, s32[512]{0:T(512)}, u32[]{:S(2)}) copy-start(s32[512]{0:T(512)} %param.12) | copy-start | bytes 6148
  0.7 0.7 %copy-start.7 = (f32[512]{0:T(512)S(1)}, f32[512]{0:T(512)}, u32[]{:S(2)}) copy-start(f32[512]{0:T(512)} %param.13) | copy-start | bytes 6148
  0.7 0.7 %copy-start.5 = (s32[512]{0:T(512)S(1)}, s32[512]{0:T(512)}, u32[]{:S(2)}) copy-start(s32[512]{0:T(512)} %param.10) | copy-start | bytes 6148
  1.4 0.8 %copy-start.1 = (bf16[137,128]{1,0:T(8,128)(2,1)S(1)}, bf16[137,128]{1,0:T(8,128)(2,1)}, u32[]{:S(2)}) copy-start(bf16[137,128]{1,0:T(8,128)(2,1)} %jac.3) | copy-start | bytes 105220
  1.4 0.9 %copy-start.2 = (bf16[1,512,137]{1,2,0:T(8,128)(2,1)S(1)}, bf16[1,512,137]{1,2,0:T(8,128)(2,1)}, u32[]{:S(2)}) copy-start(bf16[1,512,137]{1,2,0:T(8,128)(2,1)} %param.9) | copy-start | bytes 420868
  2.5 9.2 %collective-permute-start = (bf16[128,256]{1,0:T(8,128)(2,1)S(1)}, bf16[128,256]{1,0:T(8,128)(2,1)S(1)}, u32[]{:S(2)}, u32[]{:S(2)}) collective-permute-start(bf16[128,256]{1,0:T(8,128)(2,1)S(1)} %get-tuple-element.21), channel_id=1, source_target_pairs={{1,0},{0,1},{3,2},{2,3},{5,4},{4,5},{7,6},{6,7},{9,8},{8,9},{11,10... | collective-permute-start | bytes 196616 | tf_op jit(solution)/shard_map/ppermute | solution.py:238
  4.6 8.8 %collective-permute-start.1 = (bf16[128,256]{1,0:T(8,128)(2,1)S(1)}, bf16[128,256]{1,0:T(8,128)(2,1)S(1)}, u32[]{:S(2)}, u32[]{:S(2)}) collective-permute-start(bf16[128,256]{1,0:T(8,128)(2,1)S(1)} %get-tuple-element.22), channel_id=1, source_target_pairs={{31,0},{2,1},{1,2},{4,3},{3,4},{6,5},{5,6},{8,7},{7,8},{10,9},{9,1... | collective-permute-start | bytes 196616 | tf_op jit(solution)/shard_map/ppermute | solution.py:238
  13.4 9.2 %collective-permute-start.2 = (bf16[128,1024]{1,0:T(8,128)(2,1)S(1)}, bf16[128,1024]{1,0:T(8,128)(2,1)S(1)}, u32[]{:S(2)}, u32[]{:S(2)}) collective-permute-start(bf16[128,1024]{1,0:T(8,128)(2,1)S(1)} %shard_map.107.mine), channel_id=1, source_target_pairs={{32,0},{33,1},{34,2},{35,3},{36,4},{37,5},{38,6},{39,7},{40,8},{41... | collective-permute-start | bytes 786440 | tf_op jit(solution)/shard_map/ppermute | solution.py:238
  15.4 4.3 %collective-permute-start.6 = (f32[16,512]{1,0:T(8,128)S(1)}, f32[16,512]{1,0:T(8,128)S(1)}, u32[]{:S(2)}, u32[]{:S(2)}) collective-permute-start(f32[16,512]{1,0:T(8,128)S(1)} %shard_map.105.first.refs_0_.info), channel_id=1, source_target_pairs={{128,0},{129,1},{130,2},{131,3},{132,4},{133,5},{134,6},{135,7},{1... | collective-permute-start | bytes 98312 | tf_op jit(solution)/shard_map/ppermute | solution.py:238
  18.3 2.8 %collective-permute-start.3 = (f32[16,512]{1,0:T(8,128)S(1)}, f32[16,512]{1,0:T(8,128)S(1)}, u32[]{:S(2)}, u32[]{:S(2)}) collective-permute-start(f32[16,512]{1,0:T(8,128)S(1)} %shard_map.105.first.refs_0_.info), channel_id=1, source_target_pairs={{64,0},{65,1},{66,2},{67,3},{68,4},{69,5},{70,6},{71,7},{72,8},{73... | collective-permute-start | bytes 98312 | tf_op jit(solution)/shard_map/ppermute | solution.py:238
  18.7 4.0 %collective-permute-start.4 = (f32[16,512]{1,0:T(8,128)S(1)}, f32[16,512]{1,0:T(8,128)S(1)}, u32[]{:S(2)}, u32[]{:S(2)}) collective-permute-start(f32[16,512]{1,0:T(8,128)S(1)} %shard_map.105.first.refs_0_.info), channel_id=1, source_target_pairs={{192,0},{193,1},{194,2},{195,3},{196,4},{197,5},{198,6},{199,7},{2... | collective-permute-start | bytes 98312 | tf_op jit(solution)/shard_map/ppermute | solution.py:238
  23.4 5.2 %copy-start = (f32[512,128]{1,0:T(8,128)S(1)}, f32[512,128]{1,0:T(8,128)}, u32[]{:S(2)}) copy-start(f32[512,128]{1,0:T(8,128)} %source.1) | copy-start | bytes 786436
  23.4 6.6 %collective-permute-start.5 = (bf16[128,512]{1,0:T(8,128)(2,1)S(1)}, bf16[128,512]{1,0:T(8,128)(2,1)S(1)}, u32[]{:S(2)}, u32[]{:S(2)}) collective-permute-start(bf16[128,512]{1,0:T(8,128)(2,1)S(1)} %get-tuple-element.24), channel_id=1, source_target_pairs={{64,0},{65,1},{66,2},{67,3},{68,4},{69,5},{70,6},{71,7},{72,8},{73... | collective-permute-start | bytes 393224 | tf_op jit(solution)/shard_map/ppermute | solution.py:238
  24.0 6.8 %collective-permute-start.7 = (bf16[128,512]{1,0:T(8,128)(2,1)S(1)}, bf16[128,512]{1,0:T(8,128)(2,1)S(1)}, u32[]{:S(2)}, u32[]{:S(2)}) collective-permute-start(bf16[128,512]{1,0:T(8,128)(2,1)S(1)} %shard_map.111), channel_id=1, source_target_pairs={{128,0},{129,1},{130,2},{131,3},{132,4},{133,5},{134,6},{135,7},{1... | collective-permute-start | bytes 393224 | tf_op jit(solution)/shard_map/ppermute | solution.py:238
  25.8 8.0 %collective-permute-start.8 = (bf16[128,512]{1,0:T(8,128)(2,1)S(1)}, bf16[128,512]{1,0:T(8,128)(2,1)S(1)}, u32[]{:S(2)}, u32[]{:S(2)}) collective-permute-start(bf16[128,512]{1,0:T(8,128)(2,1)S(1)} %get-tuple-element.25), channel_id=1, source_target_pairs={{192,0},{193,1},{194,2},{195,3},{196,4},{197,5},{198,6},{199,7},{2... | collective-permute-start | bytes 393224 | tf_op jit(solution)/shard_map/ppermute | solution.py:238
  28.5 0.7 %copy-start.3 = (f32[128]{0:T(128)S(1)}, f32[128]{0:T(128)}, u32[]{:S(2)}) copy-start(f32[128]{0:T(128)} %param.17) | copy-start | bytes 1540
  33.9 4.4 %collective-permute-start.9 = (bf16[128,512]{1,0:T(8,128)(2,1)S(1)}, bf16[128,512]{1,0:T(8,128)(2,1)S(1)}, u32[]{:S(2)}, u32[]{:S(2)}) collective-permute-start(bf16[128,512]{1,0:T(8,128)(2,1)S(1)} %get-tuple-element.29.scaled), channel_id=1, source_target_pairs={{64,0},{65,1},{66,2},{67,3},{68,4},{69,5},{70,6},{71,7},{72,8},{73... | collective-permute-start | bytes 393224 | tf_op jit(solution)/shard_map/ppermute | solution.py:238
  34.0 6.4 %collective-permute-start.10 = (bf16[128,512]{1,0:T(8,128)(2,1)S(1)}, bf16[128,512]{1,0:T(8,128)(2,1)S(1)}, u32[]{:S(2)}, u32[]{:S(2)}) collective-permute-start(bf16[128,512]{1,0:T(8,128)(2,1)S(1)} %get-tuple-element.29.scaled), channel_id=1, source_target_pairs={{128,0},{129,1},{130,2},{131,3},{132,4},{133,5},{134,6},{135,7},{1... | collective-permute-start | bytes 393224 | tf_op jit(solution)/shard_map/ppermute | solution.py:238
  36.1 7.2 %collective-permute-start.11 = (bf16[128,512]{1,0:T(8,128)(2,1)S(1)}, bf16[128,512]{1,0:T(8,128)(2,1)S(1)}, u32[]{:S(2)}, u32[]{:S(2)}) collective-permute-start(bf16[128,512]{1,0:T(8,128)(2,1)S(1)} %get-tuple-element.29.scaled), channel_id=1, source_target_pairs={{192,0},{193,1},{194,2},{195,3},{196,4},{197,5},{198,6},{199,7},{2... | collective-permute-start | bytes 393224 | tf_op jit(solution)/shard_map/ppermute | solution.py:238
  43.8 2.9 %collective-permute-start.12 = (bf16[128,1024]{1,0:T(8,128)(2,1)S(1)}, bf16[128,1024]{1,0:T(8,128)(2,1)S(1)}, u32[]{:S(2)}, u32[]{:S(2)}) collective-permute-start(bf16[128,1024]{1,0:T(8,128)(2,1)S(1)} %get-tuple-element.34), channel_id=1, source_target_pairs={{32,0},{33,1},{34,2},{35,3},{36,4},{37,5},{38,6},{39,7},{40,8},{41... | collective-permute-start | bytes 786440 | tf_op jit(solution)/shard_map/ppermute | solution.py:238
  46.8 6.1 %collective-permute-start.13 = (bf16[128,256]{1,0:T(8,128)(2,1)S(1)}, bf16[128,256]{1,0:T(8,128)(2,1)S(1)}, u32[]{:S(2)}, u32[]{:S(2)}) collective-permute-start(bf16[128,256]{1,0:T(8,128)(2,1)S(1)} %get-tuple-element.36), channel_id=1, source_target_pairs={{1,0},{0,1},{3,2},{2,3},{5,4},{4,5},{7,6},{6,7},{9,8},{8,9},{11,10... | collective-permute-start | bytes 196616 | tf_op jit(solution)/shard_map/ppermute | solution.py:238
  46.9 7.3 %collective-permute-start.14 = (bf16[128,256]{1,0:T(8,128)(2,1)S(1)}, bf16[128,256]{1,0:T(8,128)(2,1)S(1)}, u32[]{:S(2)}, u32[]{:S(2)}) collective-permute-start(bf16[128,256]{1,0:T(8,128)(2,1)S(1)} %get-tuple-element.37), channel_id=1, source_target_pairs={{31,0},{2,1},{1,2},{4,3},{3,4},{6,5},{5,6},{8,7},{7,8},{10,9},{9,1... | collective-permute-start | bytes 196616 | tf_op jit(solution)/shard_map/ppermute | solution.py:238

commit v4 on v3

--- a/solution.py
+++ b/solution.py
@@ -11,6 +11,7 @@
 F32 = jnp.float32
 BF16 = jnp.bfloat16
 GROUP = 16
+SWAP_ORDER = (2, 3, 1)
 FIRST_FLOPS = 1 << 34
 
 
@@ -53,7 +54,7 @@
     put_rims(near, far, out[:, :half], out[:, half:])
 
 
-def info_kernel(cols, tiles, first, start, weight, slot, frac, info):
+def info_kernel(cols, tiles, start, weight, slot, frac, info):
     base = lax.axis_index("space") * cols - cols // 2
     total = cols * tiles
     local = start[...] - base
@@ -251,22 +252,20 @@
             return vector.reshape(1, -1)
 
         (first,) = call(first_kernel, [((8, 128), F32)], flops=FIRST_FLOPS)
+        full, near, far = call(
+            project_kernel,
+            [((chan, cols), BF16), ((chan, half), BF16), ((chan, half), BF16)],
+            first,
+            own.T,
+            jacobian,
+        )
         (info,) = call(
             functools.partial(info_kernel, cols, n_space),
             [((16, obs), F32)],
-            first,
             flat(obs_start),
             foot_weight.T,
             flat(obs_slot),
             flat(obs_frac),
-            flops=FIRST_FLOPS,
-        )
-        full, near, far = call(
-            project_kernel,
-            [((chan, cols), BF16), ((chan, half), BF16), ((chan, half), BF16)],
-            info,
-            own.T,
-            jacobian,
         )
         near, far = swap(near, tile="near"), swap(far, tile="far")
         infos = [info] + [swap(info, y=j) for j in range(1, lanes)]
@@ -290,7 +289,7 @@
         (far,) = call(gather_kernel, [((chan, obs), BF16)], wide, other, infos[2], mats[2])
         parts = [None] * lanes
         parts[2] = swap(far, y=2)
-        for j, part in zip((1, 3), gather([1, 3])):
+        for j, part in zip((3, 1), gather([3, 1])):
             parts[j] = swap(part, y=j)
         (parts[0],) = gather([0])
         values, scale = call(
@@ -313,7 +312,8 @@
         all_scaled = [scaled] + [swap(scaled, y=j) for j in range(1, lanes)]
         (acc,) = call(spread_first_kernel, [((2 * chan, width), F32)], info, scaled, mats[0])
         (departures,) = call(turn_kernel, [((obs, chan), F32)], gaps)
-        for j in range(1, lanes - 1):
+        *early, last = SWAP_ORDER
+        for j in early:
             (acc,) = call(
                 spread_next_kernel,
                 [((2 * chan, width), F32)],
@@ -326,9 +326,9 @@
             spread_last_kernel,
             [((chan, width), F32), ((chan, width), BF16)],
             acc,
-            infos[lanes - 1],
-            all_scaled[lanes - 1],
-            mats[lanes - 1],
+            infos[last],
+            all_scaled[last],
+            mats[last],
         )
         mid, near, far = call(
             join_kernel,

time: 55.2 us -> 55.1 us (level)
  starting transfers between devices: 29.8 us -> 27.9 us
  waiting for transfers between devices: 15.4 us -> 17.2 us
    ppermute x15, starting transfers between devices: 29.8 us -> 27.9 us  [swap(): return lax.ppermute(block, ('tm', 'space'), route)]
    ppermute x15, waiting for transfers between devices: 15.4 us -> 17.2 us  [swap(): return lax.ppermute(block, ('tm', 'space'), route)]
  transfers between devices with their start and end apart: 15 -> 15, of which waited for: 10 -> 9; matrix products, arithmetic and copies ran while one was open for 0% -> 0% of each run, Pallas kernels for 7% -> 7%
where the time goes in v4:
time: 55.1 us; the launch traced here: 55 us
  starting transfers between devices  27.9 us (51%)
  waiting for transfers between devices  17.2 us (31%)
  Pallas kernels  6.18 us (11%)
  local copies, waits for them, and re-layouts  2.23 us (4%)
  between operations  1.48 us (3%)
    ppermute x15, starting transfers between devices, swap(): return lax.ppermute(block, ('tm', 'space'), route)  27.9 us
    ppermute x15, waiting for transfers between devices, swap(): return lax.ppermute(block, ('tm', 'space'), route)  17.2 us
    pallas_call x17, Pallas kernels, call(): pl.pallas_call(kernel, out_shape=[jax.ShapeDtypeStruct(shape, dtype) for...  6.18 us
    unnamed x16, local copies, waits for them, and re-layouts  2.23 us
  transfers between devices with their start and end apart: 15, of which 9 were waited for; matrix products, arithmetic and copies ran while one was open for 0% of the time, Pallas kernels for 7%

profile of v4, /device:TPU:1, one launch (start us, length us, event | category | flops | bytes accessed | tf_op | source)
XLA Modules:
  0.0 55.0 jit_solution(4747687559611223085)
XLA Ops:
  0.6 0.0 copy-start.2
  0.6 0.0 copy-start.1
  0.7 0.9 %copy-done.2 = bf16[1,512,137]{1,2,0:T(8,128)(2,1)S(1)} copy-done((bf16[1,512,137]{1,2,0:T(8,128)(2,1)S(1)}, bf16[1,512,137]{1,2,0:T(8,128)(2,1)}, u32[]{:S(2)}) %copy-start.2) | copy-done | bytes 140312
  1.5 0.0 copy-done.1
  1.5 0.0 copy-start.6
  1.5 0.2 shard_map.105
  1.8 2.1 %collective-permute-start = (bf16[128,256]{1,0:T(8,128)(2,1)S(1)}, bf16[128,256]{1,0:T(8,128)(2,1)S(1)}, u32[]{:S(2)}, u32[]{:S(2)}) collective-permute-start(bf16[128,256]{1,0:T(8,128)(2,1)S(1)} %get-tuple-element.21), channel_id=1, source_target_pairs={{1,0},{0,1},{3,2},{2,3},{5,4},{4,5},{7,6},{6,7},{9,8},{8,9},{11,10... | collective-permute-start | bytes 196616 | tf_op jit(solution)/shard_map/ppermute | solution.py:239
  3.9 7.1 %collective-permute-start.1 = (bf16[128,256]{1,0:T(8,128)(2,1)S(1)}, bf16[128,256]{1,0:T(8,128)(2,1)S(1)}, u32[]{:S(2)}, u32[]{:S(2)}) collective-permute-start(bf16[128,256]{1,0:T(8,128)(2,1)S(1)} %get-tuple-element.22), channel_id=1, source_target_pairs={{31,0},{2,1},{1,2},{4,3},{3,4},{6,5},{5,6},{8,7},{7,8},{10,9},{9,1... | collective-permute-start | bytes 196616 | tf_op jit(solution)/shard_map/ppermute | solution.py:239
  11.0 0.0 collective-permute-done.near
  11.0 1.6 %collective-permute-done.1.far = bf16[128,256]{1,0:T(8,128)(2,1)S(1)} collective-permute-done((bf16[128,256]{1,0:T(8,128)(2,1)S(1)}, bf16[128,256]{1,0:T(8,128)(2,1)S(1)}, u32[]{:S(2)}, u32[]{:S(2)}) %collective-permute-start.1) | collective-permute-done | bytes 65568 | tf_op jit(solution)/shard_map/ppermute | solution.py:239
  12.7 0.0 copy-start.3
  12.7 1.9 %collective-permute-start.2 = (bf16[128,1024]{1,0:T(8,128)(2,1)S(1)}, bf16[128,1024]{1,0:T(8,128)(2,1)S(1)}, u32[]{:S(2)}, u32[]{:S(2)}) collective-permute-start(bf16[128,1024]{1,0:T(8,128)(2,1)S(1)} %shard_map.106.mine), channel_id=1, source_target_pairs={{32,0},{33,1},{34,2},{35,3},{36,4},{37,5},{38,6},{39,7},{40,8},{41... | collective-permute-start | bytes 786440 | tf_op jit(solution)/shard_map/ppermute | solution.py:239
  14.6 0.0 copy-start.5
  14.6 0.0 copy-start.4
  14.6 0.0 copy-done.6
  14.6 0.0 copy-done.3
  14.6 0.7 %copy-done.5 = s32[512]{0:T(512)S(1)} copy-done((s32[512]{0:T(512)S(1)}, s32[512]{0:T(512)}, u32[]{:S(2)}) %copy-start.5) | copy-done | bytes 2072
  15.3 0.0 copy-done.4
  15.3 3.0 %collective-permute-start.6 = (f32[16,512]{1,0:T(8,128)S(1)}, f32[16,512]{1,0:T(8,128)S(1)}, u32[]{:S(2)}, u32[]{:S(2)}) collective-permute-start(f32[16,512]{1,0:T(8,128)S(1)} %shard_map.107.refs_0_.info), channel_id=1, source_target_pairs={{128,0},{129,1},{130,2},{131,3},{132,4},{133,5},{134,6},{135,7},{1... | collective-permute-start | bytes 98312 | tf_op jit(solution)/shard_map/ppermute | solution.py:239
  18.3 0.8 %collective-permute-start.3 = (f32[16,512]{1,0:T(8,128)S(1)}, f32[16,512]{1,0:T(8,128)S(1)}, u32[]{:S(2)}, u32[]{:S(2)}) collective-permute-start(f32[16,512]{1,0:T(8,128)S(1)} %shard_map.107.refs_0_.info), channel_id=1, source_target_pairs={{192,0},{193,1},{194,2},{195,3},{196,4},{197,5},{198,6},{199,7},{2... | collective-permute-start | bytes 98312 | tf_op jit(solution)/shard_map/ppermute | solution.py:239
  19.1 0.0 collective-permute-start.4
  19.1 0.6 %collective-permute-done.6.info = f32[16,512]{1,0:T(8,128)S(1)} collective-permute-done((f32[16,512]{1,0:T(8,128)S(1)}, f32[16,512]{1,0:T(8,128)S(1)}, u32[]{:S(2)}, u32[]{:S(2)}) %collective-permute-start.6) | collective-permute-done | bytes 32800 | tf_op jit(solution)/shard_map/ppermute | solution.py:239
  19.7 0.2 shard_map.110.mat
  19.8 2.5 %collective-permute-done.3.refs_0_.info = f32[16,512]{1,0:T(8,128)S(1)} collective-permute-done((f32[16,512]{1,0:T(8,128)S(1)}, f32[16,512]{1,0:T(8,128)S(1)}, u32[]{:S(2)}, u32[]{:S(2)}) %collective-permute-start.3) | collective-permute-done | bytes 32800 | tf_op jit(solution)/shard_map/ppermute | solution.py:239
  22.3 0.0 collective-permute-done.4.refs_1_.info
  22.3 0.0 collective-permute-done.2.other
  22.3 0.8 %shard_map.109 = (bf16[1024,512]{1,0:T(8,128)(2,1)S(1)}, bf16[1024,512]{1,0:T(8,128)(2,1)S(1)}, bf16[128,512]{1,0:T(8,128)(2,1)S(1)}, bf16[128,512]{1,0:T(8,128)(2,1)S(1)}) custom-call(bf16[128,1024]{1,0:T(8,128)(2,1)S(1)} %shard_map.106.mine, bf16[128,1024]{1,0:T(8,128)(2,1)S(1)} %collective-permute-done.2.other, ...), custom_call_target="tpu_custom_call" | custom-call | flops 1048576 | bytes 1048576 | tf_op jit(solution)/shard_map/pallas_call | solution.py:214
  23.1 0.0 copy-start
  23.1 0.1 collective-permute-start.5
  23.2 0.4 shard_map.111
  23.6 3.0 %collective-permute-start.7 = (bf16[128,512]{1,0:T(8,128)(2,1)S(1)}, bf16[128,512]{1,0:T(8,128)(2,1)S(1)}, u32[]{:S(2)}, u32[]{:S(2)}) collective-permute-start(bf16[128,512]{1,0:T(8,128)(2,1)S(1)} %shard_map.111), channel_id=1, source_target_pairs={{128,0},{129,1},{130,2},{131,3},{132,4},{133,5},{134,6},{135,7},{1... | collective-permute-start | bytes 393224 | tf_op jit(solution)/shard_map/ppermute | solution.py:239
  26.6 0.9 %collective-permute-start.8 = (bf16[128,512]{1,0:T(8,128)(2,1)S(1)}, bf16[128,512]{1,0:T(8,128)(2,1)S(1)}, u32[]{:S(2)}, u32[]{:S(2)}) collective-permute-start(bf16[128,512]{1,0:T(8,128)(2,1)S(1)} %get-tuple-element.25), channel_id=1, source_target_pairs={{192,0},{193,1},{194,2},{195,3},{196,4},{197,5},{198,6},{199,7},{2... | collective-permute-start | bytes 393224 | tf_op jit(solution)/shard_map/ppermute | solution.py:239
  28.2 0.0 copy-start.7
  28.2 0.0 copy-done
  28.2 0.6 %copy-done.7 = f32[128]{0:T(128)S(1)} copy-done((f32[128]{0:T(128)S(1)}, f32[128]{0:T(128)}, u32[]{:S(2)}) %copy-start.7) | copy-done | bytes 536
  28.9 0.3 shard_map.112
  29.1 0.5 shard_map.108
  29.6 0.0 collective-permute-done.5.refs_1_
  29.6 1.1 %collective-permute-done.7.refs_2_ = bf16[128,512]{1,0:T(8,128)(2,1)S(1)} collective-permute-done((bf16[128,512]{1,0:T(8,128)(2,1)S(1)}, bf16[128,512]{1,0:T(8,128)(2,1)S(1)}, u32[]{:S(2)}, u32[]{:S(2)}) %collective-permute-start.7) | collective-permute-done | bytes 131104 | tf_op jit(solution)/shard_map/ppermute | solution.py:239
  30.8 3.4 %collective-permute-done.8.refs_3_ = bf16[128,512]{1,0:T(8,128)(2,1)S(1)} collective-permute-done((bf16[128,512]{1,0:T(8,128)(2,1)S(1)}, bf16[128,512]{1,0:T(8,128)(2,1)S(1)}, u32[]{:S(2)}, u32[]{:S(2)}) %collective-permute-start.8) | collective-permute-done | bytes 131104 | tf_op jit(solution)/shard_map/ppermute | solution.py:239
  34.2 0.1 shard_map.113
  34.3 0.1 collective-permute-start.9
  34.4 1.4 %collective-permute-start.10 = (bf16[128,512]{1,0:T(8,128)(2,1)S(1)}, bf16[128,512]{1,0:T(8,128)(2,1)S(1)}, u32[]{:S(2)}, u32[]{:S(2)}) collective-permute-start(bf16[128,512]{1,0:T(8,128)(2,1)S(1)} %get-tuple-element.29.scaled), channel_id=1, source_target_pairs={{192,0},{193,1},{194,2},{195,3},{196,4},{197,5},{198,6},{199,7},{2... | collective-permute-start | bytes 393224 | tf_op jit(solution)/shard_map/ppermute | solution.py:239
  35.8 1.2 %collective-permute-start.11 = (bf16[128,512]{1,0:T(8,128)(2,1)S(1)}, bf16[128,512]{1,0:T(8,128)(2,1)S(1)}, u32[]{:S(2)}, u32[]{:S(2)}) collective-permute-start(bf16[128,512]{1,0:T(8,128)(2,1)S(1)} %get-tuple-element.29.scaled), channel_id=1, source_target_pairs={{64,0},{65,1},{66,2},{67,3},{68,4},{69,5},{70,6},{71,7},{72,8},{73... | collective-permute-start | bytes 393224 | tf_op jit(solution)/shard_map/ppermute | solution.py:239
  37.0 0.5 shard_map.115.before
  37.5 2.3 %collective-permute-done.9.scaled = bf16[128,512]{1,0:T(8,128)(2,1)S(1)} collective-permute-done((bf16[128,512]{1,0:T(8,128)(2,1)S(1)}, bf16[128,512]{1,0:T(8,128)(2,1)S(1)}, u32[]{:S(2)}, u32[]{:S(2)}) %collective-permute-start.9) | collective-permute-done | bytes 131104 | tf_op jit(solution)/shard_map/ppermute | solution.py:239
  39.8 0.5 shard_map.116.before
  40.3 3.2 %collective-permute-done.10.scaled = bf16[128,512]{1,0:T(8,128)(2,1)S(1)} collective-permute-done((bf16[128,512]{1,0:T(8,128)(2,1)S(1)}, bf16[128,512]{1,0:T(8,128)(2,1)S(1)}, u32[]{:S(2)}, u32[]{:S(2)}) %collective-permute-start.10) | collective-permute-done | bytes 131104 | tf_op jit(solution)/shard_map/ppermute | solution.py:239
  43.5 0.5 shard_map.117.before
  44.0 0.0 collective-permute-done.11.scaled
  44.0 0.5 shard_map.118
  44.5 1.0 %collective-permute-start.12 = (bf16[128,1024]{1,0:T(8,128)(2,1)S(1)}, bf16[128,1024]{1,0:T(8,128)(2,1)S(1)}, u32[]{:S(2)}, u32[]{:S(2)}) collective-permute-start(bf16[128,1024]{1,0:T(8,128)(2,1)S(1)} %get-tuple-element.34), channel_id=1, source_target_pairs={{32,0},{33,1},{34,2},{35,3},{36,4},{37,5},{38,6},{39,7},{40,8},{41... | collective-permute-start | bytes 786440 | tf_op jit(solution)/shard_map/ppermute | solution.py:239
  45.5 1.2 %collective-permute-done.12.got = bf16[128,1024]{1,0:T(8,128)(2,1)S(1)} collective-permute-done((bf16[128,1024]{1,0:T(8,128)(2,1)S(1)}, bf16[128,1024]{1,0:T(8,128)(2,1)S(1)}, u32[]{:S(2)}, u32[]{:S(2)}) %collective-permute-start.12) | collective-permute-done | bytes 262176 | tf_op jit(solution)/shard_map/ppermute | solution.py:239
  46.6 0.1 shard_map.119
  46.7 0.1 collective-permute-start.13
  46.8 5.1 %collective-permute-start.14 = (bf16[128,256]{1,0:T(8,128)(2,1)S(1)}, bf16[128,256]{1,0:T(8,128)(2,1)S(1)}, u32[]{:S(2)}, u32[]{:S(2)}) collective-permute-start(bf16[128,256]{1,0:T(8,128)(2,1)S(1)} %get-tuple-element.37), channel_id=1, source_target_pairs={{31,0},{2,1},{1,2},{4,3},{3,4},{6,5},{5,6},{8,7},{7,8},{10,9},{9,1... | collective-permute-start | bytes 196616 | tf_op jit(solution)/shard_map/ppermute | solution.py:239
  51.9 0.8 %shard_map.114 = f32[512,128]{1,0:T(8,128)} custom-call(f32[128,512]{1,0:T(8,128)S(1)} %get-tuple-element.28.source), custom_call_target="tpu_custom_call" | custom-call | flops 1048576 | bytes 1048576 | tf_op jit(solution)/shard_map/pallas_call | solution.py:214
  52.8 0.0 collective-permute-done.13.near
  52.8 1.3 %collective-permute-done.14.far = bf16[128,256]{1,0:T(8,128)(2,1)S(1)} collective-permute-done((bf16[128,256]{1,0:T(8,128)(2,1)S(1)}, bf16[128,256]{1,0:T(8,128)(2,1)S(1)}, u32[]{:S(2)}, u32[]{:S(2)}) %collective-permute-start.14) | collective-permute-done | bytes 65568 | tf_op jit(solution)/shard_map/ppermute | solution.py:239
  54.0 0.9 %shard_map.120 = f32[137,1,512]{2,1,0:T(1,128)} custom-call(f32[128,512]{1,0:T(8,128)S(1)} %get-tuple-element.35.mid, bf16[128,256]{1,0:T(8,128)(2,1)S(1)} %collective-permute-done.13.near, bf16[128,256]{1,0:T(8,128)(2,1)S(1)} %collective-permute-done.14.far, bf16[137,128]{1,0:T(8,128)(2,1)S(1)} %copy-done.1), custom_call_target="tpu_custom_call" | custom-call | flops 1048576 | bytes 1048576 | tf_op jit(solution)/shard_map/pallas_call | solution.py:214
  (3 shorter events, 0.0 us)
Async XLA Ops:
  0.6 0.9 %copy-start.2 = (bf16[1,512,137]{1,2,0:T(8,128)(2,1)S(1)}, bf16[1,512,137]{1,2,0:T(8,128)(2,1)}, u32[]{:S(2)}) copy-start(bf16[1,512,137]{1,2,0:T(8,128)(2,1)} %param.9) | copy-start | bytes 420868
  0.6 0.9 %copy-start.1 = (bf16[137,128]{1,0:T(8,128)(2,1)S(1)}, bf16[137,128]{1,0:T(8,128)(2,1)}, u32[]{:S(2)}) copy-start(bf16[137,128]{1,0:T(8,128)(2,1)} %jac.3) | copy-start | bytes 105220
  1.5 13.1 %copy-start.6 = (f32[512]{0:T(512)S(1)}, f32[512]{0:T(512)}, u32[]{:S(2)}) copy-start(f32[512]{0:T(512)} %param.13) | copy-start | bytes 6148
  1.8 9.2 %collective-permute-start = (bf16[128,256]{1,0:T(8,128)(2,1)S(1)}, bf16[128,256]{1,0:T(8,128)(2,1)S(1)}, u32[]{:S(2)}, u32[]{:S(2)}) collective-permute-start(bf16[128,256]{1,0:T(8,128)(2,1)S(1)} %get-tuple-element.21), channel_id=1, source_target_pairs={{1,0},{0,1},{3,2},{2,3},{5,4},{4,5},{7,6},{6,7},{9,8},{8,9},{11,10... | collective-permute-start | bytes 196616 | tf_op jit(solution)/shard_map/ppermute | solution.py:239
  3.9 8.8 %collective-permute-start.1 = (bf16[128,256]{1,0:T(8,128)(2,1)S(1)}, bf16[128,256]{1,0:T(8,128)(2,1)S(1)}, u32[]{:S(2)}, u32[]{:S(2)}) collective-permute-start(bf16[128,256]{1,0:T(8,128)(2,1)S(1)} %get-tuple-element.22), channel_id=1, source_target_pairs={{31,0},{2,1},{1,2},{4,3},{3,4},{6,5},{5,6},{8,7},{7,8},{10,9},{9,1... | collective-permute-start | bytes 196616 | tf_op jit(solution)/shard_map/ppermute | solution.py:239
  12.7 2.0 %copy-start.3 = (bf16[512,8]{0,1:T(8,128)(2,1)S(1)}, bf16[512,8]{0,1:T(8,128)(2,1)}, u32[]{:S(2)}) copy-start(bf16[512,8]{0,1:T(8,128)(2,1)} %param.11) | copy-start | bytes 24580
  12.7 9.6 %collective-permute-start.2 = (bf16[128,1024]{1,0:T(8,128)(2,1)S(1)}, bf16[128,1024]{1,0:T(8,128)(2,1)S(1)}, u32[]{:S(2)}, u32[]{:S(2)}) collective-permute-start(bf16[128,1024]{1,0:T(8,128)(2,1)S(1)} %shard_map.106.mine), channel_id=1, source_target_pairs={{32,0},{33,1},{34,2},{35,3},{36,4},{37,5},{38,6},{39,7},{40,8},{41... | collective-permute-start | bytes 786440 | tf_op jit(solution)/shard_map/ppermute | solution.py:239
  14.6 0.7 %copy-start.5 = (s32[512]{0:T(512)S(1)}, s32[512]{0:T(512)}, u32[]{:S(2)}) copy-start(s32[512]{0:T(512)} %param.12) | copy-start | bytes 6148
  14.6 0.7 %copy-start.4 = (s32[512]{0:T(512)S(1)}, s32[512]{0:T(512)}, u32[]{:S(2)}) copy-start(s32[512]{0:T(512)} %param.10) | copy-start | bytes 6148
  15.3 4.4 %collective-permute-start.6 = (f32[16,512]{1,0:T(8,128)S(1)}, f32[16,512]{1,0:T(8,128)S(1)}, u32[]{:S(2)}, u32[]{:S(2)}) collective-permute-start(f32[16,512]{1,0:T(8,128)S(1)} %shard_map.107.refs_0_.info), channel_id=1, source_target_pairs={{128,0},{129,1},{130,2},{131,3},{132,4},{133,5},{134,6},{135,7},{1... | collective-permute-start | bytes 98312 | tf_op jit(solution)/shard_map/ppermute | solution.py:239
  18.3 4.0 %collective-permute-start.3 = (f32[16,512]{1,0:T(8,128)S(1)}, f32[16,512]{1,0:T(8,128)S(1)}, u32[]{:S(2)}, u32[]{:S(2)}) collective-permute-start(f32[16,512]{1,0:T(8,128)S(1)} %shard_map.107.refs_0_.info), channel_id=1, source_target_pairs={{192,0},{193,1},{194,2},{195,3},{196,4},{197,5},{198,6},{199,7},{2... | collective-permute-start | bytes 98312 | tf_op jit(solution)/shard_map/ppermute | solution.py:239
  19.1 3.2 %collective-permute-start.4 = (f32[16,512]{1,0:T(8,128)S(1)}, f32[16,512]{1,0:T(8,128)S(1)}, u32[]{:S(2)}, u32[]{:S(2)}) collective-permute-start(f32[16,512]{1,0:T(8,128)S(1)} %shard_map.107.refs_0_.info), channel_id=1, source_target_pairs={{64,0},{65,1},{66,2},{67,3},{68,4},{69,5},{70,6},{71,7},{72,8},{73... | collective-permute-start | bytes 98312 | tf_op jit(solution)/shard_map/ppermute | solution.py:239
  23.1 5.2 %copy-start = (f32[512,128]{1,0:T(8,128)S(1)}, f32[512,128]{1,0:T(8,128)}, u32[]{:S(2)}) copy-start(f32[512,128]{1,0:T(8,128)} %source.1) | copy-start | bytes 786436
  23.1 6.6 %collective-permute-start.5 = (bf16[128,512]{1,0:T(8,128)(2,1)S(1)}, bf16[128,512]{1,0:T(8,128)(2,1)S(1)}, u32[]{:S(2)}, u32[]{:S(2)}) collective-permute-start(bf16[128,512]{1,0:T(8,128)(2,1)S(1)} %get-tuple-element.24), channel_id=1, source_target_pairs={{64,0},{65,1},{66,2},{67,3},{68,4},{69,5},{70,6},{71,7},{72,8},{73... | collective-permute-start | bytes 393224 | tf_op jit(solution)/shard_map/ppermute | solution.py:239
  23.6 7.2 %collective-permute-start.7 = (bf16[128,512]{1,0:T(8,128)(2,1)S(1)}, bf16[128,512]{1,0:T(8,128)(2,1)S(1)}, u32[]{:S(2)}, u32[]{:S(2)}) collective-permute-start(bf16[128,512]{1,0:T(8,128)(2,1)S(1)} %shard_map.111), channel_id=1, source_target_pairs={{128,0},{129,1},{130,2},{131,3},{132,4},{133,5},{134,6},{135,7},{1... | collective-permute-start | bytes 393224 | tf_op jit(solution)/shard_map/ppermute | solution.py:239
  26.6 7.5 %collective-permute-start.8 = (bf16[128,512]{1,0:T(8,128)(2,1)S(1)}, bf16[128,512]{1,0:T(8,128)(2,1)S(1)}, u32[]{:S(2)}, u32[]{:S(2)}) collective-permute-start(bf16[128,512]{1,0:T(8,128)(2,1)S(1)} %get-tuple-element.25), channel_id=1, source_target_pairs={{192,0},{193,1},{194,2},{195,3},{196,4},{197,5},{198,6},{199,7},{2... | collective-permute-start | bytes 393224 | tf_op jit(solution)/shard_map/ppermute | solution.py:239
  28.2 0.7 %copy-start.7 = (f32[128]{0:T(128)S(1)}, f32[128]{0:T(128)}, u32[]{:S(2)}) copy-start(f32[128]{0:T(128)} %param.17) | copy-start | bytes 1540
  34.3 5.5 %collective-permute-start.9 = (bf16[128,512]{1,0:T(8,128)(2,1)S(1)}, bf16[128,512]{1,0:T(8,128)(2,1)S(1)}, u32[]{:S(2)}, u32[]{:S(2)}) collective-permute-start(bf16[128,512]{1,0:T(8,128)(2,1)S(1)} %get-tuple-element.29.scaled), channel_id=1, source_target_pairs={{128,0},{129,1},{130,2},{131,3},{132,4},{133,5},{134,6},{135,7},{1... | collective-permute-start | bytes 393224 | tf_op jit(solution)/shard_map/ppermute | solution.py:239
  34.4 9.1 %collective-permute-start.10 = (bf16[128,512]{1,0:T(8,128)(2,1)S(1)}, bf16[128,512]{1,0:T(8,128)(2,1)S(1)}, u32[]{:S(2)}, u32[]{:S(2)}) collective-permute-start(bf16[128,512]{1,0:T(8,128)(2,1)S(1)} %get-tuple-element.29.scaled), channel_id=1, source_target_pairs={{192,0},{193,1},{194,2},{195,3},{196,4},{197,5},{198,6},{199,7},{2... | collective-permute-start | bytes 393224 | tf_op jit(solution)/shard_map/ppermute | solution.py:239
  35.8 8.2 %collective-permute-start.11 = (bf16[128,512]{1,0:T(8,128)(2,1)S(1)}, bf16[128,512]{1,0:T(8,128)(2,1)S(1)}, u32[]{:S(2)}, u32[]{:S(2)}) collective-permute-start(bf16[128,512]{1,0:T(8,128)(2,1)S(1)} %get-tuple-element.29.scaled), channel_id=1, source_target_pairs={{64,0},{65,1},{66,2},{67,3},{68,4},{69,5},{70,6},{71,7},{72,8},{73... | collective-permute-start | bytes 393224 | tf_op jit(solution)/shard_map/ppermute | solution.py:239
  44.5 2.1 %collective-permute-start.12 = (bf16[128,1024]{1,0:T(8,128)(2,1)S(1)}, bf16[128,1024]{1,0:T(8,128)(2,1)S(1)}, u32[]{:S(2)}, u32[]{:S(2)}) collective-permute-start(bf16[128,1024]{1,0:T(8,128)(2,1)S(1)} %get-tuple-element.34), channel_id=1, source_target_pairs={{32,0},{33,1},{34,2},{35,3},{36,4},{37,5},{38,6},{39,7},{40,8},{41... | collective-permute-start | bytes 786440 | tf_op jit(solution)/shard_map/ppermute | solution.py:239
  46.7 6.1 %collective-permute-start.13 = (bf16[128,256]{1,0:T(8,128)(2,1)S(1)}, bf16[128,256]{1,0:T(8,128)(2,1)S(1)}, u32[]{:S(2)}, u32[]{:S(2)}) collective-permute-start(bf16[128,256]{1,0:T(8,128)(2,1)S(1)} %get-tuple-element.36), channel_id=1, source_target_pairs={{1,0},{0,1},{3,2},{2,3},{5,4},{4,5},{7,6},{6,7},{9,8},{8,9},{11,10... | collective-permute-start | bytes 196616 | tf_op jit(solution)/shard_map/ppermute | solution.py:239
  46.8 7.2 %collective-permute-start.14 = (bf16[128,256]{1,0:T(8,128)(2,1)S(1)}, bf16[128,256]{1,0:T(8,128)(2,1)S(1)}, u32[]{:S(2)}, u32[]{:S(2)}) collective-permute-start(bf16[128,256]{1,0:T(8,128)(2,1)S(1)} %get-tuple-element.37), channel_id=1, source_target_pairs={{31,0},{2,1},{1,2},{4,3},{3,4},{6,5},{5,6},{8,7},{7,8},{10,9},{9,1... | collective-permute-start | bytes 196616 | tf_op jit(solution)/shard_map/ppermute | solution.py:239

commit v5 on v4

--- a/solution.py
+++ b/solution.py
@@ -11,7 +11,6 @@
 F32 = jnp.float32
 BF16 = jnp.bfloat16
 GROUP = 16
-SWAP_ORDER = (2, 3, 1)
 FIRST_FLOPS = 1 << 34
 
 
@@ -45,17 +44,15 @@
     out[...] = jnp.zeros_like(out)
 
 
-def project_kernel(first, state, jac, full, near, far):
-    half = full.shape[1] // 2
+def enter_kernel(tiles, first, state, jac, start, weight, slot, frac, full, near, far, info):
+    cols = full.shape[1]
+    half = cols // 2
     out = lax.dot_general(
         jac[...], state[...], (((0,), (0,)), ((), ())), preferred_element_type=F32
     ).astype(BF16)
     full[...] = out
     put_rims(near, far, out[:, :half], out[:, half:])
-
-
-def info_kernel(cols, tiles, start, weight, slot, frac, info):
-    base = lax.axis_index("space") * cols - cols // 2
+    base = lax.axis_index("space") * cols - half
     total = cols * tiles
     local = start[...] - base
     local = jnp.where(local < 0, local + total, local)
@@ -155,17 +152,19 @@
     scaled[...] = (gap * scale[:, 0:1]).astype(BF16)
 
 
+def weighted(info, source, slot):
+    return (slot_weight(info, slot) * source[...].astype(F32)).astype(BF16)
+
+
+def spread_rows(rows, mat):
+    return lax.dot_general(
+        rows, mat[...], (((1,), (1,)), ((), ())), preferred_element_type=F32
+    )
+
+
 def spread_one(info, source, mat):
-    own_slot, other_slot = held_slots()
-    rows = source[...].astype(F32)
-    mine = (slot_weight(info, own_slot) * rows).astype(BF16)
-    other = (slot_weight(info, other_slot) * rows).astype(BF16)
-    return lax.dot_general(
-        jnp.concatenate([mine, other], axis=0),
-        mat[...],
-        (((1,), (1,)), ((), ())),
-        preferred_element_type=F32,
-    )
+    rows = [weighted(info, source, slot) for slot in held_slots()]
+    return spread_rows(jnp.concatenate(rows, axis=0), mat)
 
 
 def spread_first_kernel(info, scaled, mat, acc):
@@ -176,11 +175,15 @@
     acc[...] = before[...] + spread_one(info, scaled, mat)
 
 
-def spread_last_kernel(before, info, scaled, mat, own, give):
+def spread_give_kernel(before, info, scaled, mat, give):
+    chan = give.shape[0]
+    part = spread_rows(weighted(info, scaled, held_slots()[1]), mat)
+    give[...] = (before[chan:, :] + part).astype(BF16)
+
+
+def spread_keep_kernel(before, info, scaled, mat, own):
     chan = own.shape[0]
-    total = before[...] + spread_one(info, scaled, mat)
-    own[...] = total[:chan]
-    give[...] = total[chan:].astype(BF16)
+    own[...] = before[:chan, :] + spread_rows(weighted(info, scaled, held_slots()[0]), mat)
 
 
 def join_kernel(own, got, mid, near, far):
@@ -252,16 +255,17 @@
             return vector.reshape(1, -1)
 
         (first,) = call(first_kernel, [((8, 128), F32)], flops=FIRST_FLOPS)
-        full, near, far = call(
-            project_kernel,
-            [((chan, cols), BF16), ((chan, half), BF16), ((chan, half), BF16)],
+        full, near, far, info = call(
+            functools.partial(enter_kernel, n_space),
+            [
+                ((chan, cols), BF16),
+                ((chan, half), BF16),
+                ((chan, half), BF16),
+                ((16, obs), F32),
+            ],
             first,
             own.T,
             jacobian,
-        )
-        (info,) = call(
-            functools.partial(info_kernel, cols, n_space),
-            [((16, obs), F32)],
             flat(obs_start),
             foot_weight.T,
             flat(obs_slot),
@@ -289,7 +293,8 @@
         (far,) = call(gather_kernel, [((chan, obs), BF16)], wide, other, infos[2], mats[2])
         parts = [None] * lanes
         parts[2] = swap(far, y=2)
-        for j, part in zip((3, 1), gather([3, 1])):
+        for j in (1, 3):
+            (part,) = gather([j])
             parts[j] = swap(part, y=j)
         (parts[0],) = gather([0])
         values, scale = call(
@@ -312,8 +317,7 @@
         all_scaled = [scaled] + [swap(scaled, y=j) for j in range(1, lanes)]
         (acc,) = call(spread_first_kernel, [((2 * chan, width), F32)], info, scaled, mats[0])
         (departures,) = call(turn_kernel, [((obs, chan), F32)], gaps)
-        *early, last = SWAP_ORDER
-        for j in early:
+        for j in range(1, lanes - 1):
             (acc,) = call(
                 spread_next_kernel,
                 [((2 * chan, width), F32)],
@@ -322,19 +326,12 @@
                 all_scaled[j],
                 mats[j],
             )
-        mine, give = call(
-            spread_last_kernel,
-            [((chan, width), F32), ((chan, width), BF16)],
-            acc,
-            infos[last],
-            all_scaled[last],
-            mats[last],
-        )
+        rest = (acc, infos[lanes - 1], all_scaled[lanes - 1], mats[lanes - 1])
+        (give,) = call(spread_give_kernel, [((chan, width), BF16)], *rest)
+        give = swap(give, core=1)
+        (mine,) = call(spread_keep_kernel, [((chan, width), F32)], *rest)
         mid, near, far = call(
-            join_kernel,
-            [((chan, cols), F32)] + [((chan, half), BF16)] * 2,
-            mine,
-            swap(give, core=1),
+            join_kernel, [((chan, cols), F32)] + [((chan, half), BF16)] * 2, mine, give
         )
         (adjoint,) = call(
             finish_kernel,

time: 55.1 us -> 53.7 us (0.975)
  waiting for transfers between devices: 17.2 us -> 14 us
  starting transfers between devices: 27.9 us -> 29.7 us
  local copies, waits for them, and re-layouts: 2.23 us -> 1.51 us
  Pallas kernels: 6.18 us -> 6.85 us
    ppermute x15, waiting for transfers between devices: 17.2 us -> 14 us  [swap(): return lax.ppermute(block, ('tm', 'space'), route)]
    ppermute x15, starting transfers between devices: 27.9 us -> 29.7 us  [swap(): return lax.ppermute(block, ('tm', 'space'), route)]
    unnamed x16, local copies, waits for them, and re-layouts: 2.23 us -> 1.51 us
    pallas_call x17 -> x18, Pallas kernels: 6.18 us -> 6.85 us  [call(): pl.pallas_call(kernel, out_shape=[jax.ShapeDtypeStruct(shape, dtype) for...]
  transfers between devices with their start and end apart: 15 -> 15, of which waited for: 9 -> 9; matrix products, arithmetic and copies ran while one was open for 0% -> 0% of each run, Pallas kernels for 7% -> 9%
where the time goes in v5:
time: 53.7 us; the launch traced here: 53.6 us
  starting transfers between devices  29.7 us (55%)
  waiting for transfers between devices  14 us (26%)
  Pallas kernels  6.85 us (13%)
  between operations  1.53 us (3%)
  local copies, waits for them, and re-layouts  1.51 us (3%)
    ppermute x15, starting transfers between devices, swap(): return lax.ppermute(block, ('tm', 'space'), route)  29.7 us
    ppermute x15, waiting for transfers between devices, swap(): return lax.ppermute(block, ('tm', 'space'), route)  14 us
    pallas_call x18, Pallas kernels, call(): pl.pallas_call(kernel, out_shape=[jax.ShapeDtypeStruct(shape, dtype) for...  6.85 us
    unnamed x16, local copies, waits for them, and re-layouts  1.51 us
  transfers between devices with their start and end apart: 15, of which 9 were waited for; matrix products, arithmetic and copies ran while one was open for 0% of the time, Pallas kernels for 9%

profile of v5, /device:TPU:1, one launch (start us, length us, event | category | flops | bytes accessed | tf_op | source)
XLA Modules:
  0.0 53.6 jit_solution(3289995843873093157)
XLA Ops:
  0.6 0.0 copy-start.2
  0.6 0.0 copy-start.1
  0.7 0.0 copy-start.4
  0.7 0.0 copy-start.5
  0.7 0.0 copy-start.6
  0.7 0.0 copy-start.3
  0.7 0.8 %copy-done.2 = bf16[1,512,137]{1,2,0:T(8,128)(2,1)S(1)} copy-done((bf16[1,512,137]{1,2,0:T(8,128)(2,1)S(1)}, bf16[1,512,137]{1,2,0:T(8,128)(2,1)}, u32[]{:S(2)}) %copy-start.2) | copy-done | bytes 140312
  1.5 0.0 copy-done.1
  1.5 0.0 copy-done.4
  1.5 0.0 copy-done.5
  1.6 0.0 copy-done.6
  1.6 0.0 copy-done.3
  1.6 0.2 shard_map.105
  1.8 2.1 %collective-permute-start = (bf16[128,256]{1,0:T(8,128)(2,1)S(1)}, bf16[128,256]{1,0:T(8,128)(2,1)S(1)}, u32[]{:S(2)}, u32[]{:S(2)}) collective-permute-start(bf16[128,256]{1,0:T(8,128)(2,1)S(1)} %get-tuple-element.20), channel_id=1, source_target_pairs={{1,0},{0,1},{3,2},{2,3},{5,4},{4,5},{7,6},{6,7},{9,8},{8,9},{11,10... | collective-permute-start | bytes 196616 | tf_op jit(solution)/shard_map/ppermute | solution.py:242
  3.9 7.1 %collective-permute-start.1 = (bf16[128,256]{1,0:T(8,128)(2,1)S(1)}, bf16[128,256]{1,0:T(8,128)(2,1)S(1)}, u32[]{:S(2)}, u32[]{:S(2)}) collective-permute-start(bf16[128,256]{1,0:T(8,128)(2,1)S(1)} %get-tuple-element.21), channel_id=1, source_target_pairs={{31,0},{2,1},{1,2},{4,3},{3,4},{6,5},{5,6},{8,7},{7,8},{10,9},{9,1... | collective-permute-start | bytes 196616 | tf_op jit(solution)/shard_map/ppermute | solution.py:242
  11.0 0.0 collective-permute-done.near
  11.0 1.6 %collective-permute-done.1.far = bf16[128,256]{1,0:T(8,128)(2,1)S(1)} collective-permute-done((bf16[128,256]{1,0:T(8,128)(2,1)S(1)}, bf16[128,256]{1,0:T(8,128)(2,1)S(1)}, u32[]{:S(2)}, u32[]{:S(2)}) %collective-permute-start.1) | collective-permute-done | bytes 65568 | tf_op jit(solution)/shard_map/ppermute | solution.py:242
  12.7 1.9 %collective-permute-start.2 = (bf16[128,1024]{1,0:T(8,128)(2,1)S(1)}, bf16[128,1024]{1,0:T(8,128)(2,1)S(1)}, u32[]{:S(2)}, u32[]{:S(2)}) collective-permute-start(bf16[128,1024]{1,0:T(8,128)(2,1)S(1)} %shard_map.106.mine), channel_id=1, source_target_pairs={{32,0},{33,1},{34,2},{35,3},{36,4},{37,5},{38,6},{39,7},{40,8},{41... | collective-permute-start | bytes 786440 | tf_op jit(solution)/shard_map/ppermute | solution.py:242
  14.6 2.9 %collective-permute-start.5 = (f32[16,512]{1,0:T(8,128)S(1)}, f32[16,512]{1,0:T(8,128)S(1)}, u32[]{:S(2)}, u32[]{:S(2)}) collective-permute-start(f32[16,512]{1,0:T(8,128)S(1)} %get-tuple-element.22.refs_0_.info), channel_id=1, source_target_pairs={{128,0},{129,1},{130,2},{131,3},{132,4},{133,5},{134,6},{135,7},{1... | collective-permute-start | bytes 98312 | tf_op jit(solution)/shard_map/ppermute | solution.py:242
  17.6 0.4 collective-permute-start.3
  17.9 0.4 collective-permute-start.7
  18.3 0.6 %collective-permute-done.5.info = f32[16,512]{1,0:T(8,128)S(1)} collective-permute-done((f32[16,512]{1,0:T(8,128)S(1)}, f32[16,512]{1,0:T(8,128)S(1)}, u32[]{:S(2)}, u32[]{:S(2)}) %collective-permute-start.5) | collective-permute-done | bytes 32800 | tf_op jit(solution)/shard_map/ppermute | solution.py:242
  18.9 0.2 shard_map.109.mat
  19.1 1.3 %collective-permute-done.3.refs_0_.info = f32[16,512]{1,0:T(8,128)S(1)} collective-permute-done((f32[16,512]{1,0:T(8,128)S(1)}, f32[16,512]{1,0:T(8,128)S(1)}, u32[]{:S(2)}, u32[]{:S(2)}) %collective-permute-start.3) | collective-permute-done | bytes 32800 | tf_op jit(solution)/shard_map/ppermute | solution.py:242
  20.3 0.0 collective-permute-done.2.other
  20.3 0.5 shard_map.108
  20.8 1.0 %collective-permute-start.4 = (bf16[128,512]{1,0:T(8,128)(2,1)S(1)}, bf16[128,512]{1,0:T(8,128)(2,1)S(1)}, u32[]{:S(2)}, u32[]{:S(2)}) collective-permute-start(bf16[128,512]{1,0:T(8,128)(2,1)S(1)} %get-tuple-element.24), channel_id=1, source_target_pairs={{64,0},{65,1},{66,2},{67,3},{68,4},{69,5},{70,6},{71,7},{72,8},{73... | collective-permute-start | bytes 393224 | tf_op jit(solution)/shard_map/ppermute | solution.py:242
  21.8 0.4 shard_map.110
  22.2 0.0 copy-start
  22.2 1.9 %collective-permute-start.6 = (bf16[128,512]{1,0:T(8,128)(2,1)S(1)}, bf16[128,512]{1,0:T(8,128)(2,1)S(1)}, u32[]{:S(2)}, u32[]{:S(2)}) collective-permute-start(bf16[128,512]{1,0:T(8,128)(2,1)S(1)} %shard_map.110), channel_id=1, source_target_pairs={{128,0},{129,1},{130,2},{131,3},{132,4},{133,5},{134,6},{135,7},{1... | collective-permute-start | bytes 393224 | tf_op jit(solution)/shard_map/ppermute | solution.py:242
  24.1 0.0 collective-permute-done.7.refs_0_.info
  24.1 0.5 shard_map.111
  24.6 1.3 %collective-permute-start.8 = (bf16[128,512]{1,0:T(8,128)(2,1)S(1)}, bf16[128,512]{1,0:T(8,128)(2,1)S(1)}, u32[]{:S(2)}, u32[]{:S(2)}) collective-permute-start(bf16[128,512]{1,0:T(8,128)(2,1)S(1)} %get-tuple-element.25), channel_id=1, source_target_pairs={{192,0},{193,1},{194,2},{195,3},{196,4},{197,5},{198,6},{199,7},{2... | collective-permute-start | bytes 393224 | tf_op jit(solution)/shard_map/ppermute | solution.py:242
  26.5 0.0 copy-start.7
  26.5 0.0 copy-done
  26.6 0.6 %copy-done.7 = f32[128]{0:T(128)S(1)} copy-done((f32[128]{0:T(128)S(1)}, f32[128]{0:T(128)}, u32[]{:S(2)}) %copy-start.7) | copy-done | bytes 536
  27.2 0.3 shard_map.112
  27.5 0.5 shard_map.107
  28.0 0.0 collective-permute-done.4.refs_1_
  28.0 1.1 %collective-permute-done.6.refs_2_ = bf16[128,512]{1,0:T(8,128)(2,1)S(1)} collective-permute-done((bf16[128,512]{1,0:T(8,128)(2,1)S(1)}, bf16[128,512]{1,0:T(8,128)(2,1)S(1)}, u32[]{:S(2)}, u32[]{:S(2)}) %collective-permute-start.6) | collective-permute-done | bytes 131104 | tf_op jit(solution)/shard_map/ppermute | solution.py:242
  29.0 3.6 %collective-permute-done.8.refs_3_ = bf16[128,512]{1,0:T(8,128)(2,1)S(1)} collective-permute-done((bf16[128,512]{1,0:T(8,128)(2,1)S(1)}, bf16[128,512]{1,0:T(8,128)(2,1)S(1)}, u32[]{:S(2)}, u32[]{:S(2)}) %collective-permute-start.8) | collective-permute-done | bytes 131104 | tf_op jit(solution)/shard_map/ppermute | solution.py:242
  32.6 0.1 shard_map.113
  32.7 0.1 collective-permute-start.9
  32.8 1.6 %collective-permute-start.10 = (bf16[128,512]{1,0:T(8,128)(2,1)S(1)}, bf16[128,512]{1,0:T(8,128)(2,1)S(1)}, u32[]{:S(2)}, u32[]{:S(2)}) collective-permute-start(bf16[128,512]{1,0:T(8,128)(2,1)S(1)} %get-tuple-element.29.scaled), channel_id=1, source_target_pairs={{128,0},{129,1},{130,2},{131,3},{132,4},{133,5},{134,6},{135,7},{1... | collective-permute-start | bytes 393224 | tf_op jit(solution)/shard_map/ppermute | solution.py:242
  34.5 2.2 %collective-permute-start.11 = (bf16[128,512]{1,0:T(8,128)(2,1)S(1)}, bf16[128,512]{1,0:T(8,128)(2,1)S(1)}, u32[]{:S(2)}, u32[]{:S(2)}) collective-permute-start(bf16[128,512]{1,0:T(8,128)(2,1)S(1)} %get-tuple-element.29.scaled), channel_id=1, source_target_pairs={{192,0},{193,1},{194,2},{195,3},{196,4},{197,5},{198,6},{199,7},{2... | collective-permute-start | bytes 393224 | tf_op jit(solution)/shard_map/ppermute | solution.py:242
  36.7 0.5 shard_map.115.before
  37.2 0.0 collective-permute-done.9.scaled
  37.2 0.5 shard_map.116.before
  37.7 1.5 %collective-permute-done.10.scaled = bf16[128,512]{1,0:T(8,128)(2,1)S(1)} collective-permute-done((bf16[128,512]{1,0:T(8,128)(2,1)S(1)}, bf16[128,512]{1,0:T(8,128)(2,1)S(1)}, u32[]{:S(2)}, u32[]{:S(2)}) %collective-permute-start.10) | collective-permute-done | bytes 131104 | tf_op jit(solution)/shard_map/ppermute | solution.py:242
  39.2 0.5 shard_map.117.before
  39.7 2.4 %collective-permute-done.11.scaled = bf16[128,512]{1,0:T(8,128)(2,1)S(1)} collective-permute-done((bf16[128,512]{1,0:T(8,128)(2,1)S(1)}, bf16[128,512]{1,0:T(8,128)(2,1)S(1)}, u32[]{:S(2)}, u32[]{:S(2)}) %collective-permute-start.11) | collective-permute-done | bytes 131104 | tf_op jit(solution)/shard_map/ppermute | solution.py:242
  42.1 0.5 shard_map.119
  42.5 1.6 %collective-permute-start.12 = (bf16[128,1024]{1,0:T(8,128)(2,1)S(1)}, bf16[128,1024]{1,0:T(8,128)(2,1)S(1)}, u32[]{:S(2)}, u32[]{:S(2)}) collective-permute-start(bf16[128,1024]{1,0:T(8,128)(2,1)S(1)} %shard_map.119), channel_id=1, source_target_pairs={{32,0},{33,1},{34,2},{35,3},{36,4},{37,5},{38,6},{39,7},{40,8},{41... | collective-permute-start | bytes 786440 | tf_op jit(solution)/shard_map/ppermute | solution.py:242
  44.1 0.5 shard_map.118.own
  44.6 0.7 %collective-permute-done.12.got = bf16[128,1024]{1,0:T(8,128)(2,1)S(1)} collective-permute-done((bf16[128,1024]{1,0:T(8,128)(2,1)S(1)}, bf16[128,1024]{1,0:T(8,128)(2,1)S(1)}, u32[]{:S(2)}, u32[]{:S(2)}) %collective-permute-start.12) | collective-permute-done | bytes 262176 | tf_op jit(solution)/shard_map/ppermute | solution.py:242
  45.3 0.1 shard_map.120
  45.4 0.1 collective-permute-start.13
  45.5 5.1 %collective-permute-start.14 = (bf16[128,256]{1,0:T(8,128)(2,1)S(1)}, bf16[128,256]{1,0:T(8,128)(2,1)S(1)}, u32[]{:S(2)}, u32[]{:S(2)}) collective-permute-start(bf16[128,256]{1,0:T(8,128)(2,1)S(1)} %get-tuple-element.35), channel_id=1, source_target_pairs={{31,0},{2,1},{1,2},{4,3},{3,4},{6,5},{5,6},{8,7},{7,8},{10,9},{9,1... | collective-permute-start | bytes 196616 | tf_op jit(solution)/shard_map/ppermute | solution.py:242
  50.6 0.8 %shard_map.114 = f32[512,128]{1,0:T(8,128)} custom-call(f32[128,512]{1,0:T(8,128)S(1)} %get-tuple-element.28.source), custom_call_target="tpu_custom_call" | custom-call | flops 1048576 | bytes 1048576 | tf_op jit(solution)/shard_map/pallas_call | solution.py:217
  51.4 0.0 collective-permute-done.13.near
  51.4 1.3 %collective-permute-done.14.far = bf16[128,256]{1,0:T(8,128)(2,1)S(1)} collective-permute-done((bf16[128,256]{1,0:T(8,128)(2,1)S(1)}, bf16[128,256]{1,0:T(8,128)(2,1)S(1)}, u32[]{:S(2)}, u32[]{:S(2)}) %collective-permute-start.14) | collective-permute-done | bytes 65568 | tf_op jit(solution)/shard_map/ppermute | solution.py:242
  52.7 0.9 %shard_map.121 = f32[137,1,512]{2,1,0:T(1,128)} custom-call(f32[128,512]{1,0:T(8,128)S(1)} %get-tuple-element.33.mid, bf16[128,256]{1,0:T(8,128)(2,1)S(1)} %collective-permute-done.13.near, bf16[128,256]{1,0:T(8,128)(2,1)S(1)} %collective-permute-done.14.far, bf16[137,128]{1,0:T(8,128)(2,1)S(1)} %copy-done.1), custom_call_target="tpu_custom_call" | custom-call | flops 1048576 | bytes 1048576 | tf_op jit(solution)/shard_map/pallas_call | solution.py:217
  (2 shorter events, 0.0 us)
Async XLA Ops:
  0.6 0.9 %copy-start.2 = (bf16[1,512,137]{1,2,0:T(8,128)(2,1)S(1)}, bf16[1,512,137]{1,2,0:T(8,128)(2,1)}, u32[]{:S(2)}) copy-start(bf16[1,512,137]{1,2,0:T(8,128)(2,1)} %param.9) | copy-start | bytes 420868
  0.6 0.9 %copy-start.1 = (bf16[137,128]{1,0:T(8,128)(2,1)S(1)}, bf16[137,128]{1,0:T(8,128)(2,1)}, u32[]{:S(2)}) copy-start(bf16[137,128]{1,0:T(8,128)(2,1)} %jac.3) | copy-start | bytes 105220
  0.7 0.9 %copy-start.4 = (s32[512]{0:T(512)S(1)}, s32[512]{0:T(512)}, u32[]{:S(2)}) copy-start(s32[512]{0:T(512)} %param.10) | copy-start | bytes 6148
  0.7 0.9 %copy-start.5 = (s32[512]{0:T(512)S(1)}, s32[512]{0:T(512)}, u32[]{:S(2)}) copy-start(s32[512]{0:T(512)} %param.12) | copy-start | bytes 6148
  0.7 0.9 %copy-start.6 = (f32[512]{0:T(512)S(1)}, f32[512]{0:T(512)}, u32[]{:S(2)}) copy-start(f32[512]{0:T(512)} %param.13) | copy-start | bytes 6148
  0.7 0.9 %copy-start.3 = (bf16[512,8]{0,1:T(8,128)(2,1)S(1)}, bf16[512,8]{0,1:T(8,128)(2,1)}, u32[]{:S(2)}) copy-start(bf16[512,8]{0,1:T(8,128)(2,1)} %param.11) | copy-start | bytes 24580
  1.8 9.2 %collective-permute-start = (bf16[128,256]{1,0:T(8,128)(2,1)S(1)}, bf16[128,256]{1,0:T(8,128)(2,1)S(1)}, u32[]{:S(2)}, u32[]{:S(2)}) collective-permute-start(bf16[128,256]{1,0:T(8,128)(2,1)S(1)} %get-tuple-element.20), channel_id=1, source_target_pairs={{1,0},{0,1},{3,2},{2,3},{5,4},{4,5},{7,6},{6,7},{9,8},{8,9},{11,10... | collective-permute-start | bytes 196616 | tf_op jit(solution)/shard_map/ppermute | solution.py:242
  3.9 8.8 %collective-permute-start.1 = (bf16[128,256]{1,0:T(8,128)(2,1)S(1)}, bf16[128,256]{1,0:T(8,128)(2,1)S(1)}, u32[]{:S(2)}, u32[]{:S(2)}) collective-permute-start(bf16[128,256]{1,0:T(8,128)(2,1)S(1)} %get-tuple-element.21), channel_id=1, source_target_pairs={{31,0},{2,1},{1,2},{4,3},{3,4},{6,5},{5,6},{8,7},{7,8},{10,9},{9,1... | collective-permute-start | bytes 196616 | tf_op jit(solution)/shard_map/ppermute | solution.py:242
  12.7 7.6 %collective-permute-start.2 = (bf16[128,1024]{1,0:T(8,128)(2,1)S(1)}, bf16[128,1024]{1,0:T(8,128)(2,1)S(1)}, u32[]{:S(2)}, u32[]{:S(2)}) collective-permute-start(bf16[128,1024]{1,0:T(8,128)(2,1)S(1)} %shard_map.106.mine), channel_id=1, source_target_pairs={{32,0},{33,1},{34,2},{35,3},{36,4},{37,5},{38,6},{39,7},{40,8},{41... | collective-permute-start | bytes 786440 | tf_op jit(solution)/shard_map/ppermute | solution.py:242
  14.6 4.3 %collective-permute-start.5 = (f32[16,512]{1,0:T(8,128)S(1)}, f32[16,512]{1,0:T(8,128)S(1)}, u32[]{:S(2)}, u32[]{:S(2)}) collective-permute-start(f32[16,512]{1,0:T(8,128)S(1)} %get-tuple-element.22.refs_0_.info), channel_id=1, source_target_pairs={{128,0},{129,1},{130,2},{131,3},{132,4},{133,5},{134,6},{135,7},{1... | collective-permute-start | bytes 98312 | tf_op jit(solution)/shard_map/ppermute | solution.py:242
  17.6 2.8 %collective-permute-start.3 = (f32[16,512]{1,0:T(8,128)S(1)}, f32[16,512]{1,0:T(8,128)S(1)}, u32[]{:S(2)}, u32[]{:S(2)}) collective-permute-start(f32[16,512]{1,0:T(8,128)S(1)} %get-tuple-element.22.refs_0_.info), channel_id=1, source_target_pairs={{64,0},{65,1},{66,2},{67,3},{68,4},{69,5},{70,6},{71,7},{72,8},{73... | collective-permute-start | bytes 98312 | tf_op jit(solution)/shard_map/ppermute | solution.py:242
  17.9 6.2 %collective-permute-start.7 = (f32[16,512]{1,0:T(8,128)S(1)}, f32[16,512]{1,0:T(8,128)S(1)}, u32[]{:S(2)}, u32[]{:S(2)}) collective-permute-start(f32[16,512]{1,0:T(8,128)S(1)} %get-tuple-element.22.refs_0_.info), channel_id=1, source_target_pairs={{192,0},{193,1},{194,2},{195,3},{196,4},{197,5},{198,6},{199,7},{2... | collective-permute-start | bytes 98312 | tf_op jit(solution)/shard_map/ppermute | solution.py:242
  20.8 7.1 %collective-permute-start.4 = (bf16[128,512]{1,0:T(8,128)(2,1)S(1)}, bf16[128,512]{1,0:T(8,128)(2,1)S(1)}, u32[]{:S(2)}, u32[]{:S(2)}) collective-permute-start(bf16[128,512]{1,0:T(8,128)(2,1)S(1)} %get-tuple-element.24), channel_id=1, source_target_pairs={{64,0},{65,1},{66,2},{67,3},{68,4},{69,5},{70,6},{71,7},{72,8},{73... | collective-permute-start | bytes 393224 | tf_op jit(solution)/shard_map/ppermute | solution.py:242
  22.2 4.3 %copy-start = (f32[512,128]{1,0:T(8,128)S(1)}, f32[512,128]{1,0:T(8,128)}, u32[]{:S(2)}) copy-start(f32[512,128]{1,0:T(8,128)} %source.1) | copy-start | bytes 786436
  22.2 6.8 %collective-permute-start.6 = (bf16[128,512]{1,0:T(8,128)(2,1)S(1)}, bf16[128,512]{1,0:T(8,128)(2,1)S(1)}, u32[]{:S(2)}, u32[]{:S(2)}) collective-permute-start(bf16[128,512]{1,0:T(8,128)(2,1)S(1)} %shard_map.110), channel_id=1, source_target_pairs={{128,0},{129,1},{130,2},{131,3},{132,4},{133,5},{134,6},{135,7},{1... | collective-permute-start | bytes 393224 | tf_op jit(solution)/shard_map/ppermute | solution.py:242
  24.6 8.0 %collective-permute-start.8 = (bf16[128,512]{1,0:T(8,128)(2,1)S(1)}, bf16[128,512]{1,0:T(8,128)(2,1)S(1)}, u32[]{:S(2)}, u32[]{:S(2)}) collective-permute-start(bf16[128,512]{1,0:T(8,128)(2,1)S(1)} %get-tuple-element.25), channel_id=1, source_target_pairs={{192,0},{193,1},{194,2},{195,3},{196,4},{197,5},{198,6},{199,7},{2... | collective-permute-start | bytes 393224 | tf_op jit(solution)/shard_map/ppermute | solution.py:242
  26.5 0.7 %copy-start.7 = (f32[128]{0:T(128)S(1)}, f32[128]{0:T(128)}, u32[]{:S(2)}) copy-start(f32[128]{0:T(128)} %param.17) | copy-start | bytes 1540
  32.7 4.4 %collective-permute-start.9 = (bf16[128,512]{1,0:T(8,128)(2,1)S(1)}, bf16[128,512]{1,0:T(8,128)(2,1)S(1)}, u32[]{:S(2)}, u32[]{:S(2)}) collective-permute-start(bf16[128,512]{1,0:T(8,128)(2,1)S(1)} %get-tuple-element.29.scaled), channel_id=1, source_target_pairs={{64,0},{65,1},{66,2},{67,3},{68,4},{69,5},{70,6},{71,7},{72,8},{73... | collective-permute-start | bytes 393224 | tf_op jit(solution)/shard_map/ppermute | solution.py:242
  32.8 6.3 %collective-permute-start.10 = (bf16[128,512]{1,0:T(8,128)(2,1)S(1)}, bf16[128,512]{1,0:T(8,128)(2,1)S(1)}, u32[]{:S(2)}, u32[]{:S(2)}) collective-permute-start(bf16[128,512]{1,0:T(8,128)(2,1)S(1)} %get-tuple-element.29.scaled), channel_id=1, source_target_pairs={{128,0},{129,1},{130,2},{131,3},{132,4},{133,5},{134,6},{135,7},{1... | collective-permute-start | bytes 393224 | tf_op jit(solution)/shard_map/ppermute | solution.py:242
  34.5 7.6 %collective-permute-start.11 = (bf16[128,512]{1,0:T(8,128)(2,1)S(1)}, bf16[128,512]{1,0:T(8,128)(2,1)S(1)}, u32[]{:S(2)}, u32[]{:S(2)}) collective-permute-start(bf16[128,512]{1,0:T(8,128)(2,1)S(1)} %get-tuple-element.29.scaled), channel_id=1, source_target_pairs={{192,0},{193,1},{194,2},{195,3},{196,4},{197,5},{198,6},{199,7},{2... | collective-permute-start | bytes 393224 | tf_op jit(solution)/shard_map/ppermute | solution.py:242
  42.5 2.8 %collective-permute-start.12 = (bf16[128,1024]{1,0:T(8,128)(2,1)S(1)}, bf16[128,1024]{1,0:T(8,128)(2,1)S(1)}, u32[]{:S(2)}, u32[]{:S(2)}) collective-permute-start(bf16[128,1024]{1,0:T(8,128)(2,1)S(1)} %shard_map.119), channel_id=1, source_target_pairs={{32,0},{33,1},{34,2},{35,3},{36,4},{37,5},{38,6},{39,7},{40,8},{41... | collective-permute-start | bytes 786440 | tf_op jit(solution)/shard_map/ppermute | solution.py:242
  45.4 6.1 %collective-permute-start.13 = (bf16[128,256]{1,0:T(8,128)(2,1)S(1)}, bf16[128,256]{1,0:T(8,128)(2,1)S(1)}, u32[]{:S(2)}, u32[]{:S(2)}) collective-permute-start(bf16[128,256]{1,0:T(8,128)(2,1)S(1)} %get-tuple-element.34), channel_id=1, source_target_pairs={{1,0},{0,1},{3,2},{2,3},{5,4},{4,5},{7,6},{6,7},{9,8},{8,9},{11,10... | collective-permute-start | bytes 196616 | tf_op jit(solution)/shard_map/ppermute | solution.py:242
  45.5 7.2 %collective-permute-start.14 = (bf16[128,256]{1,0:T(8,128)(2,1)S(1)}, bf16[128,256]{1,0:T(8,128)(2,1)S(1)}, u32[]{:S(2)}, u32[]{:S(2)}) collective-permute-start(bf16[128,256]{1,0:T(8,128)(2,1)S(1)} %get-tuple-element.35), channel_id=1, source_target_pairs={{31,0},{2,1},{1,2},{4,3},{3,4},{6,5},{5,6},{8,7},{7,8},{10,9},{9,1... | collective-permute-start | bytes 196616 | tf_op jit(solution)/shard_map/ppermute | solution.py:242

commit v6 on v5

--- a/solution.py
+++ b/solution.py
@@ -11,6 +11,7 @@
 F32 = jnp.float32
 BF16 = jnp.bfloat16
 GROUP = 16
+SWAP_ORDER = (2, 3, 1)
 FIRST_FLOPS = 1 << 34
 
 
@@ -195,13 +196,13 @@
     put_rims(near, far, left, right)
 
 
-def finish_kernel(mid, near, far, jac, out, rows, sems):
+def finish_kernel(mid, near, far_even, far_odd, jac, out, rows, sems):
     half = near.shape[1]
     levels = jac.shape[0]
     cut = (levels // 2 + 15) // 16 * 16
     even = even_tile()
-    first = mid[:, :half] + jnp.where(even, far[...], near[...]).astype(F32)
-    last = mid[:, half:] + jnp.where(even, near[...], far[...]).astype(F32)
+    first = mid[:, :half] + jnp.where(even, far_even[...], near[...]).astype(F32)
+    last = mid[:, half:] + jnp.where(even, near[...], far_odd[...]).astype(F32)
     total = jnp.concatenate([first, last], axis=1).astype(BF16)
     copies = []
     for index, part in enumerate((slice(0, cut), slice(cut, levels))):
@@ -228,7 +229,7 @@
 def make_body(n_tm, n_space):
     lanes = n_tm // 2
 
-    def swap(block, y=0, core=0, tile=None):
+    def swap(block, y=0, core=0, tile=None, senders=(0, 1)):
         partner = {
             None: lambda s: s,
             "near": lambda s: s ^ 1,
@@ -238,7 +239,8 @@
         for t in range(n_tm):
             for s in range(n_space):
                 other = (t // 2 ^ y) * 2 + (t % 2 ^ core)
-                route.append((other * n_space + partner(s), t * n_space + s))
+                if partner(s) % 2 in senders:
+                    route.append((other * n_space + partner(s), t * n_space + s))
         return lax.ppermute(block, ("tm", "space"), route)
 
     def steps(
@@ -293,7 +295,7 @@
         (far,) = call(gather_kernel, [((chan, obs), BF16)], wide, other, infos[2], mats[2])
         parts = [None] * lanes
         parts[2] = swap(far, y=2)
-        for j in (1, 3):
+        for j in SWAP_ORDER[1:]:
             (part,) = gather([j])
             parts[j] = swap(part, y=j)
         (parts[0],) = gather([0])
@@ -317,7 +319,8 @@
         all_scaled = [scaled] + [swap(scaled, y=j) for j in range(1, lanes)]
         (acc,) = call(spread_first_kernel, [((2 * chan, width), F32)], info, scaled, mats[0])
         (departures,) = call(turn_kernel, [((obs, chan), F32)], gaps)
-        for j in range(1, lanes - 1):
+        *early, last = SWAP_ORDER
+        for j in early:
             (acc,) = call(
                 spread_next_kernel,
                 [((2 * chan, width), F32)],
@@ -326,7 +329,7 @@
                 all_scaled[j],
                 mats[j],
             )
-        rest = (acc, infos[lanes - 1], all_scaled[lanes - 1], mats[lanes - 1])
+        rest = (acc, infos[last], all_scaled[last], mats[last])
         (give,) = call(spread_give_kernel, [((chan, width), BF16)], *rest)
         give = swap(give, core=1)
         (mine,) = call(spread_keep_kernel, [((chan, width), F32)], *rest)
@@ -338,7 +341,8 @@
             [((levels, 1, cols), F32)],
             mid,
             swap(near, tile="near"),
-            swap(far, tile="far"),
+            swap(far, tile="far", senders=(1,)),
+            swap(far, tile="far", senders=(0,)),
             jacobian,
             out_specs=[HBM],
             scratch=[pltpu.VMEM((levels, 1, cols), F32), pltpu.SemaphoreType.DMA((2,))],

time: 53.7 us -> 57.8 us (1.076)
  the two profiles are of different devices: /device:TPU:1 before, /device:TPU:102 now
where the time goes in v6:
time: 57.8 us; the launch traced here: 57.7 us
  starting transfers between devices  24.7 us (43%)
  waiting for transfers between devices  23.1 us (40%)
  Pallas kernels  6.84 us (12%)
  between operations  1.55 us (3%)
  local copies, waits for them, and re-layouts  1.51 us (3%)
    ppermute x16, starting transfers between devices, swap(): return lax.ppermute(block, ('tm', 'space'), route)  24.7 us
    ppermute x16, waiting for transfers between devices, swap(): return lax.ppermute(block, ('tm', 'space'), route)  23.1 us
    pallas_call x18, Pallas kernels, call(): pl.pallas_call(kernel, out_shape=[jax.ShapeDtypeStruct(shape, dtype) for...  6.84 us
    unnamed x16, local copies, waits for them, and re-layouts  1.51 us
  transfers between devices with their start and end apart: 16, of which 9 were waited for; matrix products, arithmetic and copies ran while one was open for 0% of the time, Pallas kernels for 9%

profile of v6, /device:TPU:102, one launch (start us, length us, event | category | flops | bytes accessed | tf_op | source)
XLA Modules:
  0.0 57.7 jit_solution(6458790204807675130)
XLA Ops:
  0.6 0.0 copy-start.2
  0.6 0.0 copy-start.1
  0.7 0.0 copy-start.4
  0.7 0.0 copy-start.5
  0.7 0.0 copy-start.6
  0.7 0.0 copy-start.3
  0.7 0.8 %copy-done.2 = bf16[1,512,137]{1,2,0:T(8,128)(2,1)S(1)} copy-done((bf16[1,512,137]{1,2,0:T(8,128)(2,1)S(1)}, bf16[1,512,137]{1,2,0:T(8,128)(2,1)}, u32[]{:S(2)}) %copy-start.2) | copy-done | bytes 140312
  1.5 0.0 copy-done.1
  1.5 0.0 copy-done.4
  1.5 0.0 copy-done.5
  1.6 0.0 copy-done.6
  1.6 0.0 copy-done.3
  1.6 0.2 shard_map.105
  1.8 0.9 %collective-permute-start = (bf16[128,256]{1,0:T(8,128)(2,1)S(1)}, bf16[128,256]{1,0:T(8,128)(2,1)S(1)}, u32[]{:S(2)}, u32[]{:S(2)}) collective-permute-start(bf16[128,256]{1,0:T(8,128)(2,1)S(1)} %get-tuple-element.20), channel_id=1, source_target_pairs={{1,0},{0,1},{3,2},{2,3},{5,4},{4,5},{7,6},{6,7},{9,8},{8,9},{11,10... | collective-permute-start | bytes 196616 | tf_op jit(solution)/shard_map/ppermute | solution.py:244
  2.7 3.7 %collective-permute-start.1 = (bf16[128,256]{1,0:T(8,128)(2,1)S(1)}, bf16[128,256]{1,0:T(8,128)(2,1)S(1)}, u32[]{:S(2)}, u32[]{:S(2)}) collective-permute-start(bf16[128,256]{1,0:T(8,128)(2,1)S(1)} %get-tuple-element.21), channel_id=1, source_target_pairs={{31,0},{2,1},{1,2},{4,3},{3,4},{6,5},{5,6},{8,7},{7,8},{10,9},{9,1... | collective-permute-start | bytes 196616 | tf_op jit(solution)/shard_map/ppermute | solution.py:244
  6.4 0.0 collective-permute-done.near
  6.4 3.9 %collective-permute-done.1.far = bf16[128,256]{1,0:T(8,128)(2,1)S(1)} collective-permute-done((bf16[128,256]{1,0:T(8,128)(2,1)S(1)}, bf16[128,256]{1,0:T(8,128)(2,1)S(1)}, u32[]{:S(2)}, u32[]{:S(2)}) %collective-permute-start.1) | collective-permute-done | bytes 65568 | tf_op jit(solution)/shard_map/ppermute | solution.py:244
  10.3 0.1 collective-permute-start.2
  10.4 3.3 %collective-permute-start.5 = (f32[16,512]{1,0:T(8,128)S(1)}, f32[16,512]{1,0:T(8,128)S(1)}, u32[]{:S(2)}, u32[]{:S(2)}) collective-permute-start(f32[16,512]{1,0:T(8,128)S(1)} %get-tuple-element.22.refs_0_.info), channel_id=1, source_target_pairs={{128,0},{129,1},{130,2},{131,3},{132,4},{133,5},{134,6},{135,7},{1... | collective-permute-start | bytes 98312 | tf_op jit(solution)/shard_map/ppermute | solution.py:244
  13.7 0.7 %collective-permute-start.3 = (f32[16,512]{1,0:T(8,128)S(1)}, f32[16,512]{1,0:T(8,128)S(1)}, u32[]{:S(2)}, u32[]{:S(2)}) collective-permute-start(f32[16,512]{1,0:T(8,128)S(1)} %get-tuple-element.22.refs_0_.info), channel_id=1, source_target_pairs={{64,0},{65,1},{66,2},{67,3},{68,4},{69,5},{70,6},{71,7},{72,8},{73... | collective-permute-start | bytes 98312 | tf_op jit(solution)/shard_map/ppermute | solution.py:244
  14.4 0.4 collective-permute-start.7
  14.8 1.2 %collective-permute-done.5.info = f32[16,512]{1,0:T(8,128)S(1)} collective-permute-done((f32[16,512]{1,0:T(8,128)S(1)}, f32[16,512]{1,0:T(8,128)S(1)}, u32[]{:S(2)}, u32[]{:S(2)}) %collective-permute-start.5) | collective-permute-done | bytes 32800 | tf_op jit(solution)/shard_map/ppermute | solution.py:244
  16.0 0.2 shard_map.109.mat
  16.1 1.5 %collective-permute-done.3.refs_0_.info = f32[16,512]{1,0:T(8,128)S(1)} collective-permute-done((f32[16,512]{1,0:T(8,128)S(1)}, f32[16,512]{1,0:T(8,128)S(1)}, u32[]{:S(2)}, u32[]{:S(2)}) %collective-permute-start.3) | collective-permute-done | bytes 32800 | tf_op jit(solution)/shard_map/ppermute | solution.py:244
  17.6 0.0 collective-permute-done.2.other
  17.6 0.5 shard_map.108
  18.1 0.8 %collective-permute-start.4 = (bf16[128,512]{1,0:T(8,128)(2,1)S(1)}, bf16[128,512]{1,0:T(8,128)(2,1)S(1)}, u32[]{:S(2)}, u32[]{:S(2)}) collective-permute-start(bf16[128,512]{1,0:T(8,128)(2,1)S(1)} %get-tuple-element.24), channel_id=1, source_target_pairs={{64,0},{65,1},{66,2},{67,3},{68,4},{69,5},{70,6},{71,7},{72,8},{73... | collective-permute-start | bytes 393224 | tf_op jit(solution)/shard_map/ppermute | solution.py:244
  18.9 0.4 shard_map.110
  19.3 0.0 copy-start
  19.4 2.4 %collective-permute-start.6 = (bf16[128,512]{1,0:T(8,128)(2,1)S(1)}, bf16[128,512]{1,0:T(8,128)(2,1)S(1)}, u32[]{:S(2)}, u32[]{:S(2)}) collective-permute-start(bf16[128,512]{1,0:T(8,128)(2,1)S(1)} %shard_map.110), channel_id=1, source_target_pairs={{128,0},{129,1},{130,2},{131,3},{132,4},{133,5},{134,6},{135,7},{1... | collective-permute-start | bytes 393224 | tf_op jit(solution)/shard_map/ppermute | solution.py:244
  21.8 0.0 collective-permute-done.7.refs_0_.info
  21.8 0.5 shard_map.111
  22.2 1.8 %collective-permute-start.8 = (bf16[128,512]{1,0:T(8,128)(2,1)S(1)}, bf16[128,512]{1,0:T(8,128)(2,1)S(1)}, u32[]{:S(2)}, u32[]{:S(2)}) collective-permute-start(bf16[128,512]{1,0:T(8,128)(2,1)S(1)} %get-tuple-element.25), channel_id=1, source_target_pairs={{192,0},{193,1},{194,2},{195,3},{196,4},{197,5},{198,6},{199,7},{2... | collective-permute-start | bytes 393224 | tf_op jit(solution)/shard_map/ppermute | solution.py:244
  24.7 0.0 copy-start.7
  24.7 0.0 copy-done
  24.7 0.6 %copy-done.7 = f32[128]{0:T(128)S(1)} copy-done((f32[128]{0:T(128)S(1)}, f32[128]{0:T(128)}, u32[]{:S(2)}) %copy-start.7) | copy-done | bytes 536
  25.4 0.3 shard_map.112
  25.6 0.5 shard_map.107
  26.1 0.0 collective-permute-done.4.refs_1_
  26.1 0.9 %collective-permute-done.6.refs_2_ = bf16[128,512]{1,0:T(8,128)(2,1)S(1)} collective-permute-done((bf16[128,512]{1,0:T(8,128)(2,1)S(1)}, bf16[128,512]{1,0:T(8,128)(2,1)S(1)}, u32[]{:S(2)}, u32[]{:S(2)}) %collective-permute-start.6) | collective-permute-done | bytes 131104 | tf_op jit(solution)/shard_map/ppermute | solution.py:244
  27.0 2.3 %collective-permute-done.8.refs_3_ = bf16[128,512]{1,0:T(8,128)(2,1)S(1)} collective-permute-done((bf16[128,512]{1,0:T(8,128)(2,1)S(1)}, bf16[128,512]{1,0:T(8,128)(2,1)S(1)}, u32[]{:S(2)}, u32[]{:S(2)}) %collective-permute-start.8) | collective-permute-done | bytes 131104 | tf_op jit(solution)/shard_map/ppermute | solution.py:244
  29.4 0.1 shard_map.113
  29.5 1.3 %collective-permute-start.9 = (bf16[128,512]{1,0:T(8,128)(2,1)S(1)}, bf16[128,512]{1,0:T(8,128)(2,1)S(1)}, u32[]{:S(2)}, u32[]{:S(2)}) collective-permute-start(bf16[128,512]{1,0:T(8,128)(2,1)S(1)} %get-tuple-element.29.scaled), channel_id=1, source_target_pairs={{128,0},{129,1},{130,2},{131,3},{132,4},{133,5},{134,6},{135,7},{1... | collective-permute-start | bytes 393224 | tf_op jit(solution)/shard_map/ppermute | solution.py:244
  30.7 1.4 %collective-permute-start.10 = (bf16[128,512]{1,0:T(8,128)(2,1)S(1)}, bf16[128,512]{1,0:T(8,128)(2,1)S(1)}, u32[]{:S(2)}, u32[]{:S(2)}) collective-permute-start(bf16[128,512]{1,0:T(8,128)(2,1)S(1)} %get-tuple-element.29.scaled), channel_id=1, source_target_pairs={{192,0},{193,1},{194,2},{195,3},{196,4},{197,5},{198,6},{199,7},{2... | collective-permute-start | bytes 393224 | tf_op jit(solution)/shard_map/ppermute | solution.py:244
  32.2 0.9 %collective-permute-start.11 = (bf16[128,512]{1,0:T(8,128)(2,1)S(1)}, bf16[128,512]{1,0:T(8,128)(2,1)S(1)}, u32[]{:S(2)}, u32[]{:S(2)}) collective-permute-start(bf16[128,512]{1,0:T(8,128)(2,1)S(1)} %get-tuple-element.29.scaled), channel_id=1, source_target_pairs={{64,0},{65,1},{66,2},{67,3},{68,4},{69,5},{70,6},{71,7},{72,8},{73... | collective-permute-start | bytes 393224 | tf_op jit(solution)/shard_map/ppermute | solution.py:244
  33.1 0.5 shard_map.115.before
  33.5 3.6 %collective-permute-done.9.scaled = bf16[128,512]{1,0:T(8,128)(2,1)S(1)} collective-permute-done((bf16[128,512]{1,0:T(8,128)(2,1)S(1)}, bf16[128,512]{1,0:T(8,128)(2,1)S(1)}, u32[]{:S(2)}, u32[]{:S(2)}) %collective-permute-start.9) | collective-permute-done | bytes 131104 | tf_op jit(solution)/shard_map/ppermute | solution.py:244
  37.1 0.5 shard_map.116.before
  37.6 1.3 %collective-permute-done.10.scaled = bf16[128,512]{1,0:T(8,128)(2,1)S(1)} collective-permute-done((bf16[128,512]{1,0:T(8,128)(2,1)S(1)}, bf16[128,512]{1,0:T(8,128)(2,1)S(1)}, u32[]{:S(2)}, u32[]{:S(2)}) %collective-permute-start.10) | collective-permute-done | bytes 131104 | tf_op jit(solution)/shard_map/ppermute | solution.py:244
  38.9 0.5 shard_map.117.before
  39.3 0.0 collective-permute-done.11.scaled
  39.4 0.5 shard_map.119
  39.8 0.1 collective-permute-start.12
  39.9 0.5 shard_map.118.own
  40.4 1.0 %collective-permute-done.12.got = bf16[128,1024]{1,0:T(8,128)(2,1)S(1)} collective-permute-done((bf16[128,1024]{1,0:T(8,128)(2,1)S(1)}, bf16[128,1024]{1,0:T(8,128)(2,1)S(1)}, u32[]{:S(2)}, u32[]{:S(2)}) %collective-permute-start.12) | collective-permute-done | bytes 262176 | tf_op jit(solution)/shard_map/ppermute | solution.py:244
  41.5 0.1 shard_map.120
  41.5 0.1 collective-permute-start.13
  41.6 5.6 %collective-permute-start.14 = (bf16[128,256]{1,0:T(8,128)(2,1)S(1)}, bf16[128,256]{1,0:T(8,128)(2,1)S(1)}, u32[]{:S(2)}, u32[]{:S(2)}) collective-permute-start(bf16[128,256]{1,0:T(8,128)(2,1)S(1)} %get-tuple-element.35), channel_id=1, source_target_pairs={{31,0},{1,2},{3,4},{5,6},{7,8},{9,10},{11,12},{13,14},{15,16},{17,... | collective-permute-start | bytes 196616 | tf_op jit(solution)/shard_map/ppermute | solution.py:244
  47.3 1.3 %collective-permute-start.15 = (bf16[128,256]{1,0:T(8,128)(2,1)S(1)}, bf16[128,256]{1,0:T(8,128)(2,1)S(1)}, u32[]{:S(2)}, u32[]{:S(2)}) collective-permute-start(bf16[128,256]{1,0:T(8,128)(2,1)S(1)} %get-tuple-element.35), channel_id=1, source_target_pairs={{2,1},{4,3},{6,5},{8,7},{10,9},{12,11},{14,13},{16,15},{18,17},{20... | collective-permute-start | bytes 196616 | tf_op jit(solution)/shard_map/ppermute | solution.py:244
  48.6 0.8 %shard_map.114 = f32[512,128]{1,0:T(8,128)} custom-call(f32[128,512]{1,0:T(8,128)S(1)} %get-tuple-element.28.source), custom_call_target="tpu_custom_call" | custom-call | flops 1048576 | bytes 1048576 | tf_op jit(solution)/shard_map/pallas_call | solution.py:218
  49.4 0.0 collective-permute-done.13.near
  49.4 0.0 collective-permute-done.14.far_even
  49.4 7.3 %collective-permute-done.15.far_odd = bf16[128,256]{1,0:T(8,128)(2,1)S(1)} collective-permute-done((bf16[128,256]{1,0:T(8,128)(2,1)S(1)}, bf16[128,256]{1,0:T(8,128)(2,1)S(1)}, u32[]{:S(2)}, u32[]{:S(2)}) %collective-permute-start.15) | collective-permute-done | bytes 65568 | tf_op jit(solution)/shard_map/ppermute | solution.py:244
  56.8 0.9 %shard_map.121 = f32[137,1,512]{2,1,0:T(1,128)} custom-call(f32[128,512]{1,0:T(8,128)S(1)} %get-tuple-element.33.mid, bf16[128,256]{1,0:T(8,128)(2,1)S(1)} %collective-permute-done.13.near, bf16[128,256]{1,0:T(8,128)(2,1)S(1)} %collective-permute-done.14.far_even, bf16[128,256]{1,0:T(8,128)(2,1)S(1)} %collective-permute-done.15.far_odd, ...), custom_call_target="tpu_custom_call" | custom-call | flops 1048576 | bytes 1048576 | tf_op jit(solution)/shard_map/pallas_call | solution.py:218
  (2 shorter events, 0.0 us)
Async XLA Ops:
  0.6 0.9 %copy-start.2 = (bf16[1,512,137]{1,2,0:T(8,128)(2,1)S(1)}, bf16[1,512,137]{1,2,0:T(8,128)(2,1)}, u32[]{:S(2)}) copy-start(bf16[1,512,137]{1,2,0:T(8,128)(2,1)} %param.9) | copy-start | bytes 420868
  0.6 0.9 %copy-start.1 = (bf16[137,128]{1,0:T(8,128)(2,1)S(1)}, bf16[137,128]{1,0:T(8,128)(2,1)}, u32[]{:S(2)}) copy-start(bf16[137,128]{1,0:T(8,128)(2,1)} %jac.3) | copy-start | bytes 105220
  0.7 0.9 %copy-start.4 = (s32[512]{0:T(512)S(1)}, s32[512]{0:T(512)}, u32[]{:S(2)}) copy-start(s32[512]{0:T(512)} %param.10) | copy-start | bytes 6148
  0.7 0.9 %copy-start.5 = (s32[512]{0:T(512)S(1)}, s32[512]{0:T(512)}, u32[]{:S(2)}) copy-start(s32[512]{0:T(512)} %param.12) | copy-start | bytes 6148
  0.7 0.9 %copy-start.6 = (f32[512]{0:T(512)S(1)}, f32[512]{0:T(512)}, u32[]{:S(2)}) copy-start(f32[512]{0:T(512)} %param.13) | copy-start | bytes 6148
  0.7 0.9 %copy-start.3 = (bf16[512,8]{0,1:T(8,128)(2,1)S(1)}, bf16[512,8]{0,1:T(8,128)(2,1)}, u32[]{:S(2)}) copy-start(bf16[512,8]{0,1:T(8,128)(2,1)} %param.11) | copy-start | bytes 24580
  1.8 4.6 %collective-permute-start = (bf16[128,256]{1,0:T(8,128)(2,1)S(1)}, bf16[128,256]{1,0:T(8,128)(2,1)S(1)}, u32[]{:S(2)}, u32[]{:S(2)}) collective-permute-start(bf16[128,256]{1,0:T(8,128)(2,1)S(1)} %get-tuple-element.20), channel_id=1, source_target_pairs={{1,0},{0,1},{3,2},{2,3},{5,4},{4,5},{7,6},{6,7},{9,8},{8,9},{11,10... | collective-permute-start | bytes 196616 | tf_op jit(solution)/shard_map/ppermute | solution.py:244
  2.7 7.6 %collective-permute-start.1 = (bf16[128,256]{1,0:T(8,128)(2,1)S(1)}, bf16[128,256]{1,0:T(8,128)(2,1)S(1)}, u32[]{:S(2)}, u32[]{:S(2)}) collective-permute-start(bf16[128,256]{1,0:T(8,128)(2,1)S(1)} %get-tuple-element.21), channel_id=1, source_target_pairs={{31,0},{2,1},{1,2},{4,3},{3,4},{6,5},{5,6},{8,7},{7,8},{10,9},{9,1... | collective-permute-start | bytes 196616 | tf_op jit(solution)/shard_map/ppermute | solution.py:244
  10.3 7.3 %collective-permute-start.2 = (bf16[128,1024]{1,0:T(8,128)(2,1)S(1)}, bf16[128,1024]{1,0:T(8,128)(2,1)S(1)}, u32[]{:S(2)}, u32[]{:S(2)}) collective-permute-start(bf16[128,1024]{1,0:T(8,128)(2,1)S(1)} %shard_map.106.mine), channel_id=1, source_target_pairs={{32,0},{33,1},{34,2},{35,3},{36,4},{37,5},{38,6},{39,7},{40,8},{41... | collective-permute-start | bytes 786440 | tf_op jit(solution)/shard_map/ppermute | solution.py:244
  10.4 5.5 %collective-permute-start.5 = (f32[16,512]{1,0:T(8,128)S(1)}, f32[16,512]{1,0:T(8,128)S(1)}, u32[]{:S(2)}, u32[]{:S(2)}) collective-permute-start(f32[16,512]{1,0:T(8,128)S(1)} %get-tuple-element.22.refs_0_.info), channel_id=1, source_target_pairs={{128,0},{129,1},{130,2},{131,3},{132,4},{133,5},{134,6},{135,7},{1... | collective-permute-start | bytes 98312 | tf_op jit(solution)/shard_map/ppermute | solution.py:244
  13.7 3.9 %collective-permute-start.3 = (f32[16,512]{1,0:T(8,128)S(1)}, f32[16,512]{1,0:T(8,128)S(1)}, u32[]{:S(2)}, u32[]{:S(2)}) collective-permute-start(f32[16,512]{1,0:T(8,128)S(1)} %get-tuple-element.22.refs_0_.info), channel_id=1, source_target_pairs={{64,0},{65,1},{66,2},{67,3},{68,4},{69,5},{70,6},{71,7},{72,8},{73... | collective-permute-start | bytes 98312 | tf_op jit(solution)/shard_map/ppermute | solution.py:244
  14.4 7.3 %collective-permute-start.7 = (f32[16,512]{1,0:T(8,128)S(1)}, f32[16,512]{1,0:T(8,128)S(1)}, u32[]{:S(2)}, u32[]{:S(2)}) collective-permute-start(f32[16,512]{1,0:T(8,128)S(1)} %get-tuple-element.22.refs_0_.info), channel_id=1, source_target_pairs={{192,0},{193,1},{194,2},{195,3},{196,4},{197,5},{198,6},{199,7},{2... | collective-permute-start | bytes 98312 | tf_op jit(solution)/shard_map/ppermute | solution.py:244
  18.1 8.0 %collective-permute-start.4 = (bf16[128,512]{1,0:T(8,128)(2,1)S(1)}, bf16[128,512]{1,0:T(8,128)(2,1)S(1)}, u32[]{:S(2)}, u32[]{:S(2)}) collective-permute-start(bf16[128,512]{1,0:T(8,128)(2,1)S(1)} %get-tuple-element.24), channel_id=1, source_target_pairs={{64,0},{65,1},{66,2},{67,3},{68,4},{69,5},{70,6},{71,7},{72,8},{73... | collective-permute-start | bytes 393224 | tf_op jit(solution)/shard_map/ppermute | solution.py:244
  19.3 5.4 %copy-start = (f32[512,128]{1,0:T(8,128)S(1)}, f32[512,128]{1,0:T(8,128)}, u32[]{:S(2)}) copy-start(f32[512,128]{1,0:T(8,128)} %source.1) | copy-start | bytes 786436
  19.4 7.7 %collective-permute-start.6 = (bf16[128,512]{1,0:T(8,128)(2,1)S(1)}, bf16[128,512]{1,0:T(8,128)(2,1)S(1)}, u32[]{:S(2)}, u32[]{:S(2)}) collective-permute-start(bf16[128,512]{1,0:T(8,128)(2,1)S(1)} %shard_map.110), channel_id=1, source_target_pairs={{128,0},{129,1},{130,2},{131,3},{132,4},{133,5},{134,6},{135,7},{1... | collective-permute-start | bytes 393224 | tf_op jit(solution)/shard_map/ppermute | solution.py:244
  22.2 7.1 %collective-permute-start.8 = (bf16[128,512]{1,0:T(8,128)(2,1)S(1)}, bf16[128,512]{1,0:T(8,128)(2,1)S(1)}, u32[]{:S(2)}, u32[]{:S(2)}) collective-permute-start(bf16[128,512]{1,0:T(8,128)(2,1)S(1)} %get-tuple-element.25), channel_id=1, source_target_pairs={{192,0},{193,1},{194,2},{195,3},{196,4},{197,5},{198,6},{199,7},{2... | collective-permute-start | bytes 393224 | tf_op jit(solution)/shard_map/ppermute | solution.py:244
  24.7 0.7 %copy-start.7 = (f32[128]{0:T(128)S(1)}, f32[128]{0:T(128)}, u32[]{:S(2)}) copy-start(f32[128]{0:T(128)} %param.17) | copy-start | bytes 1540
  29.5 7.6 %collective-permute-start.9 = (bf16[128,512]{1,0:T(8,128)(2,1)S(1)}, bf16[128,512]{1,0:T(8,128)(2,1)S(1)}, u32[]{:S(2)}, u32[]{:S(2)}) collective-permute-start(bf16[128,512]{1,0:T(8,128)(2,1)S(1)} %get-tuple-element.29.scaled), channel_id=1, source_target_pairs={{128,0},{129,1},{130,2},{131,3},{132,4},{133,5},{134,6},{135,7},{1... | collective-permute-start | bytes 393224 | tf_op jit(solution)/shard_map/ppermute | solution.py:244
  30.7 8.1 %collective-permute-start.10 = (bf16[128,512]{1,0:T(8,128)(2,1)S(1)}, bf16[128,512]{1,0:T(8,128)(2,1)S(1)}, u32[]{:S(2)}, u32[]{:S(2)}) collective-permute-start(bf16[128,512]{1,0:T(8,128)(2,1)S(1)} %get-tuple-element.29.scaled), channel_id=1, source_target_pairs={{192,0},{193,1},{194,2},{195,3},{196,4},{197,5},{198,6},{199,7},{2... | collective-permute-start | bytes 393224 | tf_op jit(solution)/shard_map/ppermute | solution.py:244
  32.2 7.2 %collective-permute-start.11 = (bf16[128,512]{1,0:T(8,128)(2,1)S(1)}, bf16[128,512]{1,0:T(8,128)(2,1)S(1)}, u32[]{:S(2)}, u32[]{:S(2)}) collective-permute-start(bf16[128,512]{1,0:T(8,128)(2,1)S(1)} %get-tuple-element.29.scaled), channel_id=1, source_target_pairs={{64,0},{65,1},{66,2},{67,3},{68,4},{69,5},{70,6},{71,7},{72,8},{73... | collective-permute-start | bytes 393224 | tf_op jit(solution)/shard_map/ppermute | solution.py:244
  39.8 1.6 %collective-permute-start.12 = (bf16[128,1024]{1,0:T(8,128)(2,1)S(1)}, bf16[128,1024]{1,0:T(8,128)(2,1)S(1)}, u32[]{:S(2)}, u32[]{:S(2)}) collective-permute-start(bf16[128,1024]{1,0:T(8,128)(2,1)S(1)} %shard_map.119), channel_id=1, source_target_pairs={{32,0},{33,1},{34,2},{35,3},{36,4},{37,5},{38,6},{39,7},{40,8},{41... | collective-permute-start | bytes 786440 | tf_op jit(solution)/shard_map/ppermute | solution.py:244
  41.5 7.9 %collective-permute-start.13 = (bf16[128,256]{1,0:T(8,128)(2,1)S(1)}, bf16[128,256]{1,0:T(8,128)(2,1)S(1)}, u32[]{:S(2)}, u32[]{:S(2)}) collective-permute-start(bf16[128,256]{1,0:T(8,128)(2,1)S(1)} %get-tuple-element.34), channel_id=1, source_target_pairs={{1,0},{0,1},{3,2},{2,3},{5,4},{4,5},{7,6},{6,7},{9,8},{8,9},{11,10... | collective-permute-start | bytes 196616 | tf_op jit(solution)/shard_map/ppermute | solution.py:244
  41.6 7.8 %collective-permute-start.14 = (bf16[128,256]{1,0:T(8,128)(2,1)S(1)}, bf16[128,256]{1,0:T(8,128)(2,1)S(1)}, u32[]{:S(2)}, u32[]{:S(2)}) collective-permute-start(bf16[128,256]{1,0:T(8,128)(2,1)S(1)} %get-tuple-element.35), channel_id=1, source_target_pairs={{31,0},{1,2},{3,4},{5,6},{7,8},{9,10},{11,12},{13,14},{15,16},{17,... | collective-permute-start | bytes 196616 | tf_op jit(solution)/shard_map/ppermute | solution.py:244
  47.3 9.5 %collective-permute-start.15 = (bf16[128,256]{1,0:T(8,128)(2,1)S(1)}, bf16[128,256]{1,0:T(8,128)(2,1)S(1)}, u32[]{:S(2)}, u32[]{:S(2)}) collective-permute-start(bf16[128,256]{1,0:T(8,128)(2,1)S(1)} %get-tuple-element.35), channel_id=1, source_target_pairs={{2,1},{4,3},{6,5},{8,7},{10,9},{12,11},{14,13},{16,15},{18,17},{20... | collective-permute-start | bytes 196616 | tf_op jit(solution)/shard_map/ppermute | solution.py:244

commit v7 on v5

--- a/solution.py
+++ b/solution.py
@@ -11,6 +11,8 @@
 F32 = jnp.float32
 BF16 = jnp.bfloat16
 GROUP = 16
+SWAP_ORDER = (2, 3, 1)
+LAND_ORDER = (2, 1, 3)
 FIRST_FLOPS = 1 << 34
 
 
@@ -293,7 +295,7 @@
         (far,) = call(gather_kernel, [((chan, obs), BF16)], wide, other, infos[2], mats[2])
         parts = [None] * lanes
         parts[2] = swap(far, y=2)
-        for j in (1, 3):
+        for j in SWAP_ORDER[1:]:
             (part,) = gather([j])
             parts[j] = swap(part, y=j)
         (parts[0],) = gather([0])
@@ -317,7 +319,8 @@
         all_scaled = [scaled] + [swap(scaled, y=j) for j in range(1, lanes)]
         (acc,) = call(spread_first_kernel, [((2 * chan, width), F32)], info, scaled, mats[0])
         (departures,) = call(turn_kernel, [((obs, chan), F32)], gaps)
-        for j in range(1, lanes - 1):
+        *early, last = LAND_ORDER
+        for j in early:
             (acc,) = call(
                 spread_next_kernel,
                 [((2 * chan, width), F32)],
@@ -326,7 +329,7 @@
                 all_scaled[j],
                 mats[j],
             )
-        rest = (acc, infos[lanes - 1], all_scaled[lanes - 1], mats[lanes - 1])
+        rest = (acc, infos[last], all_scaled[last], mats[last])
         (give,) = call(spread_give_kernel, [((chan, width), BF16)], *rest)
         give = swap(give, core=1)
         (mine,) = call(spread_keep_kernel, [((chan, width), F32)], *rest)

time: 53.7 us -> 53.2 us (level)
  starting transfers between devices: 29.7 us -> 28.9 us
    ppermute x15, starting transfers between devices: 29.7 us -> 28.9 us  [swap(): return lax.ppermute(block, ('tm', 'space'), route)]
where the time goes in v7:
time: 53.2 us; the launch traced here: 53.1 us
  starting transfers between devices  28.9 us (54%)
  waiting for transfers between devices  14.4 us (27%)
  Pallas kernels  6.84 us (13%)
  between operations  1.52 us (3%)
  local copies, waits for them, and re-layouts  1.51 us (3%)
    ppermute x15, starting transfers between devices, swap(): return lax.ppermute(block, ('tm', 'space'), route)  28.9 us
    ppermute x15, waiting for transfers between devices, swap(): return lax.ppermute(block, ('tm', 'space'), route)  14.4 us
    pallas_call x18, Pallas kernels, call(): pl.pallas_call(kernel, out_shape=[jax.ShapeDtypeStruct(shape, dtype) for...  6.84 us
    unnamed x16, local copies, waits for them, and re-layouts  1.51 us
  transfers between devices with their start and end apart: 15, of which 9 were waited for; matrix products, arithmetic and copies ran while one was open for 0% of the time, Pallas kernels for 9%

profile of v7, /device:TPU:1, one launch (start us, length us, event | category | flops | bytes accessed | tf_op | source)
XLA Modules:
  0.0 53.1 jit_solution(3557695339319442654)
XLA Ops:
  0.6 0.0 copy-start.2
  0.6 0.0 copy-start.1
  0.7 0.0 copy-start.4
  0.7 0.0 copy-start.5
  0.7 0.0 copy-start.6
  0.7 0.0 copy-start.3
  0.7 0.8 %copy-done.2 = bf16[1,512,137]{1,2,0:T(8,128)(2,1)S(1)} copy-done((bf16[1,512,137]{1,2,0:T(8,128)(2,1)S(1)}, bf16[1,512,137]{1,2,0:T(8,128)(2,1)}, u32[]{:S(2)}) %copy-start.2) | copy-done | bytes 140312
  1.5 0.0 copy-done.1
  1.5 0.0 copy-done.4
  1.5 0.0 copy-done.5
  1.6 0.0 copy-done.6
  1.6 0.0 copy-done.3
  1.6 0.2 shard_map.105
  1.8 2.1 %collective-permute-start = (bf16[128,256]{1,0:T(8,128)(2,1)S(1)}, bf16[128,256]{1,0:T(8,128)(2,1)S(1)}, u32[]{:S(2)}, u32[]{:S(2)}) collective-permute-start(bf16[128,256]{1,0:T(8,128)(2,1)S(1)} %get-tuple-element.20), channel_id=1, source_target_pairs={{1,0},{0,1},{3,2},{2,3},{5,4},{4,5},{7,6},{6,7},{9,8},{8,9},{11,10... | collective-permute-start | bytes 196616 | tf_op jit(solution)/shard_map/ppermute | solution.py:244
  3.9 7.1 %collective-permute-start.1 = (bf16[128,256]{1,0:T(8,128)(2,1)S(1)}, bf16[128,256]{1,0:T(8,128)(2,1)S(1)}, u32[]{:S(2)}, u32[]{:S(2)}) collective-permute-start(bf16[128,256]{1,0:T(8,128)(2,1)S(1)} %get-tuple-element.21), channel_id=1, source_target_pairs={{31,0},{2,1},{1,2},{4,3},{3,4},{6,5},{5,6},{8,7},{7,8},{10,9},{9,1... | collective-permute-start | bytes 196616 | tf_op jit(solution)/shard_map/ppermute | solution.py:244
  11.0 0.0 collective-permute-done.near
  11.0 1.6 %collective-permute-done.1.far = bf16[128,256]{1,0:T(8,128)(2,1)S(1)} collective-permute-done((bf16[128,256]{1,0:T(8,128)(2,1)S(1)}, bf16[128,256]{1,0:T(8,128)(2,1)S(1)}, u32[]{:S(2)}, u32[]{:S(2)}) %collective-permute-start.1) | collective-permute-done | bytes 65568 | tf_op jit(solution)/shard_map/ppermute | solution.py:244
  12.7 1.9 %collective-permute-start.2 = (bf16[128,1024]{1,0:T(8,128)(2,1)S(1)}, bf16[128,1024]{1,0:T(8,128)(2,1)S(1)}, u32[]{:S(2)}, u32[]{:S(2)}) collective-permute-start(bf16[128,1024]{1,0:T(8,128)(2,1)S(1)} %shard_map.106.mine), channel_id=1, source_target_pairs={{32,0},{33,1},{34,2},{35,3},{36,4},{37,5},{38,6},{39,7},{40,8},{41... | collective-permute-start | bytes 786440 | tf_op jit(solution)/shard_map/ppermute | solution.py:244
  14.6 2.9 %collective-permute-start.5 = (f32[16,512]{1,0:T(8,128)S(1)}, f32[16,512]{1,0:T(8,128)S(1)}, u32[]{:S(2)}, u32[]{:S(2)}) collective-permute-start(f32[16,512]{1,0:T(8,128)S(1)} %get-tuple-element.22.refs_0_.info), channel_id=1, source_target_pairs={{128,0},{129,1},{130,2},{131,3},{132,4},{133,5},{134,6},{135,7},{1... | collective-permute-start | bytes 98312 | tf_op jit(solution)/shard_map/ppermute | solution.py:244
  17.6 0.4 collective-permute-start.3
  17.9 0.4 collective-permute-start.7
  18.3 0.6 %collective-permute-done.5.info = f32[16,512]{1,0:T(8,128)S(1)} collective-permute-done((f32[16,512]{1,0:T(8,128)S(1)}, f32[16,512]{1,0:T(8,128)S(1)}, u32[]{:S(2)}, u32[]{:S(2)}) %collective-permute-start.5) | collective-permute-done | bytes 32800 | tf_op jit(solution)/shard_map/ppermute | solution.py:244
  18.9 0.2 shard_map.109.mat
  19.1 1.3 %collective-permute-done.3.refs_0_.info = f32[16,512]{1,0:T(8,128)S(1)} collective-permute-done((f32[16,512]{1,0:T(8,128)S(1)}, f32[16,512]{1,0:T(8,128)S(1)}, u32[]{:S(2)}, u32[]{:S(2)}) %collective-permute-start.3) | collective-permute-done | bytes 32800 | tf_op jit(solution)/shard_map/ppermute | solution.py:244
  20.3 0.0 collective-permute-done.2.other
  20.3 0.5 shard_map.108
  20.8 1.0 %collective-permute-start.4 = (bf16[128,512]{1,0:T(8,128)(2,1)S(1)}, bf16[128,512]{1,0:T(8,128)(2,1)S(1)}, u32[]{:S(2)}, u32[]{:S(2)}) collective-permute-start(bf16[128,512]{1,0:T(8,128)(2,1)S(1)} %get-tuple-element.24), channel_id=1, source_target_pairs={{64,0},{65,1},{66,2},{67,3},{68,4},{69,5},{70,6},{71,7},{72,8},{73... | collective-permute-start | bytes 393224 | tf_op jit(solution)/shard_map/ppermute | solution.py:244
  21.8 0.4 shard_map.110
  22.2 0.0 copy-start
  22.2 1.9 %collective-permute-start.6 = (bf16[128,512]{1,0:T(8,128)(2,1)S(1)}, bf16[128,512]{1,0:T(8,128)(2,1)S(1)}, u32[]{:S(2)}, u32[]{:S(2)}) collective-permute-start(bf16[128,512]{1,0:T(8,128)(2,1)S(1)} %shard_map.110), channel_id=1, source_target_pairs={{128,0},{129,1},{130,2},{131,3},{132,4},{133,5},{134,6},{135,7},{1... | collective-permute-start | bytes 393224 | tf_op jit(solution)/shard_map/ppermute | solution.py:244
  24.1 0.0 collective-permute-done.7.refs_0_.info
  24.1 0.5 shard_map.111
  24.6 1.3 %collective-permute-start.8 = (bf16[128,512]{1,0:T(8,128)(2,1)S(1)}, bf16[128,512]{1,0:T(8,128)(2,1)S(1)}, u32[]{:S(2)}, u32[]{:S(2)}) collective-permute-start(bf16[128,512]{1,0:T(8,128)(2,1)S(1)} %get-tuple-element.25), channel_id=1, source_target_pairs={{192,0},{193,1},{194,2},{195,3},{196,4},{197,5},{198,6},{199,7},{2... | collective-permute-start | bytes 393224 | tf_op jit(solution)/shard_map/ppermute | solution.py:244
  26.5 0.0 copy-start.7
  26.5 0.0 copy-done
  26.6 0.6 %copy-done.7 = f32[128]{0:T(128)S(1)} copy-done((f32[128]{0:T(128)S(1)}, f32[128]{0:T(128)}, u32[]{:S(2)}) %copy-start.7) | copy-done | bytes 536
  27.2 0.3 shard_map.112
  27.5 0.5 shard_map.107
  28.0 0.0 collective-permute-done.4.refs_1_
  28.0 1.1 %collective-permute-done.6.refs_2_ = bf16[128,512]{1,0:T(8,128)(2,1)S(1)} collective-permute-done((bf16[128,512]{1,0:T(8,128)(2,1)S(1)}, bf16[128,512]{1,0:T(8,128)(2,1)S(1)}, u32[]{:S(2)}, u32[]{:S(2)}) %collective-permute-start.6) | collective-permute-done | bytes 131104 | tf_op jit(solution)/shard_map/ppermute | solution.py:244
  29.0 3.6 %collective-permute-done.8.refs_3_ = bf16[128,512]{1,0:T(8,128)(2,1)S(1)} collective-permute-done((bf16[128,512]{1,0:T(8,128)(2,1)S(1)}, bf16[128,512]{1,0:T(8,128)(2,1)S(1)}, u32[]{:S(2)}, u32[]{:S(2)}) %collective-permute-start.8) | collective-permute-done | bytes 131104 | tf_op jit(solution)/shard_map/ppermute | solution.py:244
  32.6 0.1 shard_map.113
  32.8 1.0 %collective-permute-start.9 = (bf16[128,512]{1,0:T(8,128)(2,1)S(1)}, bf16[128,512]{1,0:T(8,128)(2,1)S(1)}, u32[]{:S(2)}, u32[]{:S(2)}) collective-permute-start(bf16[128,512]{1,0:T(8,128)(2,1)S(1)} %get-tuple-element.29.scaled), channel_id=1, source_target_pairs={{128,0},{129,1},{130,2},{131,3},{132,4},{133,5},{134,6},{135,7},{1... | collective-permute-start | bytes 393224 | tf_op jit(solution)/shard_map/ppermute | solution.py:244
  33.7 0.2 collective-permute-start.10
  33.9 2.2 %collective-permute-start.11 = (bf16[128,512]{1,0:T(8,128)(2,1)S(1)}, bf16[128,512]{1,0:T(8,128)(2,1)S(1)}, u32[]{:S(2)}, u32[]{:S(2)}) collective-permute-start(bf16[128,512]{1,0:T(8,128)(2,1)S(1)} %get-tuple-element.29.scaled), channel_id=1, source_target_pairs={{192,0},{193,1},{194,2},{195,3},{196,4},{197,5},{198,6},{199,7},{2... | collective-permute-start | bytes 393224 | tf_op jit(solution)/shard_map/ppermute | solution.py:244
  36.1 0.5 shard_map.115.before
  36.6 1.9 %collective-permute-done.9.scaled = bf16[128,512]{1,0:T(8,128)(2,1)S(1)} collective-permute-done((bf16[128,512]{1,0:T(8,128)(2,1)S(1)}, bf16[128,512]{1,0:T(8,128)(2,1)S(1)}, u32[]{:S(2)}, u32[]{:S(2)}) %collective-permute-start.9) | collective-permute-done | bytes 131104 | tf_op jit(solution)/shard_map/ppermute | solution.py:244
  38.5 0.5 shard_map.116.before
  38.9 0.0 collective-permute-done.10.scaled
  38.9 0.5 shard_map.117.before
  39.4 2.3 %collective-permute-done.11.scaled = bf16[128,512]{1,0:T(8,128)(2,1)S(1)} collective-permute-done((bf16[128,512]{1,0:T(8,128)(2,1)S(1)}, bf16[128,512]{1,0:T(8,128)(2,1)S(1)}, u32[]{:S(2)}, u32[]{:S(2)}) %collective-permute-start.11) | collective-permute-done | bytes 131104 | tf_op jit(solution)/shard_map/ppermute | solution.py:244
  41.8 0.5 shard_map.119
  42.3 1.4 %collective-permute-start.12 = (bf16[128,1024]{1,0:T(8,128)(2,1)S(1)}, bf16[128,1024]{1,0:T(8,128)(2,1)S(1)}, u32[]{:S(2)}, u32[]{:S(2)}) collective-permute-start(bf16[128,1024]{1,0:T(8,128)(2,1)S(1)} %shard_map.119), channel_id=1, source_target_pairs={{32,0},{33,1},{34,2},{35,3},{36,4},{37,5},{38,6},{39,7},{40,8},{41... | collective-permute-start | bytes 786440 | tf_op jit(solution)/shard_map/ppermute | solution.py:244
  43.6 0.5 shard_map.118.own
  44.1 0.7 %collective-permute-done.12.got = bf16[128,1024]{1,0:T(8,128)(2,1)S(1)} collective-permute-done((bf16[128,1024]{1,0:T(8,128)(2,1)S(1)}, bf16[128,1024]{1,0:T(8,128)(2,1)S(1)}, u32[]{:S(2)}, u32[]{:S(2)}) %collective-permute-start.12) | collective-permute-done | bytes 262176 | tf_op jit(solution)/shard_map/ppermute | solution.py:244
  44.8 0.1 shard_map.120
  44.9 0.1 collective-permute-start.13
  45.0 5.2 %collective-permute-start.14 = (bf16[128,256]{1,0:T(8,128)(2,1)S(1)}, bf16[128,256]{1,0:T(8,128)(2,1)S(1)}, u32[]{:S(2)}, u32[]{:S(2)}) collective-permute-start(bf16[128,256]{1,0:T(8,128)(2,1)S(1)} %get-tuple-element.35), channel_id=1, source_target_pairs={{31,0},{2,1},{1,2},{4,3},{3,4},{6,5},{5,6},{8,7},{7,8},{10,9},{9,1... | collective-permute-start | bytes 196616 | tf_op jit(solution)/shard_map/ppermute | solution.py:244
  50.1 0.8 %shard_map.114 = f32[512,128]{1,0:T(8,128)} custom-call(f32[128,512]{1,0:T(8,128)S(1)} %get-tuple-element.28.source), custom_call_target="tpu_custom_call" | custom-call | flops 1048576 | bytes 1048576 | tf_op jit(solution)/shard_map/pallas_call | solution.py:219
  50.9 0.0 collective-permute-done.13.near
  50.9 1.3 %collective-permute-done.14.far = bf16[128,256]{1,0:T(8,128)(2,1)S(1)} collective-permute-done((bf16[128,256]{1,0:T(8,128)(2,1)S(1)}, bf16[128,256]{1,0:T(8,128)(2,1)S(1)}, u32[]{:S(2)}, u32[]{:S(2)}) %collective-permute-start.14) | collective-permute-done | bytes 65568 | tf_op jit(solution)/shard_map/ppermute | solution.py:244
  52.2 0.9 %shard_map.121 = f32[137,1,512]{2,1,0:T(1,128)} custom-call(f32[128,512]{1,0:T(8,128)S(1)} %get-tuple-element.33.mid, bf16[128,256]{1,0:T(8,128)(2,1)S(1)} %collective-permute-done.13.near, bf16[128,256]{1,0:T(8,128)(2,1)S(1)} %collective-permute-done.14.far, bf16[137,128]{1,0:T(8,128)(2,1)S(1)} %copy-done.1), custom_call_target="tpu_custom_call" | custom-call | flops 1048576 | bytes 1048576 | tf_op jit(solution)/shard_map/pallas_call | solution.py:219
  (2 shorter events, 0.0 us)
Async XLA Ops:
  0.6 0.9 %copy-start.2 = (bf16[1,512,137]{1,2,0:T(8,128)(2,1)S(1)}, bf16[1,512,137]{1,2,0:T(8,128)(2,1)}, u32[]{:S(2)}) copy-start(bf16[1,512,137]{1,2,0:T(8,128)(2,1)} %param.9) | copy-start | bytes 420868
  0.6 0.9 %copy-start.1 = (bf16[137,128]{1,0:T(8,128)(2,1)S(1)}, bf16[137,128]{1,0:T(8,128)(2,1)}, u32[]{:S(2)}) copy-start(bf16[137,128]{1,0:T(8,128)(2,1)} %jac.3) | copy-start | bytes 105220
  0.7 0.9 %copy-start.4 = (s32[512]{0:T(512)S(1)}, s32[512]{0:T(512)}, u32[]{:S(2)}) copy-start(s32[512]{0:T(512)} %param.10) | copy-start | bytes 6148
  0.7 0.9 %copy-start.5 = (s32[512]{0:T(512)S(1)}, s32[512]{0:T(512)}, u32[]{:S(2)}) copy-start(s32[512]{0:T(512)} %param.12) | copy-start | bytes 6148
  0.7 0.9 %copy-start.6 = (f32[512]{0:T(512)S(1)}, f32[512]{0:T(512)}, u32[]{:S(2)}) copy-start(f32[512]{0:T(512)} %param.13) | copy-start | bytes 6148
  0.7 0.9 %copy-start.3 = (bf16[512,8]{0,1:T(8,128)(2,1)S(1)}, bf16[512,8]{0,1:T(8,128)(2,1)}, u32[]{:S(2)}) copy-start(bf16[512,8]{0,1:T(8,128)(2,1)} %param.11) | copy-start | bytes 24580
  1.8 9.2 %collective-permute-start = (bf16[128,256]{1,0:T(8,128)(2,1)S(1)}, bf16[128,256]{1,0:T(8,128)(2,1)S(1)}, u32[]{:S(2)}, u32[]{:S(2)}) collective-permute-start(bf16[128,256]{1,0:T(8,128)(2,1)S(1)} %get-tuple-element.20), channel_id=1, source_target_pairs={{1,0},{0,1},{3,2},{2,3},{5,4},{4,5},{7,6},{6,7},{9,8},{8,9},{11,10... | collective-permute-start | bytes 196616 | tf_op jit(solution)/shard_map/ppermute | solution.py:244
  3.9 8.8 %collective-permute-start.1 = (bf16[128,256]{1,0:T(8,128)(2,1)S(1)}, bf16[128,256]{1,0:T(8,128)(2,1)S(1)}, u32[]{:S(2)}, u32[]{:S(2)}) collective-permute-start(bf16[128,256]{1,0:T(8,128)(2,1)S(1)} %get-tuple-element.21), channel_id=1, source_target_pairs={{31,0},{2,1},{1,2},{4,3},{3,4},{6,5},{5,6},{8,7},{7,8},{10,9},{9,1... | collective-permute-start | bytes 196616 | tf_op jit(solution)/shard_map/ppermute | solution.py:244
  12.7 7.6 %collective-permute-start.2 = (bf16[128,1024]{1,0:T(8,128)(2,1)S(1)}, bf16[128,1024]{1,0:T(8,128)(2,1)S(1)}, u32[]{:S(2)}, u32[]{:S(2)}) collective-permute-start(bf16[128,1024]{1,0:T(8,128)(2,1)S(1)} %shard_map.106.mine), channel_id=1, source_target_pairs={{32,0},{33,1},{34,2},{35,3},{36,4},{37,5},{38,6},{39,7},{40,8},{41... | collective-permute-start | bytes 786440 | tf_op jit(solution)/shard_map/ppermute | solution.py:244
  14.6 4.3 %collective-permute-start.5 = (f32[16,512]{1,0:T(8,128)S(1)}, f32[16,512]{1,0:T(8,128)S(1)}, u32[]{:S(2)}, u32[]{:S(2)}) collective-permute-start(f32[16,512]{1,0:T(8,128)S(1)} %get-tuple-element.22.refs_0_.info), channel_id=1, source_target_pairs={{128,0},{129,1},{130,2},{131,3},{132,4},{133,5},{134,6},{135,7},{1... | collective-permute-start | bytes 98312 | tf_op jit(solution)/shard_map/ppermute | solution.py:244
  17.6 2.8 %collective-permute-start.3 = (f32[16,512]{1,0:T(8,128)S(1)}, f32[16,512]{1,0:T(8,128)S(1)}, u32[]{:S(2)}, u32[]{:S(2)}) collective-permute-start(f32[16,512]{1,0:T(8,128)S(1)} %get-tuple-element.22.refs_0_.info), channel_id=1, source_target_pairs={{64,0},{65,1},{66,2},{67,3},{68,4},{69,5},{70,6},{71,7},{72,8},{73... | collective-permute-start | bytes 98312 | tf_op jit(solution)/shard_map/ppermute | solution.py:244
  17.9 6.2 %collective-permute-start.7 = (f32[16,512]{1,0:T(8,128)S(1)}, f32[16,512]{1,0:T(8,128)S(1)}, u32[]{:S(2)}, u32[]{:S(2)}) collective-permute-start(f32[16,512]{1,0:T(8,128)S(1)} %get-tuple-element.22.refs_0_.info), channel_id=1, source_target_pairs={{192,0},{193,1},{194,2},{195,3},{196,4},{197,5},{198,6},{199,7},{2... | collective-permute-start | bytes 98312 | tf_op jit(solution)/shard_map/ppermute | solution.py:244
  20.8 7.1 %collective-permute-start.4 = (bf16[128,512]{1,0:T(8,128)(2,1)S(1)}, bf16[128,512]{1,0:T(8,128)(2,1)S(1)}, u32[]{:S(2)}, u32[]{:S(2)}) collective-permute-start(bf16[128,512]{1,0:T(8,128)(2,1)S(1)} %get-tuple-element.24), channel_id=1, source_target_pairs={{64,0},{65,1},{66,2},{67,3},{68,4},{69,5},{70,6},{71,7},{72,8},{73... | collective-permute-start | bytes 393224 | tf_op jit(solution)/shard_map/ppermute | solution.py:244
  22.2 4.3 %copy-start = (f32[512,128]{1,0:T(8,128)S(1)}, f32[512,128]{1,0:T(8,128)}, u32[]{:S(2)}) copy-start(f32[512,128]{1,0:T(8,128)} %source.1) | copy-start | bytes 786436
  22.2 6.8 %collective-permute-start.6 = (bf16[128,512]{1,0:T(8,128)(2,1)S(1)}, bf16[128,512]{1,0:T(8,128)(2,1)S(1)}, u32[]{:S(2)}, u32[]{:S(2)}) collective-permute-start(bf16[128,512]{1,0:T(8,128)(2,1)S(1)} %shard_map.110), channel_id=1, source_target_pairs={{128,0},{129,1},{130,2},{131,3},{132,4},{133,5},{134,6},{135,7},{1... | collective-permute-start | bytes 393224 | tf_op jit(solution)/shard_map/ppermute | solution.py:244
  24.6 8.0 %collective-permute-start.8 = (bf16[128,512]{1,0:T(8,128)(2,1)S(1)}, bf16[128,512]{1,0:T(8,128)(2,1)S(1)}, u32[]{:S(2)}, u32[]{:S(2)}) collective-permute-start(bf16[128,512]{1,0:T(8,128)(2,1)S(1)} %get-tuple-element.25), channel_id=1, source_target_pairs={{192,0},{193,1},{194,2},{195,3},{196,4},{197,5},{198,6},{199,7},{2... | collective-permute-start | bytes 393224 | tf_op jit(solution)/shard_map/ppermute | solution.py:244
  26.5 0.7 %copy-start.7 = (f32[128]{0:T(128)S(1)}, f32[128]{0:T(128)}, u32[]{:S(2)}) copy-start(f32[128]{0:T(128)} %param.17) | copy-start | bytes 1540
  32.8 5.7 %collective-permute-start.9 = (bf16[128,512]{1,0:T(8,128)(2,1)S(1)}, bf16[128,512]{1,0:T(8,128)(2,1)S(1)}, u32[]{:S(2)}, u32[]{:S(2)}) collective-permute-start(bf16[128,512]{1,0:T(8,128)(2,1)S(1)} %get-tuple-element.29.scaled), channel_id=1, source_target_pairs={{128,0},{129,1},{130,2},{131,3},{132,4},{133,5},{134,6},{135,7},{1... | collective-permute-start | bytes 393224 | tf_op jit(solution)/shard_map/ppermute | solution.py:244
  33.7 5.2 %collective-permute-start.10 = (bf16[128,512]{1,0:T(8,128)(2,1)S(1)}, bf16[128,512]{1,0:T(8,128)(2,1)S(1)}, u32[]{:S(2)}, u32[]{:S(2)}) collective-permute-start(bf16[128,512]{1,0:T(8,128)(2,1)S(1)} %get-tuple-element.29.scaled), channel_id=1, source_target_pairs={{64,0},{65,1},{66,2},{67,3},{68,4},{69,5},{70,6},{71,7},{72,8},{73... | collective-permute-start | bytes 393224 | tf_op jit(solution)/shard_map/ppermute | solution.py:244
  33.9 7.9 %collective-permute-start.11 = (bf16[128,512]{1,0:T(8,128)(2,1)S(1)}, bf16[128,512]{1,0:T(8,128)(2,1)S(1)}, u32[]{:S(2)}, u32[]{:S(2)}) collective-permute-start(bf16[128,512]{1,0:T(8,128)(2,1)S(1)} %get-tuple-element.29.scaled), channel_id=1, source_target_pairs={{192,0},{193,1},{194,2},{195,3},{196,4},{197,5},{198,6},{199,7},{2... | collective-permute-start | bytes 393224 | tf_op jit(solution)/shard_map/ppermute | solution.py:244
  42.3 2.5 %collective-permute-start.12 = (bf16[128,1024]{1,0:T(8,128)(2,1)S(1)}, bf16[128,1024]{1,0:T(8,128)(2,1)S(1)}, u32[]{:S(2)}, u32[]{:S(2)}) collective-permute-start(bf16[128,1024]{1,0:T(8,128)(2,1)S(1)} %shard_map.119), channel_id=1, source_target_pairs={{32,0},{33,1},{34,2},{35,3},{36,4},{37,5},{38,6},{39,7},{40,8},{41... | collective-permute-start | bytes 786440 | tf_op jit(solution)/shard_map/ppermute | solution.py:244
  44.9 6.1 %collective-permute-start.13 = (bf16[128,256]{1,0:T(8,128)(2,1)S(1)}, bf16[128,256]{1,0:T(8,128)(2,1)S(1)}, u32[]{:S(2)}, u32[]{:S(2)}) collective-permute-start(bf16[128,256]{1,0:T(8,128)(2,1)S(1)} %get-tuple-element.34), channel_id=1, source_target_pairs={{1,0},{0,1},{3,2},{2,3},{5,4},{4,5},{7,6},{6,7},{9,8},{8,9},{11,10... | collective-permute-start | bytes 196616 | tf_op jit(solution)/shard_map/ppermute | solution.py:244
  45.0 7.2 %collective-permute-start.14 = (bf16[128,256]{1,0:T(8,128)(2,1)S(1)}, bf16[128,256]{1,0:T(8,128)(2,1)S(1)}, u32[]{:S(2)}, u32[]{:S(2)}) collective-permute-start(bf16[128,256]{1,0:T(8,128)(2,1)S(1)} %get-tuple-element.35), channel_id=1, source_target_pairs={{31,0},{2,1},{1,2},{4,3},{3,4},{6,5},{5,6},{8,7},{7,8},{10,9},{9,1... | collective-permute-start | bytes 196616 | tf_op jit(solution)/shard_map/ppermute | solution.py:244

commit v8 on v7

--- a/solution.py
+++ b/solution.py
@@ -67,6 +67,12 @@
     info[8:16, :] = extra
 
 
+def pair_kernel(own, got, pair):
+    rows = own.shape[0]
+    pair[:rows, :] = own[...]
+    pair[rows:, :] = got[...]
+
+
 def widen_kernel(full, near, far, wide):
     cols = full.shape[1]
     half = cols // 2
@@ -274,7 +280,10 @@
             flat(obs_frac),
         )
         near, far = swap(near, tile="near"), swap(far, tile="far")
-        infos = [info] + [swap(info, y=j) for j in range(1, lanes)]
+        got = swap(info, y=2)
+        (pair,) = call(pair_kernel, [((32, obs), F32)], info, got)
+        pair = swap(pair, y=1)
+        infos = [info, pair[:16], got, pair[16:]]
         (wide,) = call(widen_kernel, [((chan, width), BF16)], full, near, far)
         other = swap(wide, core=1)
         mats = [None] * lanes

time: 53.2 us -> 53.3 us (level)
  starting transfers between devices: 28.9 us -> 26.2 us
  waiting for transfers between devices: 14.4 us -> 17 us
    ppermute x15 -> x14, starting transfers between devices: 28.9 us -> 26.2 us  [swap(): return lax.ppermute(block, ('tm', 'space'), route)]
    ppermute x15 -> x14, waiting for transfers between devices: 14.4 us -> 17 us  [swap(): return lax.ppermute(block, ('tm', 'space'), route)]
    pallas_call x18 -> x19, Pallas kernels: 6.84 us -> 6.85 us  [call(): pl.pallas_call(kernel, out_shape=[jax.ShapeDtypeStruct(shape, dtype) for...]
  transfers between devices with their start and end apart: 15 -> 14, of which waited for: 9 -> 9; matrix products, arithmetic and copies ran while one was open for 0% -> 0% of each run, Pallas kernels for 9% -> 9%
where the time goes in v8:
time: 53.3 us; the launch traced here: 53.1 us
  starting transfers between devices  26.2 us (49%)
  waiting for transfers between devices  17 us (32%)
  Pallas kernels  6.85 us (13%)
  between operations  1.53 us (3%)
  local copies, waits for them, and re-layouts  1.52 us (3%)
    ppermute x14, starting transfers between devices, swap(): return lax.ppermute(block, ('tm', 'space'), route)  26.2 us
    ppermute x14, waiting for transfers between devices, swap(): return lax.ppermute(block, ('tm', 'space'), route)  17 us
    pallas_call x19, Pallas kernels, call(): pl.pallas_call(kernel, out_shape=[jax.ShapeDtypeStruct(shape, dtype) for...  6.85 us
    unnamed x16, local copies, waits for them, and re-layouts  1.51 us
  transfers between devices with their start and end apart: 14, of which 9 were waited for; matrix products, arithmetic and copies ran while one was open for 0% of the time, Pallas kernels for 9%

profile of v8, /device:TPU:1, one launch (start us, length us, event | category | flops | bytes accessed | tf_op | source)
XLA Modules:
  0.0 53.1 jit_solution(15443099095376331280)
XLA Ops:
  0.6 0.0 copy-start.2
  0.6 0.0 copy-start.1
  0.7 0.0 copy-start.4
  0.7 0.0 copy-start.5
  0.7 0.0 copy-start.6
  0.7 0.0 copy-start.3
  0.7 0.8 %copy-done.2 = bf16[1,512,137]{1,2,0:T(8,128)(2,1)S(1)} copy-done((bf16[1,512,137]{1,2,0:T(8,128)(2,1)S(1)}, bf16[1,512,137]{1,2,0:T(8,128)(2,1)}, u32[]{:S(2)}) %copy-start.2) | copy-done | bytes 140312
  1.5 0.0 copy-done.1
  1.5 0.0 copy-done.4
  1.5 0.0 copy-done.5
  1.6 0.0 copy-done.6
  1.6 0.0 copy-done.3
  1.6 0.2 shard_map.105
  1.8 2.1 %collective-permute-start = (bf16[128,256]{1,0:T(8,128)(2,1)S(1)}, bf16[128,256]{1,0:T(8,128)(2,1)S(1)}, u32[]{:S(2)}, u32[]{:S(2)}) collective-permute-start(bf16[128,256]{1,0:T(8,128)(2,1)S(1)} %get-tuple-element.20), channel_id=1, source_target_pairs={{1,0},{0,1},{3,2},{2,3},{5,4},{4,5},{7,6},{6,7},{9,8},{8,9},{11,10... | collective-permute-start | bytes 196616 | tf_op jit(solution)/shard_map/ppermute | solution.py:250
  3.9 7.1 %collective-permute-start.1 = (bf16[128,256]{1,0:T(8,128)(2,1)S(1)}, bf16[128,256]{1,0:T(8,128)(2,1)S(1)}, u32[]{:S(2)}, u32[]{:S(2)}) collective-permute-start(bf16[128,256]{1,0:T(8,128)(2,1)S(1)} %get-tuple-element.21), channel_id=1, source_target_pairs={{31,0},{2,1},{1,2},{4,3},{3,4},{6,5},{5,6},{8,7},{7,8},{10,9},{9,1... | collective-permute-start | bytes 196616 | tf_op jit(solution)/shard_map/ppermute | solution.py:250
  11.0 2.9 %collective-permute-start.3 = (f32[16,512]{1,0:T(8,128)S(1)}, f32[16,512]{1,0:T(8,128)S(1)}, u32[]{:S(2)}, u32[]{:S(2)}) collective-permute-start(f32[16,512]{1,0:T(8,128)S(1)} %get-tuple-element.22.refs_0_.own.info), channel_id=1, source_target_pairs={{128,0},{129,1},{130,2},{131,3},{132,4},{133,5},{134,6},{135,7},{1... | collective-permute-start | bytes 98312 | tf_op jit(solution)/shard_map/ppermute | solution.py:250
  14.0 1.4 %collective-permute-done.3.got.info = f32[16,512]{1,0:T(8,128)S(1)} collective-permute-done((f32[16,512]{1,0:T(8,128)S(1)}, f32[16,512]{1,0:T(8,128)S(1)}, u32[]{:S(2)}, u32[]{:S(2)}) %collective-permute-start.3) | collective-permute-done | bytes 32800 | tf_op jit(solution)/shard_map/ppermute | solution.py:250
  15.3 1.3 %collective-permute-start.4 = (f32[32,512]{1,0:T(8,128)S(1)}, f32[32,512]{1,0:T(8,128)S(1)}, u32[]{:S(2)}, u32[]{:S(2)}) collective-permute-start(f32[32,512]{1,0:T(8,128)S(1)} %shard_map.108), channel_id=1, source_target_pairs={{64,0},{65,1},{66,2},{67,3},{68,4},{69,5},{70,6},{71,7},{72,8},{73... | collective-permute-start | bytes 196616 | tf_op jit(solution)/shard_map/ppermute | solution.py:250
  16.6 0.0 collective-permute-done.near
  16.6 0.0 collective-permute-done.1.far
  16.7 2.8 %collective-permute-start.2 = (bf16[128,1024]{1,0:T(8,128)(2,1)S(1)}, bf16[128,1024]{1,0:T(8,128)(2,1)S(1)}, u32[]{:S(2)}, u32[]{:S(2)}) collective-permute-start(bf16[128,1024]{1,0:T(8,128)(2,1)S(1)} %shard_map.106.mine), channel_id=1, source_target_pairs={{32,0},{33,1},{34,2},{35,3},{36,4},{37,5},{38,6},{39,7},{40,8},{41... | collective-permute-start | bytes 786440 | tf_op jit(solution)/shard_map/ppermute | solution.py:250
  19.4 0.2 shard_map.110.mat
  19.6 0.0 collective-permute-done.4
  19.6 1.0 %collective-permute-done.2.other = bf16[128,1024]{1,0:T(8,128)(2,1)S(1)} collective-permute-done((bf16[128,1024]{1,0:T(8,128)(2,1)S(1)}, bf16[128,1024]{1,0:T(8,128)(2,1)S(1)}, u32[]{:S(2)}, u32[]{:S(2)}) %collective-permute-start.2) | collective-permute-done | bytes 262176 | tf_op jit(solution)/shard_map/ppermute | solution.py:250
  20.6 0.5 shard_map.109
  21.1 0.3 collective-permute-start.5
  21.3 0.4 shard_map.111
  21.8 3.0 %collective-permute-start.6 = (bf16[128,512]{1,0:T(8,128)(2,1)S(1)}, bf16[128,512]{1,0:T(8,128)(2,1)S(1)}, u32[]{:S(2)}, u32[]{:S(2)}) collective-permute-start(bf16[128,512]{1,0:T(8,128)(2,1)S(1)} %shard_map.111), channel_id=1, source_target_pairs={{128,0},{129,1},{130,2},{131,3},{132,4},{133,5},{134,6},{135,7},{1... | collective-permute-start | bytes 393224 | tf_op jit(solution)/shard_map/ppermute | solution.py:250
  24.8 0.0 copy-start
  24.8 0.5 shard_map.112
  25.3 0.9 %collective-permute-start.7 = (bf16[128,512]{1,0:T(8,128)(2,1)S(1)}, bf16[128,512]{1,0:T(8,128)(2,1)S(1)}, u32[]{:S(2)}, u32[]{:S(2)}) collective-permute-start(bf16[128,512]{1,0:T(8,128)(2,1)S(1)} %get-tuple-element.25), channel_id=1, source_target_pairs={{192,0},{193,1},{194,2},{195,3},{196,4},{197,5},{198,6},{199,7},{2... | collective-permute-start | bytes 393224 | tf_op jit(solution)/shard_map/ppermute | solution.py:250
  26.8 0.0 copy-start.7
  26.8 0.0 copy-done
  26.8 0.6 %copy-done.7 = f32[128]{0:T(128)S(1)} copy-done((f32[128]{0:T(128)S(1)}, f32[128]{0:T(128)}, u32[]{:S(2)}) %copy-start.7) | copy-done | bytes 536
  27.4 0.3 shard_map.113
  27.7 0.5 shard_map.107
  28.2 0.0 collective-permute-done.5.refs_1_
  28.2 0.0 collective-permute-done.6.refs_2_
  28.2 3.6 %collective-permute-done.7.refs_3_ = bf16[128,512]{1,0:T(8,128)(2,1)S(1)} collective-permute-done((bf16[128,512]{1,0:T(8,128)(2,1)S(1)}, bf16[128,512]{1,0:T(8,128)(2,1)S(1)}, u32[]{:S(2)}, u32[]{:S(2)}) %collective-permute-start.7) | collective-permute-done | bytes 131104 | tf_op jit(solution)/shard_map/ppermute | solution.py:250
  31.8 0.1 shard_map.114
  31.9 0.1 collective-permute-start.8
  32.0 3.4 %collective-permute-start.9 = (bf16[128,512]{1,0:T(8,128)(2,1)S(1)}, bf16[128,512]{1,0:T(8,128)(2,1)S(1)}, u32[]{:S(2)}, u32[]{:S(2)}) collective-permute-start(bf16[128,512]{1,0:T(8,128)(2,1)S(1)} %get-tuple-element.29.scaled), channel_id=1, source_target_pairs={{64,0},{65,1},{66,2},{67,3},{68,4},{69,5},{70,6},{71,7},{72,8},{73... | collective-permute-start | bytes 393224 | tf_op jit(solution)/shard_map/ppermute | solution.py:250
  35.4 0.0 collective-permute-start.10
  35.4 0.5 shard_map.116.before
  35.9 1.4 %collective-permute-done.8.scaled = bf16[128,512]{1,0:T(8,128)(2,1)S(1)} collective-permute-done((bf16[128,512]{1,0:T(8,128)(2,1)S(1)}, bf16[128,512]{1,0:T(8,128)(2,1)S(1)}, u32[]{:S(2)}, u32[]{:S(2)}) %collective-permute-start.8) | collective-permute-done | bytes 131104 | tf_op jit(solution)/shard_map/ppermute | solution.py:250
  37.3 0.5 shard_map.117.before
  37.8 3.2 %collective-permute-done.9.scaled = bf16[128,512]{1,0:T(8,128)(2,1)S(1)} collective-permute-done((bf16[128,512]{1,0:T(8,128)(2,1)S(1)}, bf16[128,512]{1,0:T(8,128)(2,1)S(1)}, u32[]{:S(2)}, u32[]{:S(2)}) %collective-permute-start.9) | collective-permute-done | bytes 131104 | tf_op jit(solution)/shard_map/ppermute | solution.py:250
  41.0 0.5 shard_map.118.before
  41.4 1.4 %collective-permute-done.10.scaled = bf16[128,512]{1,0:T(8,128)(2,1)S(1)} collective-permute-done((bf16[128,512]{1,0:T(8,128)(2,1)S(1)}, bf16[128,512]{1,0:T(8,128)(2,1)S(1)}, u32[]{:S(2)}, u32[]{:S(2)}) %collective-permute-start.10) | collective-permute-done | bytes 131104 | tf_op jit(solution)/shard_map/ppermute | solution.py:250
  42.9 0.5 shard_map.120
  43.3 1.0 %collective-permute-start.11 = (bf16[128,1024]{1,0:T(8,128)(2,1)S(1)}, bf16[128,1024]{1,0:T(8,128)(2,1)S(1)}, u32[]{:S(2)}, u32[]{:S(2)}) collective-permute-start(bf16[128,1024]{1,0:T(8,128)(2,1)S(1)} %shard_map.120), channel_id=1, source_target_pairs={{32,0},{33,1},{34,2},{35,3},{36,4},{37,5},{38,6},{39,7},{40,8},{41... | collective-permute-start | bytes 786440 | tf_op jit(solution)/shard_map/ppermute | solution.py:250
  44.4 0.5 shard_map.119.own
  44.8 0.7 %collective-permute-done.11.got = bf16[128,1024]{1,0:T(8,128)(2,1)S(1)} collective-permute-done((bf16[128,1024]{1,0:T(8,128)(2,1)S(1)}, bf16[128,1024]{1,0:T(8,128)(2,1)S(1)}, u32[]{:S(2)}, u32[]{:S(2)}) %collective-permute-start.11) | collective-permute-done | bytes 262176 | tf_op jit(solution)/shard_map/ppermute | solution.py:250
  45.5 0.1 shard_map.121
  45.6 0.1 collective-permute-start.12
  45.7 1.3 %collective-permute-start.13 = (bf16[128,256]{1,0:T(8,128)(2,1)S(1)}, bf16[128,256]{1,0:T(8,128)(2,1)S(1)}, u32[]{:S(2)}, u32[]{:S(2)}) collective-permute-start(bf16[128,256]{1,0:T(8,128)(2,1)S(1)} %get-tuple-element.35), channel_id=1, source_target_pairs={{31,0},{2,1},{1,2},{4,3},{3,4},{6,5},{5,6},{8,7},{7,8},{10,9},{9,1... | collective-permute-start | bytes 196616 | tf_op jit(solution)/shard_map/ppermute | solution.py:250
  47.0 0.8 %shard_map.115 = f32[512,128]{1,0:T(8,128)} custom-call(f32[128,512]{1,0:T(8,128)S(1)} %get-tuple-element.28.source), custom_call_target="tpu_custom_call" | custom-call | flops 1048576 | bytes 1048576 | tf_op jit(solution)/shard_map/pallas_call | solution.py:225
  47.8 1.0 %collective-permute-done.12.near = bf16[128,256]{1,0:T(8,128)(2,1)S(1)} collective-permute-done((bf16[128,256]{1,0:T(8,128)(2,1)S(1)}, bf16[128,256]{1,0:T(8,128)(2,1)S(1)}, u32[]{:S(2)}, u32[]{:S(2)}) %collective-permute-start.12) | collective-permute-done | bytes 65568 | tf_op jit(solution)/shard_map/ppermute | solution.py:250
  48.8 3.4 %collective-permute-done.13.far = bf16[128,256]{1,0:T(8,128)(2,1)S(1)} collective-permute-done((bf16[128,256]{1,0:T(8,128)(2,1)S(1)}, bf16[128,256]{1,0:T(8,128)(2,1)S(1)}, u32[]{:S(2)}, u32[]{:S(2)}) %collective-permute-start.13) | collective-permute-done | bytes 65568 | tf_op jit(solution)/shard_map/ppermute | solution.py:250
  52.2 0.9 %shard_map.122 = f32[137,1,512]{2,1,0:T(1,128)} custom-call(f32[128,512]{1,0:T(8,128)S(1)} %get-tuple-element.33.mid, bf16[128,256]{1,0:T(8,128)(2,1)S(1)} %collective-permute-done.12.near, bf16[128,256]{1,0:T(8,128)(2,1)S(1)} %collective-permute-done.13.far, bf16[137,128]{1,0:T(8,128)(2,1)S(1)} %copy-done.1), custom_call_target="tpu_custom_call" | custom-call | flops 1048576 | bytes 1048576 | tf_op jit(solution)/shard_map/pallas_call | solution.py:225
  (4 shorter events, 0.0 us)
Async XLA Ops:
  0.6 0.9 %copy-start.2 = (bf16[1,512,137]{1,2,0:T(8,128)(2,1)S(1)}, bf16[1,512,137]{1,2,0:T(8,128)(2,1)}, u32[]{:S(2)}) copy-start(bf16[1,512,137]{1,2,0:T(8,128)(2,1)} %param.9) | copy-start | bytes 420868
  0.6 0.9 %copy-start.1 = (bf16[137,128]{1,0:T(8,128)(2,1)S(1)}, bf16[137,128]{1,0:T(8,128)(2,1)}, u32[]{:S(2)}) copy-start(bf16[137,128]{1,0:T(8,128)(2,1)} %jac.3) | copy-start | bytes 105220
  0.7 0.9 %copy-start.4 = (s32[512]{0:T(512)S(1)}, s32[512]{0:T(512)}, u32[]{:S(2)}) copy-start(s32[512]{0:T(512)} %param.10) | copy-start | bytes 6148
  0.7 0.9 %copy-start.5 = (s32[512]{0:T(512)S(1)}, s32[512]{0:T(512)}, u32[]{:S(2)}) copy-start(s32[512]{0:T(512)} %param.12) | copy-start | bytes 6148
  0.7 0.9 %copy-start.6 = (f32[512]{0:T(512)S(1)}, f32[512]{0:T(512)}, u32[]{:S(2)}) copy-start(f32[512]{0:T(512)} %param.13) | copy-start | bytes 6148
  0.7 0.9 %copy-start.3 = (bf16[512,8]{0,1:T(8,128)(2,1)S(1)}, bf16[512,8]{0,1:T(8,128)(2,1)}, u32[]{:S(2)}) copy-start(bf16[512,8]{0,1:T(8,128)(2,1)} %param.11) | copy-start | bytes 24580
  1.8 14.8 %collective-permute-start = (bf16[128,256]{1,0:T(8,128)(2,1)S(1)}, bf16[128,256]{1,0:T(8,128)(2,1)S(1)}, u32[]{:S(2)}, u32[]{:S(2)}) collective-permute-start(bf16[128,256]{1,0:T(8,128)(2,1)S(1)} %get-tuple-element.20), channel_id=1, source_target_pairs={{1,0},{0,1},{3,2},{2,3},{5,4},{4,5},{7,6},{6,7},{9,8},{8,9},{11,10... | collective-permute-start | bytes 196616 | tf_op jit(solution)/shard_map/ppermute | solution.py:250
  3.9 12.7 %collective-permute-start.1 = (bf16[128,256]{1,0:T(8,128)(2,1)S(1)}, bf16[128,256]{1,0:T(8,128)(2,1)S(1)}, u32[]{:S(2)}, u32[]{:S(2)}) collective-permute-start(bf16[128,256]{1,0:T(8,128)(2,1)S(1)} %get-tuple-element.21), channel_id=1, source_target_pairs={{31,0},{2,1},{1,2},{4,3},{3,4},{6,5},{5,6},{8,7},{7,8},{10,9},{9,1... | collective-permute-start | bytes 196616 | tf_op jit(solution)/shard_map/ppermute | solution.py:250
  11.0 4.3 %collective-permute-start.3 = (f32[16,512]{1,0:T(8,128)S(1)}, f32[16,512]{1,0:T(8,128)S(1)}, u32[]{:S(2)}, u32[]{:S(2)}) collective-permute-start(f32[16,512]{1,0:T(8,128)S(1)} %get-tuple-element.22.refs_0_.own.info), channel_id=1, source_target_pairs={{128,0},{129,1},{130,2},{131,3},{132,4},{133,5},{134,6},{135,7},{1... | collective-permute-start | bytes 98312 | tf_op jit(solution)/shard_map/ppermute | solution.py:250
  15.3 4.2 %collective-permute-start.4 = (f32[32,512]{1,0:T(8,128)S(1)}, f32[32,512]{1,0:T(8,128)S(1)}, u32[]{:S(2)}, u32[]{:S(2)}) collective-permute-start(f32[32,512]{1,0:T(8,128)S(1)} %shard_map.108), channel_id=1, source_target_pairs={{64,0},{65,1},{66,2},{67,3},{68,4},{69,5},{70,6},{71,7},{72,8},{73... | collective-permute-start | bytes 196616 | tf_op jit(solution)/shard_map/ppermute | solution.py:250
  16.7 3.9 %collective-permute-start.2 = (bf16[128,1024]{1,0:T(8,128)(2,1)S(1)}, bf16[128,1024]{1,0:T(8,128)(2,1)S(1)}, u32[]{:S(2)}, u32[]{:S(2)}) collective-permute-start(bf16[128,1024]{1,0:T(8,128)(2,1)S(1)} %shard_map.106.mine), channel_id=1, source_target_pairs={{32,0},{33,1},{34,2},{35,3},{36,4},{37,5},{38,6},{39,7},{40,8},{41... | collective-permute-start | bytes 786440 | tf_op jit(solution)/shard_map/ppermute | solution.py:250
  21.1 7.1 %collective-permute-start.5 = (bf16[128,512]{1,0:T(8,128)(2,1)S(1)}, bf16[128,512]{1,0:T(8,128)(2,1)S(1)}, u32[]{:S(2)}, u32[]{:S(2)}) collective-permute-start(bf16[128,512]{1,0:T(8,128)(2,1)S(1)} %get-tuple-element.24), channel_id=1, source_target_pairs={{64,0},{65,1},{66,2},{67,3},{68,4},{69,5},{70,6},{71,7},{72,8},{73... | collective-permute-start | bytes 393224 | tf_op jit(solution)/shard_map/ppermute | solution.py:250
  21.8 6.4 %collective-permute-start.6 = (bf16[128,512]{1,0:T(8,128)(2,1)S(1)}, bf16[128,512]{1,0:T(8,128)(2,1)S(1)}, u32[]{:S(2)}, u32[]{:S(2)}) collective-permute-start(bf16[128,512]{1,0:T(8,128)(2,1)S(1)} %shard_map.111), channel_id=1, source_target_pairs={{128,0},{129,1},{130,2},{131,3},{132,4},{133,5},{134,6},{135,7},{1... | collective-permute-start | bytes 393224 | tf_op jit(solution)/shard_map/ppermute | solution.py:250
  24.8 2.0 %copy-start = (f32[512,128]{1,0:T(8,128)S(1)}, f32[512,128]{1,0:T(8,128)}, u32[]{:S(2)}) copy-start(f32[512,128]{1,0:T(8,128)} %source.1) | copy-start | bytes 786436
  25.3 6.5 %collective-permute-start.7 = (bf16[128,512]{1,0:T(8,128)(2,1)S(1)}, bf16[128,512]{1,0:T(8,128)(2,1)S(1)}, u32[]{:S(2)}, u32[]{:S(2)}) collective-permute-start(bf16[128,512]{1,0:T(8,128)(2,1)S(1)} %get-tuple-element.25), channel_id=1, source_target_pairs={{192,0},{193,1},{194,2},{195,3},{196,4},{197,5},{198,6},{199,7},{2... | collective-permute-start | bytes 393224 | tf_op jit(solution)/shard_map/ppermute | solution.py:250
  26.8 0.7 %copy-start.7 = (f32[128]{0:T(128)S(1)}, f32[128]{0:T(128)}, u32[]{:S(2)}) copy-start(f32[128]{0:T(128)} %param.17) | copy-start | bytes 1540
  31.9 5.4 %collective-permute-start.8 = (bf16[128,512]{1,0:T(8,128)(2,1)S(1)}, bf16[128,512]{1,0:T(8,128)(2,1)S(1)}, u32[]{:S(2)}, u32[]{:S(2)}) collective-permute-start(bf16[128,512]{1,0:T(8,128)(2,1)S(1)} %get-tuple-element.29.scaled), channel_id=1, source_target_pairs={{128,0},{129,1},{130,2},{131,3},{132,4},{133,5},{134,6},{135,7},{1... | collective-permute-start | bytes 393224 | tf_op jit(solution)/shard_map/ppermute | solution.py:250
  32.0 9.0 %collective-permute-start.9 = (bf16[128,512]{1,0:T(8,128)(2,1)S(1)}, bf16[128,512]{1,0:T(8,128)(2,1)S(1)}, u32[]{:S(2)}, u32[]{:S(2)}) collective-permute-start(bf16[128,512]{1,0:T(8,128)(2,1)S(1)} %get-tuple-element.29.scaled), channel_id=1, source_target_pairs={{64,0},{65,1},{66,2},{67,3},{68,4},{69,5},{70,6},{71,7},{72,8},{73... | collective-permute-start | bytes 393224 | tf_op jit(solution)/shard_map/ppermute | solution.py:250
  35.4 7.5 %collective-permute-start.10 = (bf16[128,512]{1,0:T(8,128)(2,1)S(1)}, bf16[128,512]{1,0:T(8,128)(2,1)S(1)}, u32[]{:S(2)}, u32[]{:S(2)}) collective-permute-start(bf16[128,512]{1,0:T(8,128)(2,1)S(1)} %get-tuple-element.29.scaled), channel_id=1, source_target_pairs={{192,0},{193,1},{194,2},{195,3},{196,4},{197,5},{198,6},{199,7},{2... | collective-permute-start | bytes 393224 | tf_op jit(solution)/shard_map/ppermute | solution.py:250
  43.3 2.2 %collective-permute-start.11 = (bf16[128,1024]{1,0:T(8,128)(2,1)S(1)}, bf16[128,1024]{1,0:T(8,128)(2,1)S(1)}, u32[]{:S(2)}, u32[]{:S(2)}) collective-permute-start(bf16[128,1024]{1,0:T(8,128)(2,1)S(1)} %shard_map.120), channel_id=1, source_target_pairs={{32,0},{33,1},{34,2},{35,3},{36,4},{37,5},{38,6},{39,7},{40,8},{41... | collective-permute-start | bytes 786440 | tf_op jit(solution)/shard_map/ppermute | solution.py:250
  45.6 3.2 %collective-permute-start.12 = (bf16[128,256]{1,0:T(8,128)(2,1)S(1)}, bf16[128,256]{1,0:T(8,128)(2,1)S(1)}, u32[]{:S(2)}, u32[]{:S(2)}) collective-permute-start(bf16[128,256]{1,0:T(8,128)(2,1)S(1)} %get-tuple-element.34), channel_id=1, source_target_pairs={{1,0},{0,1},{3,2},{2,3},{5,4},{4,5},{7,6},{6,7},{9,8},{8,9},{11,10... | collective-permute-start | bytes 196616 | tf_op jit(solution)/shard_map/ppermute | solution.py:250
  45.7 6.5 %collective-permute-start.13 = (bf16[128,256]{1,0:T(8,128)(2,1)S(1)}, bf16[128,256]{1,0:T(8,128)(2,1)S(1)}, u32[]{:S(2)}, u32[]{:S(2)}) collective-permute-start(bf16[128,256]{1,0:T(8,128)(2,1)S(1)} %get-tuple-element.35), channel_id=1, source_target_pairs={{31,0},{2,1},{1,2},{4,3},{3,4},{6,5},{5,6},{8,7},{7,8},{10,9},{9,1... | collective-permute-start | bytes 196616 | tf_op jit(solution)/shard_map/ppermute | solution.py:250

commit v9 on v7

--- a/solution.py
+++ b/solution.py
@@ -11,6 +11,7 @@
 F32 = jnp.float32
 BF16 = jnp.bfloat16
 GROUP = 16
+PIECE = 32
 SWAP_ORDER = (2, 3, 1)
 LAND_ORDER = (2, 1, 3)
 FIRST_FLOPS = 1 << 34
@@ -200,13 +201,13 @@
 def finish_kernel(mid, near, far, jac, out, rows, sems):
     half = near.shape[1]
     levels = jac.shape[0]
-    cut = (levels // 2 + 15) // 16 * 16
     even = even_tile()
     first = mid[:, :half] + jnp.where(even, far[...], near[...]).astype(F32)
     last = mid[:, half:] + jnp.where(even, near[...], far[...]).astype(F32)
     total = jnp.concatenate([first, last], axis=1).astype(BF16)
     copies = []
-    for index, part in enumerate((slice(0, cut), slice(cut, levels))):
+    for index, begin in enumerate(range(0, levels, PIECE)):
+        part = slice(begin, min(begin + PIECE, levels))
         rows[part, 0, :] = jnp.dot(jac[part, :], total, preferred_element_type=F32)
         copy = pltpu.make_async_copy(rows.at[part], out.at[part], sems.at[index])
         copy.start()
@@ -336,6 +337,7 @@
         mid, near, far = call(
             join_kernel, [((chan, cols), F32)] + [((chan, half), BF16)] * 2, mine, give
         )
+        pieces = -(-levels // PIECE)
         (adjoint,) = call(
             finish_kernel,
             [((levels, 1, cols), F32)],
@@ -344,7 +346,7 @@
             swap(far, tile="far"),
             jacobian,
             out_specs=[HBM],
-            scratch=[pltpu.VMEM((levels, 1, cols), F32), pltpu.SemaphoreType.DMA((2,))],
+            scratch=[pltpu.VMEM((levels, 1, cols), F32), pltpu.SemaphoreType.DMA((pieces,))],
         )
         return (departures, jnp.transpose(adjoint, (1, 2, 0)))
 

time: 53.2 us -> 53.2 us (level)
  no operation moved by 1% of the time
where the time goes in v9:
time: 53.2 us; the launch traced here: 53.1 us
  starting transfers between devices  28.9 us (54%)
  waiting for transfers between devices  14.4 us (27%)
  Pallas kernels  6.83 us (13%)
  between operations  1.52 us (3%)
  local copies, waits for them, and re-layouts  1.51 us (3%)
    ppermute x15, starting transfers between devices, swap(): return lax.ppermute(block, ('tm', 'space'), route)  28.9 us
    ppermute x15, waiting for transfers between devices, swap(): return lax.ppermute(block, ('tm', 'space'), route)  14.4 us
    pallas_call x18, Pallas kernels, call(): pl.pallas_call(kernel, out_shape=[jax.ShapeDtypeStruct(shape, dtype) for...  6.83 us
    unnamed x16, local copies, waits for them, and re-layouts  1.51 us
  transfers between devices with their start and end apart: 15, of which 9 were waited for; matrix products, arithmetic and copies ran while one was open for 0% of the time, Pallas kernels for 9%

profile of v9, /device:TPU:1, one launch (start us, length us, event | category | flops | bytes accessed | tf_op | source)
XLA Modules:
  0.0 53.1 jit_solution(5407383592298339525)
XLA Ops:
  0.6 0.0 copy-start.2
  0.6 0.0 copy-start.1
  0.7 0.0 copy-start.4
  0.7 0.0 copy-start.5
  0.7 0.0 copy-start.6
  0.7 0.0 copy-start.3
  0.7 0.8 %copy-done.2 = bf16[1,512,137]{1,2,0:T(8,128)(2,1)S(1)} copy-done((bf16[1,512,137]{1,2,0:T(8,128)(2,1)S(1)}, bf16[1,512,137]{1,2,0:T(8,128)(2,1)}, u32[]{:S(2)}) %copy-start.2) | copy-done | bytes 140312
  1.5 0.0 copy-done.1
  1.5 0.0 copy-done.4
  1.5 0.0 copy-done.5
  1.6 0.0 copy-done.6
  1.6 0.0 copy-done.3
  1.6 0.2 shard_map.105
  1.8 2.1 %collective-permute-start = (bf16[128,256]{1,0:T(8,128)(2,1)S(1)}, bf16[128,256]{1,0:T(8,128)(2,1)S(1)}, u32[]{:S(2)}, u32[]{:S(2)}) collective-permute-start(bf16[128,256]{1,0:T(8,128)(2,1)S(1)} %get-tuple-element.20), channel_id=1, source_target_pairs={{1,0},{0,1},{3,2},{2,3},{5,4},{4,5},{7,6},{6,7},{9,8},{8,9},{11,10... | collective-permute-start | bytes 196616 | tf_op jit(solution)/shard_map/ppermute | solution.py:245
  3.9 7.1 %collective-permute-start.1 = (bf16[128,256]{1,0:T(8,128)(2,1)S(1)}, bf16[128,256]{1,0:T(8,128)(2,1)S(1)}, u32[]{:S(2)}, u32[]{:S(2)}) collective-permute-start(bf16[128,256]{1,0:T(8,128)(2,1)S(1)} %get-tuple-element.21), channel_id=1, source_target_pairs={{31,0},{2,1},{1,2},{4,3},{3,4},{6,5},{5,6},{8,7},{7,8},{10,9},{9,1... | collective-permute-start | bytes 196616 | tf_op jit(solution)/shard_map/ppermute | solution.py:245
  11.0 0.0 collective-permute-done.near
  11.0 1.6 %collective-permute-done.1.far = bf16[128,256]{1,0:T(8,128)(2,1)S(1)} collective-permute-done((bf16[128,256]{1,0:T(8,128)(2,1)S(1)}, bf16[128,256]{1,0:T(8,128)(2,1)S(1)}, u32[]{:S(2)}, u32[]{:S(2)}) %collective-permute-start.1) | collective-permute-done | bytes 65568 | tf_op jit(solution)/shard_map/ppermute | solution.py:245
  12.7 1.9 %collective-permute-start.2 = (bf16[128,1024]{1,0:T(8,128)(2,1)S(1)}, bf16[128,1024]{1,0:T(8,128)(2,1)S(1)}, u32[]{:S(2)}, u32[]{:S(2)}) collective-permute-start(bf16[128,1024]{1,0:T(8,128)(2,1)S(1)} %shard_map.106.mine), channel_id=1, source_target_pairs={{32,0},{33,1},{34,2},{35,3},{36,4},{37,5},{38,6},{39,7},{40,8},{41... | collective-permute-start | bytes 786440 | tf_op jit(solution)/shard_map/ppermute | solution.py:245
  14.6 2.9 %collective-permute-start.5 = (f32[16,512]{1,0:T(8,128)S(1)}, f32[16,512]{1,0:T(8,128)S(1)}, u32[]{:S(2)}, u32[]{:S(2)}) collective-permute-start(f32[16,512]{1,0:T(8,128)S(1)} %get-tuple-element.22.refs_0_.info), channel_id=1, source_target_pairs={{128,0},{129,1},{130,2},{131,3},{132,4},{133,5},{134,6},{135,7},{1... | collective-permute-start | bytes 98312 | tf_op jit(solution)/shard_map/ppermute | solution.py:245
  17.6 0.4 collective-permute-start.3
  17.9 0.4 collective-permute-start.7
  18.3 0.6 %collective-permute-done.5.info = f32[16,512]{1,0:T(8,128)S(1)} collective-permute-done((f32[16,512]{1,0:T(8,128)S(1)}, f32[16,512]{1,0:T(8,128)S(1)}, u32[]{:S(2)}, u32[]{:S(2)}) %collective-permute-start.5) | collective-permute-done | bytes 32800 | tf_op jit(solution)/shard_map/ppermute | solution.py:245
  18.9 0.2 shard_map.109.mat
  19.1 1.3 %collective-permute-done.3.refs_0_.info = f32[16,512]{1,0:T(8,128)S(1)} collective-permute-done((f32[16,512]{1,0:T(8,128)S(1)}, f32[16,512]{1,0:T(8,128)S(1)}, u32[]{:S(2)}, u32[]{:S(2)}) %collective-permute-start.3) | collective-permute-done | bytes 32800 | tf_op jit(solution)/shard_map/ppermute | solution.py:245
  20.3 0.0 collective-permute-done.2.other
  20.3 0.5 shard_map.108
  20.8 1.0 %collective-permute-start.4 = (bf16[128,512]{1,0:T(8,128)(2,1)S(1)}, bf16[128,512]{1,0:T(8,128)(2,1)S(1)}, u32[]{:S(2)}, u32[]{:S(2)}) collective-permute-start(bf16[128,512]{1,0:T(8,128)(2,1)S(1)} %get-tuple-element.24), channel_id=1, source_target_pairs={{64,0},{65,1},{66,2},{67,3},{68,4},{69,5},{70,6},{71,7},{72,8},{73... | collective-permute-start | bytes 393224 | tf_op jit(solution)/shard_map/ppermute | solution.py:245
  21.8 0.4 shard_map.110
  22.2 0.0 copy-start
  22.2 1.9 %collective-permute-start.6 = (bf16[128,512]{1,0:T(8,128)(2,1)S(1)}, bf16[128,512]{1,0:T(8,128)(2,1)S(1)}, u32[]{:S(2)}, u32[]{:S(2)}) collective-permute-start(bf16[128,512]{1,0:T(8,128)(2,1)S(1)} %shard_map.110), channel_id=1, source_target_pairs={{128,0},{129,1},{130,2},{131,3},{132,4},{133,5},{134,6},{135,7},{1... | collective-permute-start | bytes 393224 | tf_op jit(solution)/shard_map/ppermute | solution.py:245
  24.1 0.0 collective-permute-done.7.refs_0_.info
  24.1 0.5 shard_map.111
  24.6 1.3 %collective-permute-start.8 = (bf16[128,512]{1,0:T(8,128)(2,1)S(1)}, bf16[128,512]{1,0:T(8,128)(2,1)S(1)}, u32[]{:S(2)}, u32[]{:S(2)}) collective-permute-start(bf16[128,512]{1,0:T(8,128)(2,1)S(1)} %get-tuple-element.25), channel_id=1, source_target_pairs={{192,0},{193,1},{194,2},{195,3},{196,4},{197,5},{198,6},{199,7},{2... | collective-permute-start | bytes 393224 | tf_op jit(solution)/shard_map/ppermute | solution.py:245
  26.5 0.0 copy-start.7
  26.5 0.0 copy-done
  26.6 0.6 %copy-done.7 = f32[128]{0:T(128)S(1)} copy-done((f32[128]{0:T(128)S(1)}, f32[128]{0:T(128)}, u32[]{:S(2)}) %copy-start.7) | copy-done | bytes 536
  27.2 0.3 shard_map.112
  27.5 0.5 shard_map.107
  28.0 0.0 collective-permute-done.4.refs_1_
  28.0 1.1 %collective-permute-done.6.refs_2_ = bf16[128,512]{1,0:T(8,128)(2,1)S(1)} collective-permute-done((bf16[128,512]{1,0:T(8,128)(2,1)S(1)}, bf16[128,512]{1,0:T(8,128)(2,1)S(1)}, u32[]{:S(2)}, u32[]{:S(2)}) %collective-permute-start.6) | collective-permute-done | bytes 131104 | tf_op jit(solution)/shard_map/ppermute | solution.py:245
  29.0 3.6 %collective-permute-done.8.refs_3_ = bf16[128,512]{1,0:T(8,128)(2,1)S(1)} collective-permute-done((bf16[128,512]{1,0:T(8,128)(2,1)S(1)}, bf16[128,512]{1,0:T(8,128)(2,1)S(1)}, u32[]{:S(2)}, u32[]{:S(2)}) %collective-permute-start.8) | collective-permute-done | bytes 131104 | tf_op jit(solution)/shard_map/ppermute | solution.py:245
  32.6 0.1 shard_map.113
  32.8 1.0 %collective-permute-start.9 = (bf16[128,512]{1,0:T(8,128)(2,1)S(1)}, bf16[128,512]{1,0:T(8,128)(2,1)S(1)}, u32[]{:S(2)}, u32[]{:S(2)}) collective-permute-start(bf16[128,512]{1,0:T(8,128)(2,1)S(1)} %get-tuple-element.29.scaled), channel_id=1, source_target_pairs={{128,0},{129,1},{130,2},{131,3},{132,4},{133,5},{134,6},{135,7},{1... | collective-permute-start | bytes 393224 | tf_op jit(solution)/shard_map/ppermute | solution.py:245
  33.7 0.2 collective-permute-start.10
  33.9 2.2 %collective-permute-start.11 = (bf16[128,512]{1,0:T(8,128)(2,1)S(1)}, bf16[128,512]{1,0:T(8,128)(2,1)S(1)}, u32[]{:S(2)}, u32[]{:S(2)}) collective-permute-start(bf16[128,512]{1,0:T(8,128)(2,1)S(1)} %get-tuple-element.29.scaled), channel_id=1, source_target_pairs={{192,0},{193,1},{194,2},{195,3},{196,4},{197,5},{198,6},{199,7},{2... | collective-permute-start | bytes 393224 | tf_op jit(solution)/shard_map/ppermute | solution.py:245
  36.1 0.5 shard_map.115.before
  36.6 1.9 %collective-permute-done.9.scaled = bf16[128,512]{1,0:T(8,128)(2,1)S(1)} collective-permute-done((bf16[128,512]{1,0:T(8,128)(2,1)S(1)}, bf16[128,512]{1,0:T(8,128)(2,1)S(1)}, u32[]{:S(2)}, u32[]{:S(2)}) %collective-permute-start.9) | collective-permute-done | bytes 131104 | tf_op jit(solution)/shard_map/ppermute | solution.py:245
  38.5 0.5 shard_map.116.before
  38.9 0.0 collective-permute-done.10.scaled
  38.9 0.5 shard_map.117.before
  39.4 2.3 %collective-permute-done.11.scaled = bf16[128,512]{1,0:T(8,128)(2,1)S(1)} collective-permute-done((bf16[128,512]{1,0:T(8,128)(2,1)S(1)}, bf16[128,512]{1,0:T(8,128)(2,1)S(1)}, u32[]{:S(2)}, u32[]{:S(2)}) %collective-permute-start.11) | collective-permute-done | bytes 131104 | tf_op jit(solution)/shard_map/ppermute | solution.py:245
  41.8 0.5 shard_map.119
  42.3 1.4 %collective-permute-start.12 = (bf16[128,1024]{1,0:T(8,128)(2,1)S(1)}, bf16[128,1024]{1,0:T(8,128)(2,1)S(1)}, u32[]{:S(2)}, u32[]{:S(2)}) collective-permute-start(bf16[128,1024]{1,0:T(8,128)(2,1)S(1)} %shard_map.119), channel_id=1, source_target_pairs={{32,0},{33,1},{34,2},{35,3},{36,4},{37,5},{38,6},{39,7},{40,8},{41... | collective-permute-start | bytes 786440 | tf_op jit(solution)/shard_map/ppermute | solution.py:245
  43.6 0.5 shard_map.118.own
  44.1 0.7 %collective-permute-done.12.got = bf16[128,1024]{1,0:T(8,128)(2,1)S(1)} collective-permute-done((bf16[128,1024]{1,0:T(8,128)(2,1)S(1)}, bf16[128,1024]{1,0:T(8,128)(2,1)S(1)}, u32[]{:S(2)}, u32[]{:S(2)}) %collective-permute-start.12) | collective-permute-done | bytes 262176 | tf_op jit(solution)/shard_map/ppermute | solution.py:245
  44.8 0.1 shard_map.120
  44.9 0.1 collective-permute-start.13
  45.0 5.2 %collective-permute-start.14 = (bf16[128,256]{1,0:T(8,128)(2,1)S(1)}, bf16[128,256]{1,0:T(8,128)(2,1)S(1)}, u32[]{:S(2)}, u32[]{:S(2)}) collective-permute-start(bf16[128,256]{1,0:T(8,128)(2,1)S(1)} %get-tuple-element.35), channel_id=1, source_target_pairs={{31,0},{2,1},{1,2},{4,3},{3,4},{6,5},{5,6},{8,7},{7,8},{10,9},{9,1... | collective-permute-start | bytes 196616 | tf_op jit(solution)/shard_map/ppermute | solution.py:245
  50.1 0.8 %shard_map.114 = f32[512,128]{1,0:T(8,128)} custom-call(f32[128,512]{1,0:T(8,128)S(1)} %get-tuple-element.28.source), custom_call_target="tpu_custom_call" | custom-call | flops 1048576 | bytes 1048576 | tf_op jit(solution)/shard_map/pallas_call | solution.py:220
  50.9 0.0 collective-permute-done.13.near
  50.9 1.3 %collective-permute-done.14.far = bf16[128,256]{1,0:T(8,128)(2,1)S(1)} collective-permute-done((bf16[128,256]{1,0:T(8,128)(2,1)S(1)}, bf16[128,256]{1,0:T(8,128)(2,1)S(1)}, u32[]{:S(2)}, u32[]{:S(2)}) %collective-permute-start.14) | collective-permute-done | bytes 65568 | tf_op jit(solution)/shard_map/ppermute | solution.py:245
  52.2 0.9 %shard_map.121 = f32[137,1,512]{2,1,0:T(1,128)} custom-call(f32[128,512]{1,0:T(8,128)S(1)} %get-tuple-element.33.mid, bf16[128,256]{1,0:T(8,128)(2,1)S(1)} %collective-permute-done.13.near, bf16[128,256]{1,0:T(8,128)(2,1)S(1)} %collective-permute-done.14.far, bf16[137,128]{1,0:T(8,128)(2,1)S(1)} %copy-done.1), custom_call_target="tpu_custom_call" | custom-call | flops 1048576 | bytes 1048576 | tf_op jit(solution)/shard_map/pallas_call | solution.py:220
  (2 shorter events, 0.0 us)
Async XLA Ops:
  0.6 0.9 %copy-start.2 = (bf16[1,512,137]{1,2,0:T(8,128)(2,1)S(1)}, bf16[1,512,137]{1,2,0:T(8,128)(2,1)}, u32[]{:S(2)}) copy-start(bf16[1,512,137]{1,2,0:T(8,128)(2,1)} %param.9) | copy-start | bytes 420868
  0.6 0.9 %copy-start.1 = (bf16[137,128]{1,0:T(8,128)(2,1)S(1)}, bf16[137,128]{1,0:T(8,128)(2,1)}, u32[]{:S(2)}) copy-start(bf16[137,128]{1,0:T(8,128)(2,1)} %jac.3) | copy-start | bytes 105220
  0.7 0.9 %copy-start.4 = (s32[512]{0:T(512)S(1)}, s32[512]{0:T(512)}, u32[]{:S(2)}) copy-start(s32[512]{0:T(512)} %param.10) | copy-start | bytes 6148
  0.7 0.9 %copy-start.5 = (s32[512]{0:T(512)S(1)}, s32[512]{0:T(512)}, u32[]{:S(2)}) copy-start(s32[512]{0:T(512)} %param.12) | copy-start | bytes 6148
  0.7 0.9 %copy-start.6 = (f32[512]{0:T(512)S(1)}, f32[512]{0:T(512)}, u32[]{:S(2)}) copy-start(f32[512]{0:T(512)} %param.13) | copy-start | bytes 6148
  0.7 0.9 %copy-start.3 = (bf16[512,8]{0,1:T(8,128)(2,1)S(1)}, bf16[512,8]{0,1:T(8,128)(2,1)}, u32[]{:S(2)}) copy-start(bf16[512,8]{0,1:T(8,128)(2,1)} %param.11) | copy-start | bytes 24580
  1.8 9.2 %collective-permute-start = (bf16[128,256]{1,0:T(8,128)(2,1)S(1)}, bf16[128,256]{1,0:T(8,128)(2,1)S(1)}, u32[]{:S(2)}, u32[]{:S(2)}) collective-permute-start(bf16[128,256]{1,0:T(8,128)(2,1)S(1)} %get-tuple-element.20), channel_id=1, source_target_pairs={{1,0},{0,1},{3,2},{2,3},{5,4},{4,5},{7,6},{6,7},{9,8},{8,9},{11,10... | collective-permute-start | bytes 196616 | tf_op jit(solution)/shard_map/ppermute | solution.py:245
  3.9 8.8 %collective-permute-start.1 = (bf16[128,256]{1,0:T(8,128)(2,1)S(1)}, bf16[128,256]{1,0:T(8,128)(2,1)S(1)}, u32[]{:S(2)}, u32[]{:S(2)}) collective-permute-start(bf16[128,256]{1,0:T(8,128)(2,1)S(1)} %get-tuple-element.21), channel_id=1, source_target_pairs={{31,0},{2,1},{1,2},{4,3},{3,4},{6,5},{5,6},{8,7},{7,8},{10,9},{9,1... | collective-permute-start | bytes 196616 | tf_op jit(solution)/shard_map/ppermute | solution.py:245
  12.7 7.6 %collective-permute-start.2 = (bf16[128,1024]{1,0:T(8,128)(2,1)S(1)}, bf16[128,1024]{1,0:T(8,128)(2,1)S(1)}, u32[]{:S(2)}, u32[]{:S(2)}) collective-permute-start(bf16[128,1024]{1,0:T(8,128)(2,1)S(1)} %shard_map.106.mine), channel_id=1, source_target_pairs={{32,0},{33,1},{34,2},{35,3},{36,4},{37,5},{38,6},{39,7},{40,8},{41... | collective-permute-start | bytes 786440 | tf_op jit(solution)/shard_map/ppermute | solution.py:245
  14.6 4.3 %collective-permute-start.5 = (f32[16,512]{1,0:T(8,128)S(1)}, f32[16,512]{1,0:T(8,128)S(1)}, u32[]{:S(2)}, u32[]{:S(2)}) collective-permute-start(f32[16,512]{1,0:T(8,128)S(1)} %get-tuple-element.22.refs_0_.info), channel_id=1, source_target_pairs={{128,0},{129,1},{130,2},{131,3},{132,4},{133,5},{134,6},{135,7},{1... | collective-permute-start | bytes 98312 | tf_op jit(solution)/shard_map/ppermute | solution.py:245
  17.6 2.8 %collective-permute-start.3 = (f32[16,512]{1,0:T(8,128)S(1)}, f32[16,512]{1,0:T(8,128)S(1)}, u32[]{:S(2)}, u32[]{:S(2)}) collective-permute-start(f32[16,512]{1,0:T(8,128)S(1)} %get-tuple-element.22.refs_0_.info), channel_id=1, source_target_pairs={{64,0},{65,1},{66,2},{67,3},{68,4},{69,5},{70,6},{71,7},{72,8},{73... | collective-permute-start | bytes 98312 | tf_op jit(solution)/shard_map/ppermute | solution.py:245
  17.9 6.2 %collective-permute-start.7 = (f32[16,512]{1,0:T(8,128)S(1)}, f32[16,512]{1,0:T(8,128)S(1)}, u32[]{:S(2)}, u32[]{:S(2)}) collective-permute-start(f32[16,512]{1,0:T(8,128)S(1)} %get-tuple-element.22.refs_0_.info), channel_id=1, source_target_pairs={{192,0},{193,1},{194,2},{195,3},{196,4},{197,5},{198,6},{199,7},{2... | collective-permute-start | bytes 98312 | tf_op jit(solution)/shard_map/ppermute | solution.py:245
  20.8 7.1 %collective-permute-start.4 = (bf16[128,512]{1,0:T(8,128)(2,1)S(1)}, bf16[128,512]{1,0:T(8,128)(2,1)S(1)}, u32[]{:S(2)}, u32[]{:S(2)}) collective-permute-start(bf16[128,512]{1,0:T(8,128)(2,1)S(1)} %get-tuple-element.24), channel_id=1, source_target_pairs={{64,0},{65,1},{66,2},{67,3},{68,4},{69,5},{70,6},{71,7},{72,8},{73... | collective-permute-start | bytes 393224 | tf_op jit(solution)/shard_map/ppermute | solution.py:245
  22.2 4.3 %copy-start = (f32[512,128]{1,0:T(8,128)S(1)}, f32[512,128]{1,0:T(8,128)}, u32[]{:S(2)}) copy-start(f32[512,128]{1,0:T(8,128)} %source.1) | copy-start | bytes 786436
  22.2 6.8 %collective-permute-start.6 = (bf16[128,512]{1,0:T(8,128)(2,1)S(1)}, bf16[128,512]{1,0:T(8,128)(2,1)S(1)}, u32[]{:S(2)}, u32[]{:S(2)}) collective-permute-start(bf16[128,512]{1,0:T(8,128)(2,1)S(1)} %shard_map.110), channel_id=1, source_target_pairs={{128,0},{129,1},{130,2},{131,3},{132,4},{133,5},{134,6},{135,7},{1... | collective-permute-start | bytes 393224 | tf_op jit(solution)/shard_map/ppermute | solution.py:245
  24.6 8.0 %collective-permute-start.8 = (bf16[128,512]{1,0:T(8,128)(2,1)S(1)}, bf16[128,512]{1,0:T(8,128)(2,1)S(1)}, u32[]{:S(2)}, u32[]{:S(2)}) collective-permute-start(bf16[128,512]{1,0:T(8,128)(2,1)S(1)} %get-tuple-element.25), channel_id=1, source_target_pairs={{192,0},{193,1},{194,2},{195,3},{196,4},{197,5},{198,6},{199,7},{2... | collective-permute-start | bytes 393224 | tf_op jit(solution)/shard_map/ppermute | solution.py:245
  26.5 0.7 %copy-start.7 = (f32[128]{0:T(128)S(1)}, f32[128]{0:T(128)}, u32[]{:S(2)}) copy-start(f32[128]{0:T(128)} %param.17) | copy-start | bytes 1540
  32.8 5.7 %collective-permute-start.9 = (bf16[128,512]{1,0:T(8,128)(2,1)S(1)}, bf16[128,512]{1,0:T(8,128)(2,1)S(1)}, u32[]{:S(2)}, u32[]{:S(2)}) collective-permute-start(bf16[128,512]{1,0:T(8,128)(2,1)S(1)} %get-tuple-element.29.scaled), channel_id=1, source_target_pairs={{128,0},{129,1},{130,2},{131,3},{132,4},{133,5},{134,6},{135,7},{1... | collective-permute-start | bytes 393224 | tf_op jit(solution)/shard_map/ppermute | solution.py:245
  33.7 5.2 %collective-permute-start.10 = (bf16[128,512]{1,0:T(8,128)(2,1)S(1)}, bf16[128,512]{1,0:T(8,128)(2,1)S(1)}, u32[]{:S(2)}, u32[]{:S(2)}) collective-permute-start(bf16[128,512]{1,0:T(8,128)(2,1)S(1)} %get-tuple-element.29.scaled), channel_id=1, source_target_pairs={{64,0},{65,1},{66,2},{67,3},{68,4},{69,5},{70,6},{71,7},{72,8},{73... | collective-permute-start | bytes 393224 | tf_op jit(solution)/shard_map/ppermute | solution.py:245
  33.9 7.9 %collective-permute-start.11 = (bf16[128,512]{1,0:T(8,128)(2,1)S(1)}, bf16[128,512]{1,0:T(8,128)(2,1)S(1)}, u32[]{:S(2)}, u32[]{:S(2)}) collective-permute-start(bf16[128,512]{1,0:T(8,128)(2,1)S(1)} %get-tuple-element.29.scaled), channel_id=1, source_target_pairs={{192,0},{193,1},{194,2},{195,3},{196,4},{197,5},{198,6},{199,7},{2... | collective-permute-start | bytes 393224 | tf_op jit(solution)/shard_map/ppermute | solution.py:245
  42.3 2.5 %collective-permute-start.12 = (bf16[128,1024]{1,0:T(8,128)(2,1)S(1)}, bf16[128,1024]{1,0:T(8,128)(2,1)S(1)}, u32[]{:S(2)}, u32[]{:S(2)}) collective-permute-start(bf16[128,1024]{1,0:T(8,128)(2,1)S(1)} %shard_map.119), channel_id=1, source_target_pairs={{32,0},{33,1},{34,2},{35,3},{36,4},{37,5},{38,6},{39,7},{40,8},{41... | collective-permute-start | bytes 786440 | tf_op jit(solution)/shard_map/ppermute | solution.py:245
  44.9 6.1 %collective-permute-start.13 = (bf16[128,256]{1,0:T(8,128)(2,1)S(1)}, bf16[128,256]{1,0:T(8,128)(2,1)S(1)}, u32[]{:S(2)}, u32[]{:S(2)}) collective-permute-start(bf16[128,256]{1,0:T(8,128)(2,1)S(1)} %get-tuple-element.34), channel_id=1, source_target_pairs={{1,0},{0,1},{3,2},{2,3},{5,4},{4,5},{7,6},{6,7},{9,8},{8,9},{11,10... | collective-permute-start | bytes 196616 | tf_op jit(solution)/shard_map/ppermute | solution.py:245
  45.0 7.2 %collective-permute-start.14 = (bf16[128,256]{1,0:T(8,128)(2,1)S(1)}, bf16[128,256]{1,0:T(8,128)(2,1)S(1)}, u32[]{:S(2)}, u32[]{:S(2)}) collective-permute-start(bf16[128,256]{1,0:T(8,128)(2,1)S(1)} %get-tuple-element.35), channel_id=1, source_target_pairs={{31,0},{2,1},{1,2},{4,3},{3,4},{6,5},{5,6},{8,7},{7,8},{10,9},{9,1... | collective-permute-start | bytes 196616 | tf_op jit(solution)/shard_map/ppermute | solution.py:245

commit v10 on v7

--- a/solution.py
+++ b/solution.py
@@ -12,7 +12,6 @@
 BF16 = jnp.bfloat16
 GROUP = 16
 SWAP_ORDER = (2, 3, 1)
-LAND_ORDER = (2, 1, 3)
 FIRST_FLOPS = 1 << 34
 
 
@@ -177,15 +176,15 @@
     acc[...] = before[...] + spread_one(info, scaled, mat)
 
 
-def spread_give_kernel(before, info, scaled, mat, give):
-    chan = give.shape[0]
-    part = spread_rows(weighted(info, scaled, held_slots()[1]), mat)
-    give[...] = (before[chan:, :] + part).astype(BF16)
-
-
-def spread_keep_kernel(before, info, scaled, mat, own):
+def spread_last_kernel(before, *refs):
+    infos, scaled, mats = refs[:2], refs[2:4], refs[4:6]
+    own, give = refs[6:]
     chan = own.shape[0]
-    own[...] = before[:chan, :] + spread_rows(weighted(info, scaled, held_slots()[0]), mat)
+    total = before[...]
+    for info, source, mat in zip(infos, scaled, mats):
+        total = total + spread_one(info, source, mat)
+    own[...] = total[:chan]
+    give[...] = total[chan:].astype(BF16)
 
 
 def join_kernel(own, got, mid, near, far):
@@ -319,20 +318,18 @@
         all_scaled = [scaled] + [swap(scaled, y=j) for j in range(1, lanes)]
         (acc,) = call(spread_first_kernel, [((2 * chan, width), F32)], info, scaled, mats[0])
         (departures,) = call(turn_kernel, [((obs, chan), F32)], gaps)
-        *early, last = LAND_ORDER
-        for j in early:
-            (acc,) = call(
-                spread_next_kernel,
-                [((2 * chan, width), F32)],
-                acc,
-                infos[j],
-                all_scaled[j],
-                mats[j],
-            )
-        rest = (acc, infos[last], all_scaled[last], mats[last])
-        (give,) = call(spread_give_kernel, [((chan, width), BF16)], *rest)
+        (acc,) = call(
+            spread_next_kernel, [((2 * chan, width), F32)], acc, infos[2], all_scaled[2], mats[2]
+        )
+        mine, give = call(
+            spread_last_kernel,
+            [((chan, width), F32), ((chan, width), BF16)],
+            acc,
+            *[infos[j] for j in (1, 3)],
+            *[all_scaled[j] for j in (1, 3)],
+            *[mats[j] for j in (1, 3)],
+        )
         give = swap(give, core=1)
-        (mine,) = call(spread_keep_kernel, [((chan, width), F32)], *rest)
         mid, near, far = call(
             join_kernel, [((chan, cols), F32)] + [((chan, half), BF16)] * 2, mine, give
         )

time: 53.2 us -> 53.5 us (level)
  waiting for transfers between devices: 14.4 us -> 15.3 us
  Pallas kernels: 6.84 us -> 6.17 us
    ppermute x15, waiting for transfers between devices: 14.4 us -> 15.3 us  [swap(): return lax.ppermute(block, ('tm', 'space'), route)]
    pallas_call x18 -> x16, Pallas kernels: 6.84 us -> 6.17 us  [call(): pl.pallas_call(kernel, out_shape=[jax.ShapeDtypeStruct(shape, dtype) for...]
  transfers between devices with their start and end apart: 15 -> 15, of which waited for: 9 -> 9; matrix products, arithmetic and copies ran while one was open for 0% -> 0% of each run, Pallas kernels for 9% -> 8%
where the time goes in v10:
time: 53.5 us; the launch traced here: 53.4 us
  starting transfers between devices  28.9 us (54%)
  waiting for transfers between devices  15.3 us (29%)
  Pallas kernels  6.17 us (12%)
  local copies, waits for them, and re-layouts  1.51 us (3%)
  between operations  1.5 us (3%)
    ppermute x15, starting transfers between devices, swap(): return lax.ppermute(block, ('tm', 'space'), route)  28.9 us
    ppermute x15, waiting for transfers between devices, swap(): return lax.ppermute(block, ('tm', 'space'), route)  15.3 us
    pallas_call x16, Pallas kernels, call(): pl.pallas_call(kernel, out_shape=[jax.ShapeDtypeStruct(shape, dtype) for...  6.17 us
    unnamed x16, local copies, waits for them, and re-layouts  1.51 us
  transfers between devices with their start and end apart: 15, of which 9 were waited for; matrix products, arithmetic and copies ran while one was open for 0% of the time, Pallas kernels for 8%

profile of v10, /device:TPU:1, one launch (start us, length us, event | category | flops | bytes accessed | tf_op | source)
XLA Modules:
  0.0 53.4 jit_solution(5460517152999525584)
XLA Ops:
  0.6 0.0 copy-start.2
  0.6 0.0 copy-start.1
  0.7 0.0 copy-start.4
  0.7 0.0 copy-start.5
  0.7 0.0 copy-start.6
  0.7 0.0 copy-start.3
  0.7 0.8 %copy-done.2 = bf16[1,512,137]{1,2,0:T(8,128)(2,1)S(1)} copy-done((bf16[1,512,137]{1,2,0:T(8,128)(2,1)S(1)}, bf16[1,512,137]{1,2,0:T(8,128)(2,1)}, u32[]{:S(2)}) %copy-start.2) | copy-done | bytes 140312
  1.5 0.0 copy-done.1
  1.5 0.0 copy-done.4
  1.5 0.0 copy-done.5
  1.6 0.0 copy-done.6
  1.6 0.0 copy-done.3
  1.6 0.2 shard_map.105
  1.8 2.1 %collective-permute-start = (bf16[128,256]{1,0:T(8,128)(2,1)S(1)}, bf16[128,256]{1,0:T(8,128)(2,1)S(1)}, u32[]{:S(2)}, u32[]{:S(2)}) collective-permute-start(bf16[128,256]{1,0:T(8,128)(2,1)S(1)} %get-tuple-element.22), channel_id=1, source_target_pairs={{1,0},{0,1},{3,2},{2,3},{5,4},{4,5},{7,6},{6,7},{9,8},{8,9},{11,10... | collective-permute-start | bytes 196616 | tf_op jit(solution)/shard_map/ppermute | solution.py:243
  3.9 7.1 %collective-permute-start.1 = (bf16[128,256]{1,0:T(8,128)(2,1)S(1)}, bf16[128,256]{1,0:T(8,128)(2,1)S(1)}, u32[]{:S(2)}, u32[]{:S(2)}) collective-permute-start(bf16[128,256]{1,0:T(8,128)(2,1)S(1)} %get-tuple-element.23), channel_id=1, source_target_pairs={{31,0},{2,1},{1,2},{4,3},{3,4},{6,5},{5,6},{8,7},{7,8},{10,9},{9,1... | collective-permute-start | bytes 196616 | tf_op jit(solution)/shard_map/ppermute | solution.py:243
  11.0 0.0 collective-permute-done.near
  11.0 1.6 %collective-permute-done.1.far = bf16[128,256]{1,0:T(8,128)(2,1)S(1)} collective-permute-done((bf16[128,256]{1,0:T(8,128)(2,1)S(1)}, bf16[128,256]{1,0:T(8,128)(2,1)S(1)}, u32[]{:S(2)}, u32[]{:S(2)}) %collective-permute-start.1) | collective-permute-done | bytes 65568 | tf_op jit(solution)/shard_map/ppermute | solution.py:243
  12.7 1.9 %collective-permute-start.2 = (bf16[128,1024]{1,0:T(8,128)(2,1)S(1)}, bf16[128,1024]{1,0:T(8,128)(2,1)S(1)}, u32[]{:S(2)}, u32[]{:S(2)}) collective-permute-start(bf16[128,1024]{1,0:T(8,128)(2,1)S(1)} %shard_map.106.mine), channel_id=1, source_target_pairs={{32,0},{33,1},{34,2},{35,3},{36,4},{37,5},{38,6},{39,7},{40,8},{41... | collective-permute-start | bytes 786440 | tf_op jit(solution)/shard_map/ppermute | solution.py:243
  14.6 2.9 %collective-permute-start.5 = (f32[16,512]{1,0:T(8,128)S(1)}, f32[16,512]{1,0:T(8,128)S(1)}, u32[]{:S(2)}, u32[]{:S(2)}) collective-permute-start(f32[16,512]{1,0:T(8,128)S(1)} %get-tuple-element.24.refs_0_.info), channel_id=1, source_target_pairs={{128,0},{129,1},{130,2},{131,3},{132,4},{133,5},{134,6},{135,7},{1... | collective-permute-start | bytes 98312 | tf_op jit(solution)/shard_map/ppermute | solution.py:243
  17.6 0.4 collective-permute-start.3
  17.9 0.4 collective-permute-start.7
  18.3 0.6 %collective-permute-done.5.info = f32[16,512]{1,0:T(8,128)S(1)} collective-permute-done((f32[16,512]{1,0:T(8,128)S(1)}, f32[16,512]{1,0:T(8,128)S(1)}, u32[]{:S(2)}, u32[]{:S(2)}) %collective-permute-start.5) | collective-permute-done | bytes 32800 | tf_op jit(solution)/shard_map/ppermute | solution.py:243
  18.9 0.2 shard_map.109.mat
  19.1 1.3 %collective-permute-done.3.refs_0_ = f32[16,512]{1,0:T(8,128)S(1)} collective-permute-done((f32[16,512]{1,0:T(8,128)S(1)}, f32[16,512]{1,0:T(8,128)S(1)}, u32[]{:S(2)}, u32[]{:S(2)}) %collective-permute-start.3) | collective-permute-done | bytes 32800 | tf_op jit(solution)/shard_map/ppermute | solution.py:243
  20.3 0.0 collective-permute-done.2.other
  20.3 0.5 shard_map.108
  20.8 1.0 %collective-permute-start.4 = (bf16[128,512]{1,0:T(8,128)(2,1)S(1)}, bf16[128,512]{1,0:T(8,128)(2,1)S(1)}, u32[]{:S(2)}, u32[]{:S(2)}) collective-permute-start(bf16[128,512]{1,0:T(8,128)(2,1)S(1)} %get-tuple-element.26), channel_id=1, source_target_pairs={{64,0},{65,1},{66,2},{67,3},{68,4},{69,5},{70,6},{71,7},{72,8},{73... | collective-permute-start | bytes 393224 | tf_op jit(solution)/shard_map/ppermute | solution.py:243
  21.8 0.4 shard_map.110
  22.2 0.0 copy-start
  22.2 1.9 %collective-permute-start.6 = (bf16[128,512]{1,0:T(8,128)(2,1)S(1)}, bf16[128,512]{1,0:T(8,128)(2,1)S(1)}, u32[]{:S(2)}, u32[]{:S(2)}) collective-permute-start(bf16[128,512]{1,0:T(8,128)(2,1)S(1)} %shard_map.110), channel_id=1, source_target_pairs={{128,0},{129,1},{130,2},{131,3},{132,4},{133,5},{134,6},{135,7},{1... | collective-permute-start | bytes 393224 | tf_op jit(solution)/shard_map/ppermute | solution.py:243
  24.1 0.0 collective-permute-done.7.refs_0_.refs_1_
  24.1 0.5 shard_map.111
  24.6 1.3 %collective-permute-start.8 = (bf16[128,512]{1,0:T(8,128)(2,1)S(1)}, bf16[128,512]{1,0:T(8,128)(2,1)S(1)}, u32[]{:S(2)}, u32[]{:S(2)}) collective-permute-start(bf16[128,512]{1,0:T(8,128)(2,1)S(1)} %get-tuple-element.27), channel_id=1, source_target_pairs={{192,0},{193,1},{194,2},{195,3},{196,4},{197,5},{198,6},{199,7},{2... | collective-permute-start | bytes 393224 | tf_op jit(solution)/shard_map/ppermute | solution.py:243
  26.5 0.0 copy-start.7
  26.5 0.0 copy-done
  26.6 0.6 %copy-done.7 = f32[128]{0:T(128)S(1)} copy-done((f32[128]{0:T(128)S(1)}, f32[128]{0:T(128)}, u32[]{:S(2)}) %copy-start.7) | copy-done | bytes 536
  27.2 0.3 shard_map.112
  27.5 0.5 shard_map.107
  28.0 0.0 collective-permute-done.4.refs_1_
  28.0 1.1 %collective-permute-done.6.refs_2_ = bf16[128,512]{1,0:T(8,128)(2,1)S(1)} collective-permute-done((bf16[128,512]{1,0:T(8,128)(2,1)S(1)}, bf16[128,512]{1,0:T(8,128)(2,1)S(1)}, u32[]{:S(2)}, u32[]{:S(2)}) %collective-permute-start.6) | collective-permute-done | bytes 131104 | tf_op jit(solution)/shard_map/ppermute | solution.py:243
  29.0 3.6 %collective-permute-done.8.refs_3_ = bf16[128,512]{1,0:T(8,128)(2,1)S(1)} collective-permute-done((bf16[128,512]{1,0:T(8,128)(2,1)S(1)}, bf16[128,512]{1,0:T(8,128)(2,1)S(1)}, u32[]{:S(2)}, u32[]{:S(2)}) %collective-permute-start.8) | collective-permute-done | bytes 131104 | tf_op jit(solution)/shard_map/ppermute | solution.py:243
  32.6 0.1 shard_map.113
  32.8 1.0 %collective-permute-start.9 = (bf16[128,512]{1,0:T(8,128)(2,1)S(1)}, bf16[128,512]{1,0:T(8,128)(2,1)S(1)}, u32[]{:S(2)}, u32[]{:S(2)}) collective-permute-start(bf16[128,512]{1,0:T(8,128)(2,1)S(1)} %get-tuple-element.31.scaled), channel_id=1, source_target_pairs={{128,0},{129,1},{130,2},{131,3},{132,4},{133,5},{134,6},{135,7},{1... | collective-permute-start | bytes 393224 | tf_op jit(solution)/shard_map/ppermute | solution.py:243
  33.7 0.2 collective-permute-start.10
  33.9 2.2 %collective-permute-start.11 = (bf16[128,512]{1,0:T(8,128)(2,1)S(1)}, bf16[128,512]{1,0:T(8,128)(2,1)S(1)}, u32[]{:S(2)}, u32[]{:S(2)}) collective-permute-start(bf16[128,512]{1,0:T(8,128)(2,1)S(1)} %get-tuple-element.31.scaled), channel_id=1, source_target_pairs={{192,0},{193,1},{194,2},{195,3},{196,4},{197,5},{198,6},{199,7},{2... | collective-permute-start | bytes 393224 | tf_op jit(solution)/shard_map/ppermute | solution.py:243
  36.1 0.5 shard_map.115.before
  36.6 1.9 %collective-permute-done.9.scaled = bf16[128,512]{1,0:T(8,128)(2,1)S(1)} collective-permute-done((bf16[128,512]{1,0:T(8,128)(2,1)S(1)}, bf16[128,512]{1,0:T(8,128)(2,1)S(1)}, u32[]{:S(2)}, u32[]{:S(2)}) %collective-permute-start.9) | collective-permute-done | bytes 131104 | tf_op jit(solution)/shard_map/ppermute | solution.py:243
  38.5 0.5 shard_map.116.before
  38.9 0.0 collective-permute-done.10.refs_2_
  38.9 2.8 %collective-permute-done.11.refs_3_ = bf16[128,512]{1,0:T(8,128)(2,1)S(1)} collective-permute-done((bf16[128,512]{1,0:T(8,128)(2,1)S(1)}, bf16[128,512]{1,0:T(8,128)(2,1)S(1)}, u32[]{:S(2)}, u32[]{:S(2)}) %collective-permute-start.11) | collective-permute-done | bytes 131104 | tf_op jit(solution)/shard_map/ppermute | solution.py:243
  41.8 0.8 %shard_map.117 = (f32[128,1024]{1,0:T(8,128)S(1)}, bf16[128,1024]{1,0:T(8,128)(2,1)S(1)}) custom-call(f32[256,1024]{1,0:T(8,128)S(1)} %shard_map.116.before, f32[16,512]{1,0:T(8,128)S(1)} %collective-permute-done.3.refs_0_, f32[16,512]{1,0:T(8,128)S(1)} %collective-permute-done.7.refs_0_.refs_1_, bf16[128,512]{1,0:T(8,128)(2,1)S(1)} %collective-permute-done.10.refs_2_, ...), custom_call_target="tpu_custom_call" | custom-call | flops 1048576 | bytes 1048576 | tf_op jit(solution)/shard_map/pallas_call | solution.py:218
  42.5 1.4 %collective-permute-start.12 = (bf16[128,1024]{1,0:T(8,128)(2,1)S(1)}, bf16[128,1024]{1,0:T(8,128)(2,1)S(1)}, u32[]{:S(2)}, u32[]{:S(2)}) collective-permute-start(bf16[128,1024]{1,0:T(8,128)(2,1)S(1)} %get-tuple-element.36), channel_id=1, source_target_pairs={{32,0},{33,1},{34,2},{35,3},{36,4},{37,5},{38,6},{39,7},{40,8},{41... | collective-permute-start | bytes 786440 | tf_op jit(solution)/shard_map/ppermute | solution.py:243
  43.9 1.2 %collective-permute-done.12.got = bf16[128,1024]{1,0:T(8,128)(2,1)S(1)} collective-permute-done((bf16[128,1024]{1,0:T(8,128)(2,1)S(1)}, bf16[128,1024]{1,0:T(8,128)(2,1)S(1)}, u32[]{:S(2)}, u32[]{:S(2)}) %collective-permute-start.12) | collective-permute-done | bytes 262176 | tf_op jit(solution)/shard_map/ppermute | solution.py:243
  45.1 0.1 shard_map.118
  45.1 0.1 collective-permute-start.13
  45.2 5.1 %collective-permute-start.14 = (bf16[128,256]{1,0:T(8,128)(2,1)S(1)}, bf16[128,256]{1,0:T(8,128)(2,1)S(1)}, u32[]{:S(2)}, u32[]{:S(2)}) collective-permute-start(bf16[128,256]{1,0:T(8,128)(2,1)S(1)} %get-tuple-element.39), channel_id=1, source_target_pairs={{31,0},{2,1},{1,2},{4,3},{3,4},{6,5},{5,6},{8,7},{7,8},{10,9},{9,1... | collective-permute-start | bytes 196616 | tf_op jit(solution)/shard_map/ppermute | solution.py:243
  50.4 0.8 %shard_map.114 = f32[512,128]{1,0:T(8,128)} custom-call(f32[128,512]{1,0:T(8,128)S(1)} %get-tuple-element.30.source), custom_call_target="tpu_custom_call" | custom-call | flops 1048576 | bytes 1048576 | tf_op jit(solution)/shard_map/pallas_call | solution.py:218
  51.2 0.0 collective-permute-done.13.near
  51.2 1.2 %collective-permute-done.14.far = bf16[128,256]{1,0:T(8,128)(2,1)S(1)} collective-permute-done((bf16[128,256]{1,0:T(8,128)(2,1)S(1)}, bf16[128,256]{1,0:T(8,128)(2,1)S(1)}, u32[]{:S(2)}, u32[]{:S(2)}) %collective-permute-start.14) | collective-permute-done | bytes 65568 | tf_op jit(solution)/shard_map/ppermute | solution.py:243
  52.5 0.9 %shard_map.119 = f32[137,1,512]{2,1,0:T(1,128)} custom-call(f32[128,512]{1,0:T(8,128)S(1)} %get-tuple-element.37.mid, bf16[128,256]{1,0:T(8,128)(2,1)S(1)} %collective-permute-done.13.near, bf16[128,256]{1,0:T(8,128)(2,1)S(1)} %collective-permute-done.14.far, bf16[137,128]{1,0:T(8,128)(2,1)S(1)} %copy-done.1), custom_call_target="tpu_custom_call" | custom-call | flops 1048576 | bytes 1048576 | tf_op jit(solution)/shard_map/pallas_call | solution.py:218
  (2 shorter events, 0.0 us)
Async XLA Ops:
  0.6 0.9 %copy-start.2 = (bf16[1,512,137]{1,2,0:T(8,128)(2,1)S(1)}, bf16[1,512,137]{1,2,0:T(8,128)(2,1)}, u32[]{:S(2)}) copy-start(bf16[1,512,137]{1,2,0:T(8,128)(2,1)} %param.9) | copy-start | bytes 420868
  0.6 0.9 %copy-start.1 = (bf16[137,128]{1,0:T(8,128)(2,1)S(1)}, bf16[137,128]{1,0:T(8,128)(2,1)}, u32[]{:S(2)}) copy-start(bf16[137,128]{1,0:T(8,128)(2,1)} %jac.3) | copy-start | bytes 105220
  0.7 0.9 %copy-start.4 = (s32[512]{0:T(512)S(1)}, s32[512]{0:T(512)}, u32[]{:S(2)}) copy-start(s32[512]{0:T(512)} %param.10) | copy-start | bytes 6148
  0.7 0.9 %copy-start.5 = (s32[512]{0:T(512)S(1)}, s32[512]{0:T(512)}, u32[]{:S(2)}) copy-start(s32[512]{0:T(512)} %param.12) | copy-start | bytes 6148
  0.7 0.9 %copy-start.6 = (f32[512]{0:T(512)S(1)}, f32[512]{0:T(512)}, u32[]{:S(2)}) copy-start(f32[512]{0:T(512)} %param.13) | copy-start | bytes 6148
  0.7 0.9 %copy-start.3 = (bf16[512,8]{0,1:T(8,128)(2,1)S(1)}, bf16[512,8]{0,1:T(8,128)(2,1)}, u32[]{:S(2)}) copy-start(bf16[512,8]{0,1:T(8,128)(2,1)} %param.11) | copy-start | bytes 24580
  1.8 9.2 %collective-permute-start = (bf16[128,256]{1,0:T(8,128)(2,1)S(1)}, bf16[128,256]{1,0:T(8,128)(2,1)S(1)}, u32[]{:S(2)}, u32[]{:S(2)}) collective-permute-start(bf16[128,256]{1,0:T(8,128)(2,1)S(1)} %get-tuple-element.22), channel_id=1, source_target_pairs={{1,0},{0,1},{3,2},{2,3},{5,4},{4,5},{7,6},{6,7},{9,8},{8,9},{11,10... | collective-permute-start | bytes 196616 | tf_op jit(solution)/shard_map/ppermute | solution.py:243
  3.9 8.8 %collective-permute-start.1 = (bf16[128,256]{1,0:T(8,128)(2,1)S(1)}, bf16[128,256]{1,0:T(8,128)(2,1)S(1)}, u32[]{:S(2)}, u32[]{:S(2)}) collective-permute-start(bf16[128,256]{1,0:T(8,128)(2,1)S(1)} %get-tuple-element.23), channel_id=1, source_target_pairs={{31,0},{2,1},{1,2},{4,3},{3,4},{6,5},{5,6},{8,7},{7,8},{10,9},{9,1... | collective-permute-start | bytes 196616 | tf_op jit(solution)/shard_map/ppermute | solution.py:243
  12.7 7.6 %collective-permute-start.2 = (bf16[128,1024]{1,0:T(8,128)(2,1)S(1)}, bf16[128,1024]{1,0:T(8,128)(2,1)S(1)}, u32[]{:S(2)}, u32[]{:S(2)}) collective-permute-start(bf16[128,1024]{1,0:T(8,128)(2,1)S(1)} %shard_map.106.mine), channel_id=1, source_target_pairs={{32,0},{33,1},{34,2},{35,3},{36,4},{37,5},{38,6},{39,7},{40,8},{41... | collective-permute-start | bytes 786440 | tf_op jit(solution)/shard_map/ppermute | solution.py:243
  14.6 4.3 %collective-permute-start.5 = (f32[16,512]{1,0:T(8,128)S(1)}, f32[16,512]{1,0:T(8,128)S(1)}, u32[]{:S(2)}, u32[]{:S(2)}) collective-permute-start(f32[16,512]{1,0:T(8,128)S(1)} %get-tuple-element.24.refs_0_.info), channel_id=1, source_target_pairs={{128,0},{129,1},{130,2},{131,3},{132,4},{133,5},{134,6},{135,7},{1... | collective-permute-start | bytes 98312 | tf_op jit(solution)/shard_map/ppermute | solution.py:243
  17.6 2.8 %collective-permute-start.3 = (f32[16,512]{1,0:T(8,128)S(1)}, f32[16,512]{1,0:T(8,128)S(1)}, u32[]{:S(2)}, u32[]{:S(2)}) collective-permute-start(f32[16,512]{1,0:T(8,128)S(1)} %get-tuple-element.24.refs_0_.info), channel_id=1, source_target_pairs={{64,0},{65,1},{66,2},{67,3},{68,4},{69,5},{70,6},{71,7},{72,8},{73... | collective-permute-start | bytes 98312 | tf_op jit(solution)/shard_map/ppermute | solution.py:243
  17.9 6.2 %collective-permute-start.7 = (f32[16,512]{1,0:T(8,128)S(1)}, f32[16,512]{1,0:T(8,128)S(1)}, u32[]{:S(2)}, u32[]{:S(2)}) collective-permute-start(f32[16,512]{1,0:T(8,128)S(1)} %get-tuple-element.24.refs_0_.info), channel_id=1, source_target_pairs={{192,0},{193,1},{194,2},{195,3},{196,4},{197,5},{198,6},{199,7},{2... | collective-permute-start | bytes 98312 | tf_op jit(solution)/shard_map/ppermute | solution.py:243
  20.8 7.1 %collective-permute-start.4 = (bf16[128,512]{1,0:T(8,128)(2,1)S(1)}, bf16[128,512]{1,0:T(8,128)(2,1)S(1)}, u32[]{:S(2)}, u32[]{:S(2)}) collective-permute-start(bf16[128,512]{1,0:T(8,128)(2,1)S(1)} %get-tuple-element.26), channel_id=1, source_target_pairs={{64,0},{65,1},{66,2},{67,3},{68,4},{69,5},{70,6},{71,7},{72,8},{73... | collective-permute-start | bytes 393224 | tf_op jit(solution)/shard_map/ppermute | solution.py:243
  22.2 4.3 %copy-start = (f32[512,128]{1,0:T(8,128)S(1)}, f32[512,128]{1,0:T(8,128)}, u32[]{:S(2)}) copy-start(f32[512,128]{1,0:T(8,128)} %source.1) | copy-start | bytes 786436
  22.2 6.8 %collective-permute-start.6 = (bf16[128,512]{1,0:T(8,128)(2,1)S(1)}, bf16[128,512]{1,0:T(8,128)(2,1)S(1)}, u32[]{:S(2)}, u32[]{:S(2)}) collective-permute-start(bf16[128,512]{1,0:T(8,128)(2,1)S(1)} %shard_map.110), channel_id=1, source_target_pairs={{128,0},{129,1},{130,2},{131,3},{132,4},{133,5},{134,6},{135,7},{1... | collective-permute-start | bytes 393224 | tf_op jit(solution)/shard_map/ppermute | solution.py:243
  24.6 8.0 %collective-permute-start.8 = (bf16[128,512]{1,0:T(8,128)(2,1)S(1)}, bf16[128,512]{1,0:T(8,128)(2,1)S(1)}, u32[]{:S(2)}, u32[]{:S(2)}) collective-permute-start(bf16[128,512]{1,0:T(8,128)(2,1)S(1)} %get-tuple-element.27), channel_id=1, source_target_pairs={{192,0},{193,1},{194,2},{195,3},{196,4},{197,5},{198,6},{199,7},{2... | collective-permute-start | bytes 393224 | tf_op jit(solution)/shard_map/ppermute | solution.py:243
  26.5 0.7 %copy-start.7 = (f32[128]{0:T(128)S(1)}, f32[128]{0:T(128)}, u32[]{:S(2)}) copy-start(f32[128]{0:T(128)} %param.17) | copy-start | bytes 1540
  32.8 5.7 %collective-permute-start.9 = (bf16[128,512]{1,0:T(8,128)(2,1)S(1)}, bf16[128,512]{1,0:T(8,128)(2,1)S(1)}, u32[]{:S(2)}, u32[]{:S(2)}) collective-permute-start(bf16[128,512]{1,0:T(8,128)(2,1)S(1)} %get-tuple-element.31.scaled), channel_id=1, source_target_pairs={{128,0},{129,1},{130,2},{131,3},{132,4},{133,5},{134,6},{135,7},{1... | collective-permute-start | bytes 393224 | tf_op jit(solution)/shard_map/ppermute | solution.py:243
  33.7 5.2 %collective-permute-start.10 = (bf16[128,512]{1,0:T(8,128)(2,1)S(1)}, bf16[128,512]{1,0:T(8,128)(2,1)S(1)}, u32[]{:S(2)}, u32[]{:S(2)}) collective-permute-start(bf16[128,512]{1,0:T(8,128)(2,1)S(1)} %get-tuple-element.31.scaled), channel_id=1, source_target_pairs={{64,0},{65,1},{66,2},{67,3},{68,4},{69,5},{70,6},{71,7},{72,8},{73... | collective-permute-start | bytes 393224 | tf_op jit(solution)/shard_map/ppermute | solution.py:243
  33.9 7.9 %collective-permute-start.11 = (bf16[128,512]{1,0:T(8,128)(2,1)S(1)}, bf16[128,512]{1,0:T(8,128)(2,1)S(1)}, u32[]{:S(2)}, u32[]{:S(2)}) collective-permute-start(bf16[128,512]{1,0:T(8,128)(2,1)S(1)} %get-tuple-element.31.scaled), channel_id=1, source_target_pairs={{192,0},{193,1},{194,2},{195,3},{196,4},{197,5},{198,6},{199,7},{2... | collective-permute-start | bytes 393224 | tf_op jit(solution)/shard_map/ppermute | solution.py:243
  42.5 2.5 %collective-permute-start.12 = (bf16[128,1024]{1,0:T(8,128)(2,1)S(1)}, bf16[128,1024]{1,0:T(8,128)(2,1)S(1)}, u32[]{:S(2)}, u32[]{:S(2)}) collective-permute-start(bf16[128,1024]{1,0:T(8,128)(2,1)S(1)} %get-tuple-element.36), channel_id=1, source_target_pairs={{32,0},{33,1},{34,2},{35,3},{36,4},{37,5},{38,6},{39,7},{40,8},{41... | collective-permute-start | bytes 786440 | tf_op jit(solution)/shard_map/ppermute | solution.py:243
  45.1 6.1 %collective-permute-start.13 = (bf16[128,256]{1,0:T(8,128)(2,1)S(1)}, bf16[128,256]{1,0:T(8,128)(2,1)S(1)}, u32[]{:S(2)}, u32[]{:S(2)}) collective-permute-start(bf16[128,256]{1,0:T(8,128)(2,1)S(1)} %get-tuple-element.38), channel_id=1, source_target_pairs={{1,0},{0,1},{3,2},{2,3},{5,4},{4,5},{7,6},{6,7},{9,8},{8,9},{11,10... | collective-permute-start | bytes 196616 | tf_op jit(solution)/shard_map/ppermute | solution.py:243
  45.2 7.2 %collective-permute-start.14 = (bf16[128,256]{1,0:T(8,128)(2,1)S(1)}, bf16[128,256]{1,0:T(8,128)(2,1)S(1)}, u32[]{:S(2)}, u32[]{:S(2)}) collective-permute-start(bf16[128,256]{1,0:T(8,128)(2,1)S(1)} %get-tuple-element.39), channel_id=1, source_target_pairs={{31,0},{2,1},{1,2},{4,3},{3,4},{6,5},{5,6},{8,7},{7,8},{10,9},{9,1... | collective-permute-start | bytes 196616 | tf_op jit(solution)/shard_map/ppermute | solution.py:243
